TPU v7x, 32 devices: a whole 2x2x4 slice. The times are simulated.
32 devices in a mesh: col: 8 (over y, x, core), row: 4 (over z).
Axes of the slice: x: 2, y: 2, z: 4, core: 2. Of those that a mesh axis runs over, the one named last changes fastest.
Arguments:
- visibilities: bfloat16 [2, 8192, 4096], P(None, 'col', 'row'), may hold values from -6 to 6
- col_offsets: int32 [8], P('col'), may hold values from 0 to 15360
- row_offsets: int32 [4], replicated, may hold values from 0 to 15360
- facet_offsets: int32 [8, 2], replicated, may hold values from 0 to 16383
- facet_order: int32 [8], replicated, may hold values from 0 to 7, each once
- vis_counts: int32 [8, 4], P('col', 'row'), may hold values from 512 to 1024
Outputs:
- facet_images: float32 [8, 2, 64, 4096], P('col', None, None, 'row')
- peak: float32 [8], P('col')
Inputs may be any that keep to these rules, and one draw needn't show every extreme that they name: `facet_order`: each slot names a different facet.
All inputs are finite; a program needn't handle non-finite values.
Results may differ from a plain program's by a relative error of at most 0.0078.
Values may be sent and summed in bfloat16 or wider, within the bound.
No kernel may reach another device: no remote copies, remote signals or barrier semaphores. Data moves between devices by JAX's collectives and lax.ppermute only.
A program may use at most 128 MiB of HBM per device.

v0:
```python
import math

import jax
import jax.numpy as jnp
from jax import lax
from jax.sharding import PartitionSpec as P

M = 1024
FS = 4096
NG = 16384
FR = 64


TWO_PI = 2.0 * math.pi
BEAM_SLOPE = 0.66


def phase_table(first_ids, second_ids, factor):
    product = first_ids[:, None] * second_ids[None, :] % NG
    angles = product.astype(jnp.float32) * (TWO_PI / NG)
    return (
        (jnp.cos(angles) * factor).astype(jnp.bfloat16),
        (jnp.sin(angles) * factor).astype(jnp.bfloat16),
    )


def complex_product(left_real, left_imag, right_real, right_imag):
    left_rows = jnp.concatenate([left_real, left_imag], axis=0)
    right_cols = jnp.concatenate([right_real, right_imag], axis=1)
    product = jnp.dot(left_rows, right_cols, preferred_element_type=jnp.float32)
    product = product.reshape(2, left_real.shape[0], 2, right_real.shape[1])
    real_part = product[0, :, 0] - product[1, :, 1]
    imag_part = product[0, :, 1] + product[1, :, 0]
    return (real_part, imag_part)


def local(visibilities, col_offsets, row_offsets, facet_offsets, facet_order, vis_counts):
    col_count = lax.axis_size("col")
    row_count = lax.axis_size("row")
    col_index = lax.axis_index("col")
    row_index = lax.axis_index("row")
    facets = facet_order.shape[0]
    block_cols = FS // row_count
    slot_pick = (facet_order[:, None] == jnp.arange(facets, dtype=jnp.int32)[None, :]).astype(
        jnp.int32
    )
    slot_offsets = jnp.sum(slot_pick[:, :, None] * facet_offsets[None, :, :], axis=1)
    own_pick = (jnp.arange(facets, dtype=jnp.int32) == col_index).astype(jnp.int32)
    own_facet = jnp.sum(slot_offsets * own_pick[:, None], axis=0)
    row_ids = jnp.arange(M, dtype=jnp.int32)
    live_rows = row_ids < vis_counts[0, 0]
    masked = jnp.where(live_rows[None, :, None], visibilities, jnp.zeros_like(visibilities))
    grid_u = col_offsets[0] + row_ids
    pixel_rows = jnp.arange(FR, dtype=jnp.int32) + (FS // 2 - FR // 2)
    first_scale = 1.0 / math.sqrt(M * col_count)
    second_scale = 0.5 / math.sqrt(M * row_count)
    chosen = slot_offsets[:, 0]
    image_rows = ((chosen[:, None] + pixel_rows[None, :]) % NG).reshape(
        1 * lax.axis_size("col") * FR
    )
    table_real, table_imag = phase_table(image_rows, grid_u, first_scale)
    part_real, part_imag = complex_product(table_real, table_imag, masked[0], masked[1])
    facet_partial = lax.psum_scatter(
        jnp.stack(
            [
                part_real.reshape(1 * lax.axis_size("col"), FR, M),
                part_imag.reshape(1 * lax.axis_size("col"), FR, M),
            ],
            axis=1,
        ),
        "col",
        scatter_dimension=0,
        tiled=True,
    )[0]
    columns = facet_partial.astype(jnp.bfloat16)
    image_cols = (
        own_facet[1] + row_index * block_cols + jnp.arange(block_cols, dtype=jnp.int32)
    ) % NG
    slab_piece = lax.all_gather(columns, "row", axis=2, tiled=True)
    pieces = slab_piece.shape[2] // M
    grid_many = (row_offsets[:, None] + row_ids[None, :]).reshape(pieces * M)
    second_real, second_imag = phase_table(grid_many, image_cols, second_scale)
    out_real, out_imag = complex_product(slab_piece[0], slab_piece[1], second_real, second_imag)
    facet_block = jnp.stack([out_real, out_imag], axis=0)
    beam_cols = (row_index * block_cols + jnp.arange(block_cols, dtype=jnp.int32)).astype(
        jnp.float32
    )
    beam = 1.0 - BEAM_SLOPE * (beam_cols + 0.5) / FS
    facet_images = facet_block / beam[None, None, :]
    magnitude = jnp.sqrt(facet_images[0] * facet_images[0] + facet_images[1] * facet_images[1])
    local_peak = jnp.max(magnitude)
    peak = lax.pmax(local_peak[None], "row")
    return (facet_images[None], peak)


def solution(mesh):
    in_specs = (P(None, "col", "row"), P("col"), P(), P(), P(), P("col", "row"))
    out_specs = (P("col", None, None, "row"), P("col"))
    return jax.shard_map(local, mesh=mesh, in_specs=in_specs, out_specs=out_specs, check_vma=False)
```

profile of v0, /device:TPU:0, one launch (start us, length us, event | category | flops | bytes accessed | tf_op | source)
XLA Modules:
  0.0 214.2 jit_solution(18039350447489056323)
XLA Ops:
  7.2 0.0 reduce-scatter.2.cloned.1.call-start
  7.2 0.7 fusion.31
  7.9 0.8 multiply_reduce_fusion
  8.8 0.1 broadcast_add_fusion
  8.8 0.1 add.171
  10.3 2.5 %broadcast_select_fusion = bf16[2,1024,1024]{2,1,0:T(8,128)(2,1)S(1)} fusion(bf16[2,1024,1024]{2,1,0:T(8,128)(2,1)} %param.6, pred[1024]{0:T(1024)(128)(4,1)S(1)} %iota_compare_fusion), kind=kLoop, calls=%fused_computation.19 | loop fusion | flops 2097152 | bytes 8389632 | tf_op jit(solution)/shard_map/jit(_where)/select_n | solution.py:52
  12.8 0.4 slice_bitcast_fusion.1
  13.3 9.1 %multiply_convert_fusion.3 = (bf16[512,1024]{1,0:T(8,128)(2,1)S(1)}, bf16[512,1024]{1,0:T(8,128)(2,1)S(1)}) fusion(s32[1024]{0:T(1024)S(1)} %iota_add_fusion, s32[512]{0:T(512)S(1)} %add_select_fusion.3), kind=kLoop, calls=%fused_computation.36 | loop fusion | flops 9437184 | bytes 2103296 | tf_op jit(solution)/shard_map/convert_element_type | solution.py:22
  22.4 6.9 %fusion.7 = f32[1024,2048]{1,0:T(8,128)} fusion(bf16[1024,1024]{1,0:T(8,128)(2,1)S(1)} %get-tuple-element.5, bf16[1024,1024]{1,0:T(8,128)(2,1)S(1)} %get-tuple-element.4, bf16[512,1024]{1,0:T(8,128)(2,1)S(1)} %get-tuple-element.19, bf16[512,1024]{1,0:T(8,128)(2,1)S(1)} %get-tuple-element.18), kind=kOutput, calls=%fused_computation.14 | convolution fusion | flops 4307550208 | bytes 14680064 | tf_op jit(solution)/shard_map/dot_general | solution.py:30
  29.2 11.7 %reshape.233 = f32[2,512,2,1024]{3,2,1,0:T(2,128)} reshape(f32[1024,2048]{1,0:T(8,128)} %fusion.7) | data formatting | bytes 16777216 | tf_op jit(solution)/shard_map/reshape | solution.py:31
  41.0 10.9 %slice_subtract_fusion = (f32[1,512,1,1024]{3,2,1,0:T(1,128)S(1)}, f32[1,512,1,1024]{3,2,1,0:T(1,128)S(1)}) fusion(f32[2,512,2,1024]{3,2,1,0:T(2,128)} %reshape.233), kind=kLoop, calls=%fused_computation.29 | loop fusion | flops 1048576 | bytes 12582912 | tf_op jit(solution)/shard_map/sub | solution.py:32
  51.8 0.5 copy.23
  52.3 0.5 copy.24
  52.8 2.4 %pad_maximum_fusion = f32[8,2,64,1024]{3,2,1,0:T(8,128)} fusion(f32[8,1,64,1024]{3,2,1,0:T(8,128)S(1)} %bitcast.32, f32[8,1,64,1024]{3,2,1,0:T(8,128)S(1)} %bitcast.31), kind=kLoop, calls=%fused_computation.18 | loop fusion | flops 1048576 | bytes 8388608 | tf_op jit(solution)/shard_map/stack | solution.py:64
  55.2 0.0 reduce-scatter.2.cloned.1.call-update
  55.2 0.2 all-gather.3.cloned.1.call-start
  55.5 0.1 multiply_reduce_fusion.1
  55.6 0.6 slice.59
  56.2 0.1 add_bitcast_fusion
  57.0 52.3 %reduce-scatter.2.cloned.1.call-done = f32[1,2,64,1024]{3,2,1,0:T(8,128)} async-done(((f32[8,2,64,1024]{3,2,1,0:T(8,128)}), f32[1,2,64,1024]{3,2,1,0:T(8,128)}) %reduce-scatter.2.cloned.1.call-update) | async-done | bytes 524304 | tf_op jit(solution)/shard_map/reduce_scatter | solution.py:63
  109.3 1.8 convert_element_type.49
  111.1 0.0 all-gather.3.cloned.1.call-update
  111.1 71.4 %multiply_convert_fusion.1 = (bf16[4096,1024]{1,0:T(8,128)(2,1)}, bf16[4096,1024]{1,0:T(8,128)(2,1)}) fusion(s32[1024]{0:T(1024)S(1)} %add_select_fusion.2, s32[4096]{0:T(1024)S(1)} %bitcast.33), kind=kLoop, calls=%fused_computation.13 | loop fusion | flops 75497472 | bytes 16797696 | tf_op jit(solution)/shard_map/convert_element_type | solution.py:22
  182.5 1.3 slice_bitcast_fusion.3
  183.8 7.8 %fusion.3 = f32[128,2048]{1,0:T(8,128)S(1)} fusion(bf16[4096,1024]{1,0:T(8,128)(2,1)} %get-tuple-element.17, bf16[4096,1024]{1,0:T(8,128)(2,1)} %get-tuple-element.16, bf16[64,4096]{1,0:T(8,128)(2,1)S(1)} %get-tuple-element.11, bf16[64,4096]{1,0:T(8,128)(2,1)S(1)} %get-tuple-element.10), kind=kOutput, calls=%fused_computation.8 | convolution fusion | flops 2183135232 | bytes 18874368 | tf_op jit(solution)/shard_map/dot_general | solution.py:30
  191.5 0.9 reshape.234
  192.4 0.8 fusion.35
  193.2 0.2 fusion.23
  193.4 0.1 maximum_divide_fusion.1
  193.5 0.7 fusion.22
  194.2 12.3 %pmax.7 = f32[1]{0:T(128)} all-reduce(f32[1]{0:T(128)} %bitcast.12), channel_id=1, replica_groups=mesh['col'=8,'row'=4] {'row'}, use_global_device_ids=true, to_apply=%region_4.5 | all-reduce | flops 1 | bytes 8 | tf_op jit(solution)/shard_map/pmax | solution.py:92
  206.5 0.9 maximum_divide_fusion
  (12 shorter events, 0.1 us)
Async XLA Ops:
  7.2 102.1 %reduce-scatter.2.cloned.1.call-start = ((), (), s32[]{:S(2)}) async-start(), calls=%async_computation.1 | async-start | bytes 4718592 | tf_op jit(solution)/shard_map/reduce_scatter | solution.py:63
  55.2 1.0 copy-start
  55.2 127.2 %all-gather.3.cloned.1.call-start = ((), (), s32[]{:S(2)}) async-start(), calls=%async_computation.2 | async-start | bytes 1310720 | tf_op jit(solution)/shard_map/all_gather | solution.py:79
Sparse Core Ops, SparseCore 0:
  55.4 53.8 reduce-scatter.1
  111.4 27.9 all-gather.2
where the time goes:
time: 215 us; the launch traced here: 214 us
  other arithmetic  102 us (47%)
  waiting for transfers between devices  52.4 us (24%)
  local copies, waits for them, and re-layouts  16.8 us (8%)
  between operations  16.1 us (7%)
  matrix products  14.6 us (7%)
  blocking collectives  12.3 us (6%)
    convert_element_type x2, other arithmetic, phase_table(): (jnp.cos(angles) * factor).astype(jnp.bfloat16)  80.4 us
    reduce_scatter x1, waiting for transfers between devices, local(): lax.psum_scatter(jnp.stack([part_real.reshape(1 * lax.axis_size('col'), F...  52.3 us
    dot_general x2, matrix products, complex_product(): product = jnp.dot(left_rows, right_cols, preferred_element_type=jnp.float32)  14.6 us
    reshape x2, local copies, waits for them, and re-layouts, complex_product(): product = product.reshape(2, left_real.shape[0], 2, right_real.shape[1])  12.6 us
    pmax x1, blocking collectives, local(): peak = lax.pmax(local_peak[None], 'row')  12.3 us
    sub x2, other arithmetic, complex_product(): real_part = product[0, :, 0] - product[1, :, 1]  11.1 us
  transfers between devices with their start and end apart: 2, of which 1 were waited for; matrix products, arithmetic and copies ran while one was open for 34% of the time, Pallas kernels for 0%

commit v1 on v0

v1 whole, which is shorter than its diff:
```python
import functools
import math

import jax
import jax.numpy as jnp
from jax import lax
from jax.experimental import pallas as pl
from jax.experimental.pallas import tpu as pltpu
from jax.sharding import PartitionSpec as P

FS = 4096
NG = 16384
FR = 64
BEAM_SLOPE = 0.66
LANES = 128
TILE = 8
MIB = 1 << 20
VMEM = pl.BlockSpec(memory_space=pltpu.VMEM)
SMEM = pl.BlockSpec(memory_space=pltpu.SMEM)
HBM = pl.BlockSpec(memory_space=pl.ANY)


def cis(phase):
    quarter = NG // 4
    turned = phase + quarter // 2
    quadrant = (turned & (NG - 1)) // quarter
    rest = (turned & (quarter - 1)) - quarter // 2
    t = rest.astype(jnp.float32) * (2.0 * math.pi / NG)
    t2 = t * t
    s = t * (1 + t2 * (-1 / 6 + t2 * (1 / 120 + t2 * (-1 / 5040 + t2 * (1 / 362880)))))
    c = 1 + t2 * (-1 / 2 + t2 * (1 / 24 + t2 * (-1 / 720 + t2 * (1 / 40320))))
    odd = (quadrant & 1) == 1
    real = jnp.where(odd, s, c)
    imag = jnp.where(odd, c, s)
    real = jnp.where((quadrant == 1) | (quadrant == 2), -real, real)
    imag = jnp.where(quadrant >= 2, -imag, imag)
    return real, imag


def times(a, b):
    return a[0] * b[0] - a[1] * b[1], a[0] * b[1] + a[1] * b[0]


def iota(shape, dim):
    return lax.broadcasted_iota(jnp.int32, shape, dim)


def stacked_rows(values, height):
    row = iota((height, 1), 0)
    result = jnp.zeros((height, 1), jnp.int32)
    for k, value in enumerate(values):
        result = jnp.where(row == k, value, result)
    return result


def store_stacked(ref, row, high, depth, real, imag):
    h = real.shape[0]
    real, imag, minus = (x.astype(jnp.bfloat16) for x in (real, imag, -imag))
    ref[row : row + h, :depth] = real
    ref[row : row + h, depth:] = minus
    ref[row + high : row + high + h, :depth] = imag
    ref[row + high : row + high + h, depth:] = real


def column_kernel(flip, slots, scale, offs, order, col, count, vis, out, table, fine):
    depth = vis.shape[1]

    @pl.when(pl.program_id(0) == 0)
    def build():
        c = lax.axis_index("col")
        lane = iota((TILE, depth), 1)
        sub = iota((TILE, depth), 0)
        u = col[0] + lane
        few = cis(u * sub)
        many = cis(u * (sub * TILE))
        starts = []
        for k in range(slots):
            slot = (((c // 2) ^ k) * 2) + ((c % 2) ^ flip)
            starts.append((offs[order[slot], 0] + (FS // 2 - FR // 2)) % NG)
        height = -(-slots // TILE) * TILE
        xs = cis((col[0] + iota((height, depth), 1)) * stacked_rows(starts, height))
        live = jnp.where(iota((height, depth), 1) < count[0, 0], scale, 0.0)
        xs = (xs[0] * live, xs[1] * live)
        for k in range(slots):
            x = tuple(jnp.broadcast_to(v[k : k + 1], (TILE, depth)) for v in xs)
            xa = times(x, many)
            fine[0], fine[1] = xa
            for a in range(0, FR // TILE, 2):
                parts = []
                for step in range(2):
                    row = tuple(
                        jnp.broadcast_to(fine[z, a + step : a + step + 1, :], (TILE, depth)) for z in range(2)
                    )
                    parts.append(times(row, few))
                real = jnp.concatenate([parts[0][0], parts[1][0]], axis=0)
                imag = jnp.concatenate([parts[0][1], parts[1][1]], axis=0)
                store_stacked(table, k * 2 * FR + a * TILE, FR, depth, real, imag)

    right = vis[...].reshape(2 * depth, vis.shape[2])
    out[...] = jnp.dot(table[...], right, preferred_element_type=jnp.float32).astype(out.dtype)


def columns_of(flip, slots, scale, offs, order, col, count, vis):
    _, depth, width = vis.shape
    block = 256
    rows = slots * 2 * FR
    return pl.pallas_call(
        functools.partial(column_kernel, flip, slots, scale),
        grid=(width // block,),
        in_specs=[SMEM, SMEM, SMEM, SMEM, pl.BlockSpec((2, depth, block), lambda n: (0, 0, n))],
        out_specs=pl.BlockSpec((rows, block), lambda n: (0, n)),
        out_shape=jax.ShapeDtypeStruct((rows, width), jnp.bfloat16),
        scratch_shapes=[
            pltpu.VMEM((rows, 2 * depth), jnp.bfloat16),
            pltpu.VMEM((2, TILE, depth), jnp.float32),
        ],
        compiler_params=pltpu.CompilerParams(vmem_limit_bytes=20 * MIB),
        cost_estimate=pl.CostEstimate(
            flops=rows * 4 * depth * width, bytes_accessed=4 * depth * width, transcendentals=0
        ),
        name=f"columns_{flip}",
    )(offs, order, col, count, vis)


def wave_kernel(after, out):
    del after
    depth, width = out.shape[0] // 2, out.shape[1]
    lane = iota((TILE, width), 1)
    sub = iota((TILE, width), 0)
    few = cis(lane * sub)

    def body(block, carry):
        coarse = cis(lane * ((block * TILE + sub) * TILE))
        base = block * (TILE * TILE)
        for a in range(0, TILE, 2):
            parts = [
                times(tuple(jnp.broadcast_to(v[a + s : a + s + 1], (TILE, width)) for v in coarse), few)
                for s in range(2)
            ]
            row = pl.multiple_of(base + a * TILE, 2 * TILE)
            for z in range(2):
                value = jnp.concatenate([parts[0][z], parts[1][z]], axis=0)
                out[pl.ds(row + z * depth, 2 * TILE), :] = value.astype(out.dtype)
        return carry

    lax.fori_loop(0, depth // (TILE * TILE), body, 0)


def waves(after, depth, width):
    return pl.pallas_call(
        wave_kernel,
        in_specs=[HBM],
        out_specs=VMEM,
        out_shape=jax.ShapeDtypeStruct((2 * depth, width), jnp.bfloat16),
        compiler_params=pltpu.CompilerParams(vmem_limit_bytes=20 * MIB),
        cost_estimate=pl.CostEstimate(flops=4 * 10**9, bytes_accessed=4 * depth * width, transcendentals=0),
        name="waves",
    )(after)


def row_kernel(scale, rows, offs, order, roff, *refs):
    pieces, wave, outs = refs[:rows], refs[rows], refs[rows + 1 : 2 * rows + 1]
    left, turned = refs[2 * rows + 1 :]
    depth = pieces[0].shape[1]
    high = pieces[0].shape[0] // 2
    width = wave.shape[1]
    r = lax.axis_index("row")
    start = offs[order[lax.axis_index("col")], 1]
    height = -(-rows // TILE) * TILE
    sources = [roff[r ^ p] for p in range(rows)]
    blocks = stacked_rows([(start + (r ^ b) * width) % NG for b in range(rows)], height)
    for p in range(rows):
        phase = cis((sources[p] + iota((height, depth), 1)) * blocks)
        turned[0], turned[1] = phase[0] * scale, phase[1] * scale
        value = pieces[p][...].astype(jnp.float32)
        value = (value[:high], value[high:])
        for b in range(rows):
            turn = tuple(jnp.broadcast_to(turned[z, b : b + 1, :], (high, depth)) for z in range(2))
            real, imag = times(value, turn)
            store_stacked(left, (p * rows + b) * 2 * high, high, depth, real, imag)
    lane = iota((height, width), 1)
    after = cis(lane * stacked_rows(sources, height))
    piece = min(2 * LANES, width)
    largest = jnp.zeros((high, LANES), jnp.float32)
    for n in range(0, width, piece):
        product = jnp.dot(left[...], wave[:, n : n + piece], preferred_element_type=jnp.float32)
        for b in range(rows):
            real = imag = None
            for p in range(rows):
                at = (p * rows + b) * 2 * high
                value = (product[at : at + high], product[at + high : at + 2 * high])
                turn = tuple(v[p : p + 1, n : n + piece] for v in after)
                x, y = times(value, turn)
                real = x if real is None else real + x
                imag = y if imag is None else imag + y
            j = ((r ^ b) * width + n + iota((1, piece), 1)).astype(jnp.float32)
            beam = 1.0 / (1.0 - BEAM_SLOPE * (j + 0.5) / FS)
            real = real * beam
            imag = imag * beam
            power = real * real + imag * imag
            for m in range(0, piece, LANES):
                at = (n + m) // LANES * 2 * high
                outs[b][at : at + high] = real[:, m : m + LANES].astype(jnp.bfloat16)
                outs[b][at + high : at + 2 * high] = imag[:, m : m + LANES].astype(jnp.bfloat16)
                largest = jnp.maximum(largest, power[:, m : m + LANES])
    peak = jnp.broadcast_to(jnp.sqrt(jnp.max(largest, keepdims=True)), (2 * TILE, LANES))
    first = peak.astype(jnp.bfloat16).astype(jnp.float32)
    second = (peak - first).astype(jnp.bfloat16).astype(jnp.float32)
    third = peak - first - second
    sub = iota((2 * TILE, LANES), 0)
    peak = jnp.where(sub == 0, first, jnp.where(sub == 1, second, jnp.where(sub == 2, third, 0.0)))
    for b in range(rows):
        outs[b][width // LANES * 2 * high :] = peak.astype(jnp.bfloat16)


def rows_of(scale, offs, order, roff, pieces, wave):
    rows = len(pieces)
    double, depth = pieces[0].shape
    width = wave.shape[1]
    shape = jax.ShapeDtypeStruct((width // LANES * double + 2 * TILE, LANES), jnp.bfloat16)
    return pl.pallas_call(
        functools.partial(row_kernel, scale, rows),
        in_specs=[SMEM] * 3 + [VMEM] * (rows + 1),
        out_specs=[VMEM] * rows,
        out_shape=[shape] * rows,
        scratch_shapes=[
            pltpu.VMEM((rows * rows * double, 2 * depth), jnp.bfloat16),
            pltpu.VMEM((2, -(-rows // TILE) * TILE, depth), jnp.float32),
        ],
        compiler_params=pltpu.CompilerParams(vmem_limit_bytes=32 * MIB),
        cost_estimate=pl.CostEstimate(
            flops=rows * rows * double * 4 * depth * width, bytes_accessed=4 * depth * width, transcendentals=0
        ),
        name="rows",
    )(offs, order, roff, *pieces, wave)


def finish_kernel(rows, *refs):
    pieces, (image, peak) = refs[:rows], refs[rows:]
    width = image.shape[3]
    high = image.shape[2] // rows
    r = lax.axis_index("row")
    largest = None
    for p in range(rows):
        for n in range(0, width, LANES):
            row = n // LANES * 2 * high
            if high % TILE == 0:
                at = pl.ds(pl.multiple_of((r ^ p) * high, high), high)
                value = pieces[p][row : row + 2 * high, :].astype(jnp.float32)
            else:
                at = pl.ds(p * high, high)
                value = pieces[0][row : row + 2 * high, :].astype(jnp.float32)
                for q in range(1, rows):
                    other = pieces[q][row : row + 2 * high, :].astype(jnp.float32)
                    value = jnp.where((r ^ p) == q, other, value)
            image[0, 0, at, n : n + LANES] = value[:high]
            image[0, 1, at, n : n + LANES] = value[high:]
        parts = pieces[p][width // LANES * 2 * high :, :].astype(jnp.float32)
        value = (parts[0:1] + parts[1:2]) + parts[2:3]
        largest = value if largest is None else jnp.maximum(largest, value)
    peak[0] = jnp.max(largest)


def finish(pieces, width):
    rows = len(pieces)
    return pl.pallas_call(
        functools.partial(finish_kernel, rows),
        in_specs=[VMEM] * rows,
        out_specs=[VMEM, SMEM],
        out_shape=[
            jax.ShapeDtypeStruct((1, 2, FR, width), jnp.float32),
            jax.ShapeDtypeStruct((1,), jnp.float32),
        ],
        compiler_params=pltpu.CompilerParams(vmem_limit_bytes=16 * MIB),
        name="finish",
    )(*pieces)


def local(visibilities, col_offsets, row_offsets, facet_offsets, facet_order, vis_counts):
    cols = lax.axis_size("col")
    rows = lax.axis_size("row")
    _, depth, width = visibilities.shape
    slots = cols // 2
    high = FR // rows
    scalars = (facet_offsets, facet_order, col_offsets, vis_counts)
    first_scale = 1.0 / math.sqrt(depth * cols)
    second_scale = 0.5 / math.sqrt(width * rows)

    def swap(value, axis, count, bit):
        return lax.ppermute(value, axis, [(i, i ^ bit) for i in range(count)])

    given = columns_of(1, slots, first_scale, *scalars, visibilities)
    taken = swap(given, "col", cols, 1)
    mine = columns_of(0, slots, first_scale, *scalars, visibilities)
    pair = (mine.astype(jnp.float32) + taken.astype(jnp.float32)).reshape(slots, 2 * FR, width)
    total = pair[0]
    sent = [swap(pair[k].astype(jnp.bfloat16), "col", cols, 2 * k) for k in range(1, slots)]
    wave = waves(mine, width, FS // rows)
    for value in sent:
        total = total + value.astype(jnp.float32)
    total = total.astype(jnp.bfloat16).reshape(2, FR, width)
    r = lax.axis_index("row")
    pieces = []
    for p in range(rows):
        part = lax.dynamic_slice_in_dim(total, (r ^ p) * high, high, 1).reshape(2 * high, width)
        pieces.append(part if p == 0 else swap(part, "row", rows, p))
    parts = rows_of(second_scale, facet_offsets, facet_order, row_offsets, pieces, wave)
    parts = [part if p == 0 else swap(part, "row", rows, p) for p, part in enumerate(parts)]
    image, peak = finish(parts, FS // rows)
    return image, peak


def solution(mesh):
    in_specs = (P(None, "col", "row"), P("col"), P(), P(), P(), P("col", "row"))
    out_specs = (P("col", None, None, "row"), P("col"))
    return jax.shard_map(local, mesh=mesh, in_specs=in_specs, out_specs=out_specs, check_vma=False)
```

time: 215 us -> 58.7 us (0.27)
  other arithmetic: 102 us -> 1.65 us
  waiting for transfers between devices: 52.4 us -> 20.8 us
  Pallas kernels: 0 us -> 16.3 us
  matrix products: 14.6 us -> 0 us
  between operations: 16.1 us -> 2.01 us
  starting transfers between devices: 0.26 us -> 13.3 us
  blocking collectives: 12.3 us -> 0 us
  local copies, waits for them, and re-layouts: 16.8 us -> 4.51 us
    convert_element_type x5 -> x1, other arithmetic: 82.9 us -> 1.18 us  [local(): total = total.astype(jnp.bfloat16).reshape(2, FR, width)]
    reduce_scatter x1 -> x0, waiting for transfers between devices: 52.3 us -> none  [local(): lax.psum_scatter(jnp.stack([part_real.reshape(1 * lax.axis_size('col'), F...]
    ppermute x0 -> x10, waiting for transfers between devices: none -> 20.8 us  [swap(): return lax.ppermute(value, axis, [(i, i ^ bit) for i in range(count)])]
    pallas_call x0 -> x5, Pallas kernels: none -> 16.3 us  [the longest x2 9.39 us: columns_of(): pl.pallas_call(functools.partial(column_kernel, flip, slots, scale), grid...]
    dot_general x2 -> x0, matrix products: 14.6 us -> none  [complex_product(): product = jnp.dot(left_rows, right_cols, preferred_element_type=jnp.float32)]
    ppermute x0 -> x10, starting transfers between devices: none -> 13.3 us  [swap(): return lax.ppermute(value, axis, [(i, i ^ bit) for i in range(count)])]
    reshape x2 -> x0, local copies, waits for them, and re-layouts: 12.6 us -> none  [complex_product(): product = product.reshape(2, left_real.shape[0], 2, right_real.shape[1])]
    pmax x1 -> x0, blocking collectives: 12.3 us -> none  [local(): peak = lax.pmax(local_peak[None], 'row')]
  transfers between devices with their start and end apart: 2 -> 10, of which waited for: 1 -> 7; matrix products, arithmetic and copies ran while one was open for 34% -> 0% of each run, Pallas kernels for 0% -> 12%
where the time goes in v1:
time: 58.7 us; the launch traced here: 58.5 us
  waiting for transfers between devices  20.8 us (35%)
  Pallas kernels  16.3 us (28%)
  starting transfers between devices  13.3 us (23%)
  local copies, waits for them, and re-layouts  4.51 us (8%)
  between operations  2.01 us (3%)
  other arithmetic  1.65 us (3%)
    ppermute x10, waiting for transfers between devices, swap(): return lax.ppermute(value, axis, [(i, i ^ bit) for i in range(count)])  20.8 us
    ppermute x10, starting transfers between devices, swap(): return lax.ppermute(value, axis, [(i, i ^ bit) for i in range(count)])  13.3 us
    pallas_call x2, Pallas kernels, columns_of(): pl.pallas_call(functools.partial(column_kernel, flip, slots, scale), grid...  9.39 us
    unnamed x9, local copies, waits for them, and re-layouts  3.6 us
    pallas_call x1, Pallas kernels, rows_of(): pl.pallas_call(functools.partial(row_kernel, scale, rows), in_specs=[SMEM...  3.49 us
    pallas_call x1, Pallas kernels, waves(): pl.pallas_call(wave_kernel, in_specs=[HBM], out_specs=VMEM, out_shape=jax...  2.53 us
    convert_element_type x1, other arithmetic, local(): total = total.astype(jnp.bfloat16).reshape(2, FR, width)  1.18 us
  transfers between devices with their start and end apart: 10, of which 7 were waited for; matrix products, arithmetic and copies ran while one was open for 0% of the time, Pallas kernels for 12%

profile of v1, /device:TPU:0, one launch (start us, length us, event | category | flops | bytes accessed | tf_op | source)
XLA Modules:
  0.0 58.5 jit_solution(6449037264021679550)
XLA Ops:
  1.9 0.8 %copy.10.offs = s32[8,2]{1,0:T(8,128)S(1)} copy(s32[8,2]{0,1:T(2,128)} %param.9) | data formatting | bytes 128 | tf_op args[3]
  2.7 2.2 %copy-done = bf16[2,1024,1024]{2,1,0:T(8,128)(2,1)S(1)} copy-done((bf16[2,1024,1024]{2,1,0:T(8,128)(2,1)S(1)}, bf16[2,1024,1024]{2,1,0:T(8,128)(2,1)}, u32[]{:S(2)}) %copy-start) | copy-done | bytes 4194328
  4.9 0.7 %copy-done.1 = s32[8]{0:T(128)S(1)} copy-done((s32[8]{0:T(128)S(1)}, s32[8]{0:T(128)}, u32[]{:S(2)}) %copy-start.1) | copy-done | bytes 56
  5.5 4.7 %columns_1.1 = bf16[512,1024]{1,0:T(8,128)(2,1)S(1)} custom-call(s32[8,2]{1,0:T(8,128)S(1)} %copy.10.offs, s32[8]{0:T(128)S(1)} %copy-done.1, s32[1]{0:T(128)S(6)} %copy.11.col, s32[1,1]{1,0:T(1,128)S(6)} %copy.12.count, bf16[2,1024,1024]{2,1,0:T(8,128)(2,1)S(1)} %copy-done), custom_call_target="tpu_custom_call" | custom-call | flops 2147483648 | bytes 4194304 | tf_op jit(solution)/shard_map/columns_1/pallas_call | solution.py:107
  10.2 0.6 collective-permute-start
  10.8 4.7 %columns_0.1.after = bf16[512,1024]{1,0:T(8,128)(2,1)S(1)} custom-call(s32[8,2]{1,0:T(8,128)S(1)} %copy.10.offs, s32[8]{0:T(128)S(1)} %copy-done.1, s32[1]{0:T(128)S(6)} %copy.11.col, s32[1,1]{1,0:T(1,128)S(6)} %copy.12.count, bf16[2,1024,1024]{2,1,0:T(8,128)(2,1)S(1)} %copy-done), custom_call_target="tpu_custom_call" | custom-call | flops 2147483648 | bytes 4194304 | tf_op jit(solution)/shard_map/columns_0/pallas_call | solution.py:107
  15.5 0.0 collective-permute-done
  15.5 0.5 fusion.3
  16.0 0.9 %fusion.4 = (bf16[128,1024]{1,0:T(8,128)(2,1)}, bf16[128,1024]{1,0:T(8,128)(2,1)}, bf16[128,1024]{1,0:T(8,128)(2,1)}) fusion(bf16[512,1024]{1,0:T(8,128)(2,1)S(1)} %get-tuple-element.10), kind=kLoop, calls=%fused_computation.10 | loop fusion | bytes 1572864 | tf_op jit(solution)/shard_map/slice | solution.py:297
  16.8 2.5 %collective-permute-start.1 = (bf16[128,1024]{1,0:T(8,128)(2,1)}, bf16[128,1024]{1,0:T(8,128)(2,1)S(1)}, u32[]{:S(2)}, u32[]{:S(2)}) collective-permute-start(bf16[128,1024]{1,0:T(8,128)(2,1)} %get-tuple-element.12), channel_id=1, source_target_pairs={{0,8},{4,12},{8,0},{12,4},{16,24},{20,28},{24,16},{28,20},{1,9},{5... | collective-permute-start | bytes 786440 | tf_op jit(solution)/shard_map/ppermute | solution.py:290
  19.4 1.5 %collective-permute-start.3 = (bf16[128,1024]{1,0:T(8,128)(2,1)}, bf16[128,1024]{1,0:T(8,128)(2,1)}, u32[]{:S(2)}, u32[]{:S(2)}) collective-permute-start(bf16[128,1024]{1,0:T(8,128)(2,1)} %get-tuple-element.13), channel_id=1, source_target_pairs={{0,24},{4,28},{8,16},{12,20},{16,8},{20,12},{24,0},{28,4},{1,25},{... | collective-permute-start | bytes 786440 | tf_op jit(solution)/shard_map/ppermute | solution.py:290
  20.8 0.0 collective-permute-start.2
  20.9 5.8 %collective-permute-done.1 = bf16[128,1024]{1,0:T(8,128)(2,1)S(1)} collective-permute-done((bf16[128,1024]{1,0:T(8,128)(2,1)}, bf16[128,1024]{1,0:T(8,128)(2,1)S(1)}, u32[]{:S(2)}, u32[]{:S(2)}) %collective-permute-start.1) | collective-permute-done | bytes 262176 | tf_op jit(solution)/shard_map/ppermute | solution.py:290
  26.7 6.8 %collective-permute-done.3 = bf16[128,1024]{1,0:T(8,128)(2,1)} collective-permute-done((bf16[128,1024]{1,0:T(8,128)(2,1)}, bf16[128,1024]{1,0:T(8,128)(2,1)}, u32[]{:S(2)}, u32[]{:S(2)}) %collective-permute-start.3) | collective-permute-done | bytes 262176 | tf_op jit(solution)/shard_map/ppermute | solution.py:290
  33.5 1.4 %collective-permute-done.2 = bf16[128,1024]{1,0:T(8,128)(2,1)} collective-permute-done((bf16[128,1024]{1,0:T(8,128)(2,1)}, bf16[128,1024]{1,0:T(8,128)(2,1)}, u32[]{:S(2)}, u32[]{:S(2)}) %collective-permute-start.2) | collective-permute-done | bytes 262176 | tf_op jit(solution)/shard_map/ppermute | solution.py:290
  34.9 1.2 %fusion.2 = bf16[128,1024]{1,0:T(8,128)(2,1)S(1)} fusion(f32[512,1024]{1,0:T(8,128)S(1)} %get-tuple-element.11, bf16[128,1024]{1,0:T(8,128)(2,1)} %collective-permute-done.3, bf16[128,1024]{1,0:T(8,128)(2,1)} %collective-permute-done.2, bf16[128,1024]{1,0:T(8,128)(2,1)S(1)} %collective-permute-done.1), kind=kLoop, calls=%fused_computation.4 | loop fusion | flops 917504 | bytes 1572864 | tf_op jit(solution)/shard_map/convert_element_type | solution.py:301
  36.1 2.7 %collective-permute-start.5 = (bf16[32,1024]{1,0:T(8,128)(2,1)S(1)}, bf16[32,1024]{1,0:T(8,128)(2,1)S(1)}, u32[]{:S(2)}, u32[]{:S(2)}) collective-permute-start(bf16[32,1024]{1,0:T(8,128)(2,1)S(1)} %bitcast.9), channel_id=1, source_target_pairs={{0,2},{1,3},{2,0},{3,1},{4,6},{5,7},{6,4},{7,5},{8,10},{9,11},{10,... | collective-permute-start | bytes 196616 | tf_op jit(solution)/shard_map/ppermute | solution.py:290
  38.8 1.4 %collective-permute-start.6 = (bf16[32,1024]{1,0:T(8,128)(2,1)S(1)}, bf16[32,1024]{1,0:T(8,128)(2,1)S(1)}, u32[]{:S(2)}, u32[]{:S(2)}) collective-permute-start(bf16[32,1024]{1,0:T(8,128)(2,1)S(1)} %bitcast.8), channel_id=1, source_target_pairs={{0,3},{1,2},{2,1},{3,0},{4,7},{5,6},{6,5},{7,4},{8,11},{9,10},{10,... | collective-permute-start | bytes 196616 | tf_op jit(solution)/shard_map/ppermute | solution.py:290
  40.1 0.2 collective-permute-start.4
  40.4 2.5 %waves.1.refs_4_ = bf16[2048,1024]{1,0:T(8,128)(2,1)S(1)} custom-call(bf16[512,1024]{1,0:T(8,128)(2,1)S(1)} %columns_0.1.after), custom_call_target="tpu_custom_call" | custom-call | flops 4000000000 | bytes 4194304 | tf_op jit(solution)/shard_map/waves/pallas_call | solution.py:150
  42.9 0.0 collective-permute-done.5.refs_2_
  42.9 2.0 %collective-permute-done.6.refs_3_ = bf16[32,1024]{1,0:T(8,128)(2,1)S(1)} collective-permute-done((bf16[32,1024]{1,0:T(8,128)(2,1)S(1)}, bf16[32,1024]{1,0:T(8,128)(2,1)S(1)}, u32[]{:S(2)}, u32[]{:S(2)}) %collective-permute-start.6) | collective-permute-done | bytes 65568 | tf_op jit(solution)/shard_map/ppermute | solution.py:290
  45.0 0.2 collective-permute-done.4.refs_1_
  45.1 0.0 copy-done.2
  45.1 3.5 %rows.1 = (bf16[272,128]{1,0:T(8,128)(2,1)S(1)}, bf16[272,128]{1,0:T(8,128)(2,1)S(1)}, bf16[272,128]{1,0:T(8,128)(2,1)S(1)}, bf16[272,128]{1,0:T(8,128)(2,1)S(1)}) custom-call(s32[8,2]{1,0:T(8,128)S(1)} %copy.10.offs, s32[8]{0:T(128)S(1)} %copy-done.2, s32[4]{0:T(128)S(1)} %copy-done.3, bf16[32,1024]{1,0:T(8,128)(2,1)S(1)} %bitcast.5, ...), custom_call_target="tpu_custom_call" | custom-call | flops 2147483648 | bytes 4194304 | tf_op jit(solution)/shard_map/rows/pallas_call | solution.py:221
  48.6 0.1 collective-permute-start.7
  48.7 2.8 %collective-permute-start.8 = (bf16[272,128]{1,0:T(8,128)(2,1)S(1)}, bf16[272,128]{1,0:T(8,128)(2,1)S(1)}, u32[]{:S(2)}, u32[]{:S(2)}) collective-permute-start(bf16[272,128]{1,0:T(8,128)(2,1)S(1)} %get-tuple-element.8), channel_id=1, source_target_pairs={{0,2},{1,3},{2,0},{3,1},{4,6},{5,7},{6,4},{7,5},{8,10},{9,11},{10,... | collective-permute-start | bytes 208904 | tf_op jit(solution)/shard_map/ppermute | solution.py:290
  51.4 1.6 %collective-permute-start.9 = (bf16[272,128]{1,0:T(8,128)(2,1)S(1)}, bf16[272,128]{1,0:T(8,128)(2,1)S(1)}, u32[]{:S(2)}, u32[]{:S(2)}) collective-permute-start(bf16[272,128]{1,0:T(8,128)(2,1)S(1)} %get-tuple-element.9), channel_id=1, source_target_pairs={{0,3},{1,2},{2,1},{3,0},{4,7},{5,6},{6,5},{7,4},{8,11},{9,10},{10,... | collective-permute-start | bytes 208904 | tf_op jit(solution)/shard_map/ppermute | solution.py:290
  53.1 0.0 collective-permute-done.7.refs_1_
  53.1 3.5 %collective-permute-done.8.refs_2_ = bf16[272,128]{1,0:T(8,128)(2,1)S(1)} collective-permute-done((bf16[272,128]{1,0:T(8,128)(2,1)S(1)}, bf16[272,128]{1,0:T(8,128)(2,1)S(1)}, u32[]{:S(2)}, u32[]{:S(2)}) %collective-permute-start.8) | collective-permute-done | bytes 69664 | tf_op jit(solution)/shard_map/ppermute | solution.py:290
  56.5 1.1 %collective-permute-done.9.refs_3_ = bf16[272,128]{1,0:T(8,128)(2,1)S(1)} collective-permute-done((bf16[272,128]{1,0:T(8,128)(2,1)S(1)}, bf16[272,128]{1,0:T(8,128)(2,1)S(1)}, u32[]{:S(2)}, u32[]{:S(2)}) %collective-permute-start.9) | collective-permute-done | bytes 69664 | tf_op jit(solution)/shard_map/ppermute | solution.py:290
  57.7 0.8 %finish.1 = (f32[1,2,64,1024]{3,2,1,0:T(8,128)}, f32[1]{0:T(128)}) custom-call(bf16[272,128]{1,0:T(8,128)(2,1)S(1)} %get-tuple-element.6.refs_0_, bf16[272,128]{1,0:T(8,128)(2,1)S(1)} %collective-permute-done.7.refs_1_, bf16[272,128]{1,0:T(8,128)(2,1)S(1)} %collective-permute-done.8.refs_2_, bf16[272,128]{1,0:T(8,128)(2,1)S(1)} %collective-permute-done.9.refs_3_), custom_call_target="tpu_custom_call" | custom-call | tf_op jit(solution)/shard_map/finish/pallas_call | solution.py:266
  (6 shorter events, 0.0 us)
Async XLA Ops:
  2.7 2.2 %copy-start = (bf16[2,1024,1024]{2,1,0:T(8,128)(2,1)S(1)}, bf16[2,1024,1024]{2,1,0:T(8,128)(2,1)}, u32[]{:S(2)}) copy-start(bf16[2,1024,1024]{2,1,0:T(8,128)(2,1)} %vis.3) | copy-start | bytes 12582916
  4.9 0.7 %copy-start.1 = (s32[8]{0:T(128)S(1)}, s32[8]{0:T(128)}, u32[]{:S(2)}) copy-start(s32[8]{0:T(128)} %order.5) | copy-start | bytes 100
  10.2 5.3 %collective-permute-start = (bf16[512,1024]{1,0:T(8,128)(2,1)S(1)}, bf16[512,1024]{1,0:T(8,128)(2,1)S(1)}, u32[]{:S(2)}, u32[]{:S(2)}) collective-permute-start(bf16[512,1024]{1,0:T(8,128)(2,1)S(1)} %columns_1.1), channel_id=1, source_target_pairs={{0,4},{4,0},{8,12},{12,8},{16,20},{20,16},{24,28},{28,24},{1,5},{5... | collective-permute-start | bytes 3145736 | tf_op jit(solution)/shard_map/ppermute | solution.py:290
  16.8 9.9 %collective-permute-start.1 = (bf16[128,1024]{1,0:T(8,128)(2,1)}, bf16[128,1024]{1,0:T(8,128)(2,1)S(1)}, u32[]{:S(2)}, u32[]{:S(2)}) collective-permute-start(bf16[128,1024]{1,0:T(8,128)(2,1)} %get-tuple-element.12), channel_id=1, source_target_pairs={{0,8},{4,12},{8,0},{12,4},{16,24},{20,28},{24,16},{28,20},{1,9},{5... | collective-permute-start | bytes 786440 | tf_op jit(solution)/shard_map/ppermute | solution.py:290
  19.4 14.2 %collective-permute-start.3 = (bf16[128,1024]{1,0:T(8,128)(2,1)}, bf16[128,1024]{1,0:T(8,128)(2,1)}, u32[]{:S(2)}, u32[]{:S(2)}) collective-permute-start(bf16[128,1024]{1,0:T(8,128)(2,1)} %get-tuple-element.13), channel_id=1, source_target_pairs={{0,24},{4,28},{8,16},{12,20},{16,8},{20,12},{24,0},{28,4},{1,25},{... | collective-permute-start | bytes 786440 | tf_op jit(solution)/shard_map/ppermute | solution.py:290
  20.8 14.1 %collective-permute-start.2 = (bf16[128,1024]{1,0:T(8,128)(2,1)}, bf16[128,1024]{1,0:T(8,128)(2,1)}, u32[]{:S(2)}, u32[]{:S(2)}) collective-permute-start(bf16[128,1024]{1,0:T(8,128)(2,1)} %get-tuple-element.14), channel_id=1, source_target_pairs={{0,16},{4,20},{8,24},{12,28},{16,0},{20,4},{24,8},{28,12},{1,17},{... | collective-permute-start | bytes 786440 | tf_op jit(solution)/shard_map/ppermute | solution.py:290
  36.1 6.8 %collective-permute-start.5 = (bf16[32,1024]{1,0:T(8,128)(2,1)S(1)}, bf16[32,1024]{1,0:T(8,128)(2,1)S(1)}, u32[]{:S(2)}, u32[]{:S(2)}) collective-permute-start(bf16[32,1024]{1,0:T(8,128)(2,1)S(1)} %bitcast.9), channel_id=1, source_target_pairs={{0,2},{1,3},{2,0},{3,1},{4,6},{5,7},{6,4},{7,5},{8,10},{9,11},{10,... | collective-permute-start | bytes 196616 | tf_op jit(solution)/shard_map/ppermute | solution.py:290
  38.8 6.2 %collective-permute-start.6 = (bf16[32,1024]{1,0:T(8,128)(2,1)S(1)}, bf16[32,1024]{1,0:T(8,128)(2,1)S(1)}, u32[]{:S(2)}, u32[]{:S(2)}) collective-permute-start(bf16[32,1024]{1,0:T(8,128)(2,1)S(1)} %bitcast.8), channel_id=1, source_target_pairs={{0,3},{1,2},{2,1},{3,0},{4,7},{5,6},{6,5},{7,4},{8,11},{9,10},{10,... | collective-permute-start | bytes 196616 | tf_op jit(solution)/shard_map/ppermute | solution.py:290
  40.1 5.0 %copy-start.2 = (s32[8]{0:T(128)S(1)}, s32[8]{0:T(128)}, u32[]{:S(2)}) copy-start(s32[8]{0:T(128)} %order.5) | copy-start | bytes 100
  40.1 5.0 %copy-start.3 = (s32[4]{0:T(128)S(1)}, s32[4]{0:T(128)}, u32[]{:S(2)}) copy-start(s32[4]{0:T(128)} %roff.1) | copy-start | bytes 52
  40.1 5.0 %collective-permute-start.4 = (bf16[32,1024]{1,0:T(8,128)(2,1)S(1)}, bf16[32,1024]{1,0:T(8,128)(2,1)S(1)}, u32[]{:S(2)}, u32[]{:S(2)}) collective-permute-start(bf16[32,1024]{1,0:T(8,128)(2,1)S(1)} %bitcast.7), channel_id=1, source_target_pairs={{0,1},{1,0},{2,3},{3,2},{4,5},{5,4},{6,7},{7,6},{8,9},{9,8},{10,11... | collective-permute-start | bytes 196616 | tf_op jit(solution)/shard_map/ppermute | solution.py:290
  48.6 4.5 %collective-permute-start.7 = (bf16[272,128]{1,0:T(8,128)(2,1)S(1)}, bf16[272,128]{1,0:T(8,128)(2,1)S(1)}, u32[]{:S(2)}, u32[]{:S(2)}) collective-permute-start(bf16[272,128]{1,0:T(8,128)(2,1)S(1)} %get-tuple-element.7), channel_id=1, source_target_pairs={{0,1},{1,0},{2,3},{3,2},{4,5},{5,4},{6,7},{7,6},{8,9},{9,8},{10,11... | collective-permute-start | bytes 208904 | tf_op jit(solution)/shard_map/ppermute | solution.py:290
  48.7 7.9 %collective-permute-start.8 = (bf16[272,128]{1,0:T(8,128)(2,1)S(1)}, bf16[272,128]{1,0:T(8,128)(2,1)S(1)}, u32[]{:S(2)}, u32[]{:S(2)}) collective-permute-start(bf16[272,128]{1,0:T(8,128)(2,1)S(1)} %get-tuple-element.8), channel_id=1, source_target_pairs={{0,2},{1,3},{2,0},{3,1},{4,6},{5,7},{6,4},{7,5},{8,10},{9,11},{10,... | collective-permute-start | bytes 208904 | tf_op jit(solution)/shard_map/ppermute | solution.py:290
  51.4 6.2 %collective-permute-start.9 = (bf16[272,128]{1,0:T(8,128)(2,1)S(1)}, bf16[272,128]{1,0:T(8,128)(2,1)S(1)}, u32[]{:S(2)}, u32[]{:S(2)}) collective-permute-start(bf16[272,128]{1,0:T(8,128)(2,1)S(1)} %get-tuple-element.9), channel_id=1, source_target_pairs={{0,3},{1,2},{2,1},{3,0},{4,7},{5,6},{6,5},{7,4},{8,11},{9,10},{10,... | collective-permute-start | bytes 208904 | tf_op jit(solution)/shard_map/ppermute | solution.py:290

commit v2 on v1

v2 whole, which is shorter than its diff:
```python
import functools
import math

import jax
import jax.numpy as jnp
from jax import lax
from jax.experimental import pallas as pl
from jax.experimental.pallas import tpu as pltpu
from jax.sharding import PartitionSpec as P

FS = 4096
NG = 16384
FR = 64
BEAM_SLOPE = 0.66
LANES = 128
TILE = 8
MIB = 1 << 20
VMEM = pl.BlockSpec(memory_space=pltpu.VMEM)
SMEM = pl.BlockSpec(memory_space=pltpu.SMEM)
HBM = pl.BlockSpec(memory_space=pl.ANY)


def cis(phase):
    quarter = NG // 4
    turned = phase + quarter // 2
    quadrant = (turned & (NG - 1)) // quarter
    rest = (turned & (quarter - 1)) - quarter // 2
    t = rest.astype(jnp.float32) * (2.0 * math.pi / NG)
    t2 = t * t
    s = t * (1 + t2 * (-1 / 6 + t2 * (1 / 120 + t2 * (-1 / 5040 + t2 * (1 / 362880)))))
    c = 1 + t2 * (-1 / 2 + t2 * (1 / 24 + t2 * (-1 / 720 + t2 * (1 / 40320))))
    odd = (quadrant & 1) == 1
    real = jnp.where(odd, s, c)
    imag = jnp.where(odd, c, s)
    real = jnp.where((quadrant == 1) | (quadrant == 2), -real, real)
    imag = jnp.where(quadrant >= 2, -imag, imag)
    return real, imag


def times(a, b):
    return a[0] * b[0] - a[1] * b[1], a[0] * b[1] + a[1] * b[0]


def iota(shape, dim):
    return lax.broadcasted_iota(jnp.int32, shape, dim)


def stacked_rows(values, height):
    row = iota((height, 1), 0)
    result = jnp.zeros((height, 1), jnp.int32)
    for k, value in enumerate(values):
        result = jnp.where(row == k, value, result)
    return result


def store_stacked(ref, row, high, depth, real, imag):
    h = real.shape[0]
    real, imag, minus = (x.astype(jnp.bfloat16) for x in (real, imag, -imag))
    ref[row : row + h, :depth] = real
    ref[row : row + h, depth:] = minus
    ref[row + high : row + high + h, :depth] = imag
    ref[row + high : row + high + h, depth:] = real


def in_hbm(*arrays):
    return [pltpu.with_memory_space_constraint(x, pltpu.HBM) for x in arrays]


def small_copies(sources, targets, sems):
    return [pltpu.make_async_copy(s, t, sems.at[k]) for k, (s, t) in enumerate(zip(sources, targets))]


def build_table(table, small, first, slots, depth):
    few = (small[0], small[1])
    many = (small[2], small[3])
    for k in range(slots):
        k0, k1 = divmod(first + k, TILE)
        x = tuple(jnp.broadcast_to(small[4 + 2 * k0 + z, k1 : k1 + 1, :], (TILE, depth)) for z in range(2))
        xa = times(x, many)
        for a in range(0, FR // TILE, 2):
            parts = [
                times(tuple(jnp.broadcast_to(v[a + t : a + t + 1], (TILE, depth)) for v in xa), few)
                for t in range(2)
            ]
            real = jnp.concatenate([parts[0][0], parts[1][0]], axis=0)
            imag = jnp.concatenate([parts[0][1], parts[1][1]], axis=0)
            store_stacked(table, k * 2 * FR + a * TILE, FR, depth, real, imag)


def multiply(table, right, n, piece):
    value = right[:, :, n : n + piece]
    value = value.reshape(value.shape[0] * value.shape[1], piece)
    return jnp.dot(table[...], value, preferred_element_type=jnp.float32)


def given_kernel(slots, scale, *refs):
    sources, col, count, vis, out, kept, small = refs[:2], *refs[2:8]
    targets, table, small_sems, vis_sems = refs[8:10], *refs[10:]
    _, depth, width = vis.shape
    piece = width // vis_sems.shape[0]
    loads = small_copies(sources, targets, small_sems)
    blocks = [
        pltpu.make_async_copy(
            vis.at[:, :, pl.ds(n * piece, piece)], kept.at[:, :, pl.ds(n * piece, piece)], vis_sems.at[n]
        )
        for n in range(width // piece)
    ]
    for copy in loads + blocks:
        copy.start()
    for copy in loads:
        copy.wait()
    offs, order = targets
    c = lax.axis_index("col")
    u = col[0] + iota((TILE, depth), 1)
    sub = iota((TILE, depth), 0)
    small[0], small[1] = cis(u * sub)
    small[2], small[3] = cis(u * (sub * TILE))
    live = jnp.where(iota((TILE, depth), 1) < count[0, 0], scale, 0.0)
    starts = []
    for flip in (1, 0):
        for k in range(slots):
            slot = (((c // 2) ^ k) * 2) + ((c % 2) ^ flip)
            starts.append((offs[0, order[slot]] + (FS // 2 - FR // 2)) % NG)
    for k in range(0, 2 * slots, TILE):
        xs = cis(u * stacked_rows(starts[k : k + TILE], TILE))
        at = 4 + 2 * (k // TILE)
        small[at], small[at + 1] = xs[0] * live, xs[1] * live
    build_table(table, small, 0, slots, depth)
    for n in range(width // piece):
        blocks[n].wait()
        out[:, n * piece : (n + 1) * piece] = multiply(table, kept, n * piece, piece).astype(out.dtype)


def given_columns(slots, scale, offs, order, col, count, vis):
    _, depth, width = vis.shape
    rows = slots * 2 * FR
    smalls = 4 + 2 * -(-2 * slots // TILE)
    return pl.pallas_call(
        functools.partial(given_kernel, slots, scale),
        in_specs=[HBM] * 2 + [SMEM] * 2 + [HBM],
        out_specs=[VMEM] * 3,
        out_shape=[
            jax.ShapeDtypeStruct((rows, width), jnp.bfloat16),
            jax.ShapeDtypeStruct(vis.shape, vis.dtype),
            jax.ShapeDtypeStruct((smalls, TILE, depth), jnp.float32),
        ],
        scratch_shapes=[pltpu.SMEM(x.shape, x.dtype) for x in (offs, order)]
        + [
            pltpu.VMEM((rows, 2 * depth), jnp.bfloat16),
            pltpu.SemaphoreType.DMA((2,)),
            pltpu.SemaphoreType.DMA((4,)),
        ],
        compiler_params=pltpu.CompilerParams(vmem_limit_bytes=16 * MIB),
        cost_estimate=pl.CostEstimate(
            flops=rows * 4 * depth * width, bytes_accessed=4 * depth * width, transcendentals=0
        ),
        name="given",
    )(*in_hbm(offs, order), col, count, *in_hbm(vis))


def mine_kernel(slots, kept, small, out, table):
    _, depth, width = kept.shape
    build_table(table, small, slots, slots, depth)
    piece = 2 * LANES
    for n in range(0, width, piece):
        out[:, n : n + piece] = multiply(table, kept, n, piece)


def mine_columns(slots, kept, small):
    _, depth, width = kept.shape
    rows = slots * 2 * FR
    return pl.pallas_call(
        functools.partial(mine_kernel, slots),
        in_specs=[VMEM] * 2,
        out_specs=VMEM,
        out_shape=jax.ShapeDtypeStruct((rows, width), jnp.float32),
        scratch_shapes=[pltpu.VMEM((rows, 2 * depth), jnp.bfloat16)],
        compiler_params=pltpu.CompilerParams(vmem_limit_bytes=16 * MIB),
        cost_estimate=pl.CostEstimate(
            flops=rows * 4 * depth * width, bytes_accessed=4 * depth * width, transcendentals=0
        ),
        name="mine",
    )(kept, small)


def pair_kernel(mine, taken, total, *sent):
    high = total.shape[0]
    total[...] = mine[:high] + taken[:high].astype(jnp.float32)
    for k, out in enumerate(sent):
        at = slice((k + 1) * high, (k + 2) * high)
        out[...] = (mine[at] + taken[at].astype(jnp.float32)).astype(out.dtype)


def pair_sum(slots, mine, taken):
    rows, width = mine.shape
    high = rows // slots
    return pl.pallas_call(
        pair_kernel,
        in_specs=[VMEM] * 2,
        out_specs=[VMEM] * slots,
        out_shape=[jax.ShapeDtypeStruct((high, width), jnp.float32)]
        + [jax.ShapeDtypeStruct((high, width), jnp.bfloat16)] * (slots - 1),
        compiler_params=pltpu.CompilerParams(vmem_limit_bytes=8 * MIB),
        name="pair",
    )(mine, taken)


def sum_kernel(arrived, total, *refs):
    taken, outs = refs[:arrived], refs[arrived + 1 :]
    double, depth = outs[0].shape
    high = double // 2
    rows = len(outs)
    r = lax.axis_index("row")

    def rows_at(at):
        value = total[at, :]
        for other in taken:
            value = value + other[at, :].astype(jnp.float32)
        return value

    for p in range(rows):
        for z in range(2):
            if high % (2 * TILE) == 0:
                at = pl.ds(pl.multiple_of(z * FR + (r ^ p) * high, high), high)
                outs[p][z * high : (z + 1) * high, :] = rows_at(at).astype(outs[p].dtype)
    if high % (2 * TILE) != 0:
        value = rows_at(slice(0, 2 * FR))
        for p in range(rows):
            parts = []
            for z in range(2):
                part = value[z * FR : z * FR + high]
                for q in range(1, rows):
                    part = jnp.where((r ^ p) == q, value[z * FR + q * high : z * FR + (q + 1) * high], part)
                parts.append(part)
            outs[p][...] = jnp.concatenate(parts, axis=0).astype(outs[p].dtype)


def sum_of(rows, total, taken, wave):
    depth = total.shape[1]
    return pl.pallas_call(
        functools.partial(sum_kernel, len(taken)),
        in_specs=[VMEM] * (len(taken) + 1) + [HBM],
        out_specs=[VMEM] * rows,
        out_shape=[jax.ShapeDtypeStruct((2 * FR // rows, depth), jnp.bfloat16)] * rows,
        compiler_params=pltpu.CompilerParams(vmem_limit_bytes=16 * MIB),
        name="sum",
    )(total, *taken, wave)


def wave_kernel(rows, scale, after, *refs):
    del after
    sources, (out, turned, later) = refs[:3], refs[3:6]
    targets, sems = refs[6:9], refs[9]
    loads = small_copies(sources, targets, sems)
    for copy in loads:
        copy.start()
    depth, width = out.shape[0] // 2, out.shape[1]
    lane = iota((TILE, width), 1)
    sub = iota((TILE, width), 0)
    few = cis(lane * sub)

    def body(block, carry):
        coarse = cis(lane * ((block * TILE + sub) * TILE))
        base = block * (TILE * TILE)
        for a in range(0, TILE, 2):
            parts = [
                times(tuple(jnp.broadcast_to(v[a + s : a + s + 1], (TILE, width)) for v in coarse), few)
                for s in range(2)
            ]
            row = pl.multiple_of(base + a * TILE, 2 * TILE)
            for z in range(2):
                value = jnp.concatenate([parts[0][z], parts[1][z]], axis=0)
                out[pl.ds(row + z * depth, 2 * TILE), :] = value.astype(out.dtype)
        return carry

    lax.fori_loop(0, depth // (TILE * TILE), body, 0)
    for copy in loads:
        copy.wait()
    offs, order, roff = targets
    r = lax.axis_index("row")
    start = offs[1, order[lax.axis_index("col")]]
    height = later.shape[1]
    blocks = stacked_rows([(start + (r ^ b) * width) % NG for b in range(rows)], height)
    origins = [roff[r ^ p] for p in range(rows)]
    for p in range(rows):
        phase = cis((origins[p] + iota((height, depth), 1)) * blocks)
        turned[2 * p], turned[2 * p + 1] = phase[0] * scale, phase[1] * scale
    later[0], later[1] = cis(iota((height, width), 1) * stacked_rows(origins, height))
    j = ((r * width) + iota((height, width), 1)).astype(jnp.float32)
    for b in range(rows):
        j = ((r ^ b) * width + iota((1, width), 1)).astype(jnp.float32)
        later[2, b : b + 1, :] = 1.0 / (1.0 - BEAM_SLOPE * (j + 0.5) / FS)


def waves(rows, scale, offs, order, roff, after, depth, width):
    height = -(-rows // TILE) * TILE
    return pl.pallas_call(
        functools.partial(wave_kernel, rows, scale),
        in_specs=[HBM] * 4,
        out_specs=[VMEM] * 3,
        out_shape=[
            jax.ShapeDtypeStruct((2 * depth, width), jnp.bfloat16),
            jax.ShapeDtypeStruct((2 * rows, height, depth), jnp.float32),
            jax.ShapeDtypeStruct((3, height, width), jnp.float32),
        ],
        scratch_shapes=[pltpu.SMEM(x.shape, x.dtype) for x in (offs, order, roff)]
        + [pltpu.SemaphoreType.DMA((3,))],
        compiler_params=pltpu.CompilerParams(vmem_limit_bytes=16 * MIB),
        cost_estimate=pl.CostEstimate(flops=4 * 10**9, bytes_accessed=4 * depth * width, transcendentals=0),
        name="waves",
    )(after, *in_hbm(offs, order, roff))


def row_kernel(rows, wave, turned, later, *refs):
    pieces, outs, left = refs[:rows], refs[rows : 2 * rows], refs[2 * rows]
    double, depth = pieces[0].shape
    high = double // 2
    width = wave.shape[1]
    for p in range(rows):
        value = pieces[p][...].astype(jnp.float32)
        value = (value[:high], value[high:])
        for b in range(rows):
            turn = tuple(jnp.broadcast_to(turned[2 * p + z, b : b + 1, :], (high, depth)) for z in range(2))
            real, imag = times(value, turn)
            store_stacked(left, (p * rows + b) * double, high, depth, real, imag)
    piece = min(2 * LANES, width)
    largest = jnp.zeros((high, LANES), jnp.float32)
    for n in range(0, width, piece):
        product = jnp.dot(left[...], wave[:, n : n + piece], preferred_element_type=jnp.float32)
        for b in range(rows):
            real = imag = None
            for p in range(rows):
                at = (p * rows + b) * double
                value = (product[at : at + high], product[at + high : at + double])
                turn = tuple(later[z, p : p + 1, n : n + piece] for z in range(2))
                x, y = times(value, turn)
                real = x if real is None else real + x
                imag = y if imag is None else imag + y
            beam = later[2, b : b + 1, n : n + piece]
            real = real * beam
            imag = imag * beam
            power = real * real + imag * imag
            for m in range(0, piece, LANES):
                at = (n + m) // LANES * double
                outs[b][at : at + high] = real[:, m : m + LANES].astype(jnp.bfloat16)
                outs[b][at + high : at + double] = imag[:, m : m + LANES].astype(jnp.bfloat16)
                largest = jnp.maximum(largest, power[:, m : m + LANES])
    peak = jnp.broadcast_to(jnp.sqrt(jnp.max(largest, keepdims=True)), (2 * TILE, LANES))
    first = peak.astype(jnp.bfloat16).astype(jnp.float32)
    second = (peak - first).astype(jnp.bfloat16).astype(jnp.float32)
    third = peak - first - second
    sub = iota((2 * TILE, LANES), 0)
    peak = jnp.where(sub == 0, first, jnp.where(sub == 1, second, jnp.where(sub == 2, third, 0.0)))
    for b in range(rows):
        outs[b][width // LANES * double :] = peak.astype(jnp.bfloat16)


def rows_of(pieces, wave, turned, later):
    rows = len(pieces)
    double, depth = pieces[0].shape
    width = wave.shape[1]
    shape = jax.ShapeDtypeStruct((width // LANES * double + 2 * TILE, LANES), jnp.bfloat16)
    return pl.pallas_call(
        functools.partial(row_kernel, rows),
        in_specs=[VMEM] * (rows + 3),
        out_specs=[VMEM] * rows,
        out_shape=[shape] * rows,
        scratch_shapes=[pltpu.VMEM((rows * rows * double, 2 * depth), jnp.bfloat16)],
        compiler_params=pltpu.CompilerParams(vmem_limit_bytes=24 * MIB),
        cost_estimate=pl.CostEstimate(
            flops=rows * rows * double * 4 * depth * width, bytes_accessed=4 * depth * width, transcendentals=0
        ),
        name="rows",
    )(wave, turned, later, *pieces)


def finish_kernel(rows, *refs):
    pieces, (image, peak) = refs[:rows], refs[rows:]
    width = image.shape[3]
    high = image.shape[2] // rows
    r = lax.axis_index("row")
    largest = None
    for p in range(rows):
        for n in range(0, width, LANES):
            row = n // LANES * 2 * high
            if high % TILE == 0:
                at = pl.ds(pl.multiple_of((r ^ p) * high, high), high)
                value = pieces[p][row : row + 2 * high, :].astype(jnp.float32)
            else:
                at = pl.ds(p * high, high)
                value = pieces[0][row : row + 2 * high, :].astype(jnp.float32)
                for q in range(1, rows):
                    other = pieces[q][row : row + 2 * high, :].astype(jnp.float32)
                    value = jnp.where((r ^ p) == q, other, value)
            image[0, 0, at, n : n + LANES] = value[:high]
            image[0, 1, at, n : n + LANES] = value[high:]
        parts = pieces[p][width // LANES * 2 * high :, :].astype(jnp.float32)
        value = (parts[0:1] + parts[1:2]) + parts[2:3]
        largest = value if largest is None else jnp.maximum(largest, value)
    peak[0] = jnp.max(largest)


def finish(pieces, width):
    rows = len(pieces)
    return pl.pallas_call(
        functools.partial(finish_kernel, rows),
        in_specs=[VMEM] * rows,
        out_specs=[VMEM, SMEM],
        out_shape=[
            jax.ShapeDtypeStruct((1, 2, FR, width), jnp.float32),
            jax.ShapeDtypeStruct((1,), jnp.float32),
        ],
        compiler_params=pltpu.CompilerParams(vmem_limit_bytes=16 * MIB),
        name="finish",
    )(*pieces)


def local(visibilities, col_offsets, row_offsets, facet_offsets, facet_order, vis_counts):
    cols = lax.axis_size("col")
    rows = lax.axis_size("row")
    _, depth, width = visibilities.shape
    slots = cols // 2
    offsets = facet_offsets.T
    first_scale = 1.0 / math.sqrt(depth * cols)
    second_scale = 0.5 / math.sqrt(width * rows)

    def swap(value, axis, count, bit):
        return lax.ppermute(value, axis, [(i, i ^ bit) for i in range(count)])

    given, kept, small = given_columns(
        slots, first_scale, offsets, facet_order, col_offsets, vis_counts, visibilities
    )
    taken = swap(given, "col", cols, 1)
    mine = mine_columns(slots, kept, small)
    total, *sent = pair_sum(slots, mine, taken)
    sent = [swap(value, "col", cols, 2 * k + 2) for k, value in enumerate(sent)]
    wave, turned, later = waves(
        rows, second_scale, offsets, facet_order, row_offsets, total, width, FS // rows
    )
    pieces = sum_of(rows, total, sent, wave)
    pieces = [piece if p == 0 else swap(piece, "row", rows, p) for p, piece in enumerate(pieces)]
    parts = rows_of(pieces, wave, turned, later)
    parts = [part if p == 0 else swap(part, "row", rows, p) for p, part in enumerate(parts)]
    image, peak = finish(parts, FS // rows)
    return image, peak


def solution(mesh):
    in_specs = (P(None, "col", "row"), P("col"), P(), P(), P(), P("col", "row"))
    out_specs = (P("col", None, None, "row"), P("col"))
    return jax.shard_map(local, mesh=mesh, in_specs=in_specs, out_specs=out_specs, check_vma=False)
```

time: 58.7 us -> 49.8 us (0.85)
  local copies, waits for them, and re-layouts: 4.51 us -> 0 us
  waiting for transfers between devices: 20.8 us -> 18.5 us
  other arithmetic: 1.65 us -> 0 us
  Pallas kernels: 16.3 us -> 15.3 us
    unnamed x9 -> x0, local copies, waits for them, and re-layouts: 3.6 us -> none
    ppermute x10, waiting for transfers between devices: 20.8 us -> 18.5 us  [swap(): return lax.ppermute(value, axis, [(i, i ^ bit) for i in range(count)])]
    convert_element_type x1 -> x0, other arithmetic: 1.18 us -> none  [local(): total = total.astype(jnp.bfloat16).reshape(2, FR, width)]
    pallas_call x4 -> x6, Pallas kernels: 15.4 us -> 14.5 us  [the longest x1 6.32 us: given_columns(): pl.pallas_call(functools.partial(given_kernel, slots, scale), in_specs=[H...]
    slice x1 -> x0, local copies, waits for them, and re-layouts: 0.88 us -> none  [local(): pair[k].astype(jnp.bfloat16)]
  transfers between devices with their start and end apart: 10 -> 10, of which waited for: 7 -> 8; matrix products, arithmetic and copies ran while one was open for 0% -> 0% of each run, Pallas kernels for 12% -> 11%
where the time goes in v2:
time: 49.8 us; the launch traced here: 49.6 us
  waiting for transfers between devices  18.5 us (37%)
  Pallas kernels  15.3 us (31%)
  starting transfers between devices  13.8 us (28%)
  between operations  1.98 us (4%)
    ppermute x10, waiting for transfers between devices, swap(): return lax.ppermute(value, axis, [(i, i ^ bit) for i in range(count)])  18.5 us
    ppermute x10, starting transfers between devices, swap(): return lax.ppermute(value, axis, [(i, i ^ bit) for i in range(count)])  13.8 us
    pallas_call x1, Pallas kernels, given_columns(): pl.pallas_call(functools.partial(given_kernel, slots, scale), in_specs=[H...  6.32 us
    pallas_call x1, Pallas kernels, waves(): pl.pallas_call(functools.partial(wave_kernel, rows, scale), in_specs=[HBM...  2.97 us
    pallas_call x1, Pallas kernels, rows_of(): pl.pallas_call(functools.partial(row_kernel, rows), in_specs=[VMEM] * (ro...  2.56 us
    pallas_call x1, Pallas kernels, mine_columns(): pl.pallas_call(functools.partial(mine_kernel, slots), in_specs=[VMEM] * 2...  2.34 us
  transfers between devices with their start and end apart: 10, of which 8 were waited for; matrix products, arithmetic and copies ran while one was open for 0% of the time, Pallas kernels for 11%

profile of v2, /device:TPU:0, one launch (start us, length us, event | category | flops | bytes accessed | tf_op | source)
XLA Modules:
  0.0 49.6 jit_solution(11024997312869931073)
XLA Ops:
  1.9 6.3 %given.1 = (bf16[512,1024]{1,0:T(8,128)(2,1)S(1)}, bf16[2,1024,1024]{2,1,0:T(8,128)(2,1)S(1)}, f32[6,8,1024]{2,1,0:T(8,128)S(1)}) custom-call(s32[2,8]{1,0:T(2,128)} %bitcast.1, s32[8]{0:T(128)} %refs_1_.3, s32[1]{0:T(128)S(6)} %copy.8.refs_2_, s32[1,1]{1,0:T(1,128)S(6)} %copy.9.refs_3_, bf16[2,1024,1024]{2,1,0:T(8,128)(2,1)} %refs_4_.1), custom_call_target="tpu_custom_call" | custom-call | flops 2147483648 | bytes 4194304 | tf_op jit(solution)/shard_map/given/pallas_call | solution.py:138
  8.2 0.6 %collective-permute-start = (bf16[512,1024]{1,0:T(8,128)(2,1)S(1)}, bf16[512,1024]{1,0:T(8,128)(2,1)S(1)}, u32[]{:S(2)}, u32[]{:S(2)}) collective-permute-start(bf16[512,1024]{1,0:T(8,128)(2,1)S(1)} %get-tuple-element.22), channel_id=1, source_target_pairs={{0,4},{4,0},{8,12},{12,8},{16,20},{20,16},{24,28},{28,24},{1,5},{5... | collective-permute-start | bytes 3145736 | tf_op jit(solution)/shard_map/ppermute | solution.py:428
  8.8 2.3 %mine.1 = f32[512,1024]{1,0:T(8,128)S(1)} custom-call(bf16[2,1024,1024]{2,1,0:T(8,128)(2,1)S(1)} %get-tuple-element.20.kept, f32[6,8,1024]{2,1,0:T(8,128)S(1)} %get-tuple-element.21.small), custom_call_target="tpu_custom_call" | custom-call | flops 2147483648 | bytes 4194304 | tf_op jit(solution)/shard_map/mine/pallas_call | solution.py:172
  11.2 0.0 collective-permute-done.taken
  11.2 0.2 pair.1
  11.3 2.8 %collective-permute-start.1 = (bf16[128,1024]{1,0:T(8,128)(2,1)S(1)}, bf16[128,1024]{1,0:T(8,128)(2,1)S(1)}, u32[]{:S(2)}, u32[]{:S(2)}) collective-permute-start(bf16[128,1024]{1,0:T(8,128)(2,1)S(1)} %get-tuple-element.27), channel_id=1, source_target_pairs={{0,8},{4,12},{8,0},{12,4},{16,24},{20,28},{24,16},{28,20},{1,9},{5... | collective-permute-start | bytes 786440 | tf_op jit(solution)/shard_map/ppermute | solution.py:428
  14.2 1.5 %collective-permute-start.2 = (bf16[128,1024]{1,0:T(8,128)(2,1)S(1)}, bf16[128,1024]{1,0:T(8,128)(2,1)S(1)}, u32[]{:S(2)}, u32[]{:S(2)}) collective-permute-start(bf16[128,1024]{1,0:T(8,128)(2,1)S(1)} %get-tuple-element.28), channel_id=1, source_target_pairs={{0,16},{4,20},{8,24},{12,28},{16,0},{20,4},{24,8},{28,12},{1,17},{... | collective-permute-start | bytes 786440 | tf_op jit(solution)/shard_map/ppermute | solution.py:428
  15.7 0.0 collective-permute-start.3
  15.7 3.0 %waves.1 = (bf16[2048,1024]{1,0:T(8,128)(2,1)S(1)}, f32[8,8,1024]{2,1,0:T(8,128)S(1)}, f32[3,8,1024]{2,1,0:T(8,128)S(1)}) custom-call(f32[128,1024]{1,0:T(8,128)S(1)} %get-tuple-element.23.after.total, s32[2,8]{1,0:T(2,128)} %bitcast.2, s32[8]{0:T(128)} %refs_1_.3, s32[4]{0:T(128)} %refs_2_.2), custom_call_target="tpu_custom_call" | custom-call | flops 4000000000 | bytes 4194304 | tf_op jit(solution)/shard_map/waves/pallas_call | solution.py:297
  18.7 2.6 %collective-permute-done.1.refs_0_ = bf16[128,1024]{1,0:T(8,128)(2,1)S(1)} collective-permute-done((bf16[128,1024]{1,0:T(8,128)(2,1)S(1)}, bf16[128,1024]{1,0:T(8,128)(2,1)S(1)}, u32[]{:S(2)}, u32[]{:S(2)}) %collective-permute-start.1) | collective-permute-done | bytes 262176 | tf_op jit(solution)/shard_map/ppermute | solution.py:428
  21.3 6.6 %collective-permute-done.2.refs_1_ = bf16[128,1024]{1,0:T(8,128)(2,1)S(1)} collective-permute-done((bf16[128,1024]{1,0:T(8,128)(2,1)S(1)}, bf16[128,1024]{1,0:T(8,128)(2,1)S(1)}, u32[]{:S(2)}, u32[]{:S(2)}) %collective-permute-start.2) | collective-permute-done | bytes 262176 | tf_op jit(solution)/shard_map/ppermute | solution.py:428
  27.9 0.0 collective-permute-done.3.refs_2_
  28.0 0.1 sum.1
  28.1 1.6 %collective-permute-start.4 = (bf16[32,1024]{1,0:T(8,128)(2,1)S(1)}, bf16[32,1024]{1,0:T(8,128)(2,1)S(1)}, u32[]{:S(2)}, u32[]{:S(2)}) collective-permute-start(bf16[32,1024]{1,0:T(8,128)(2,1)S(1)} %get-tuple-element.31), channel_id=1, source_target_pairs={{0,1},{1,0},{2,3},{3,2},{4,5},{5,4},{6,7},{7,6},{8,9},{9,8},{10,11... | collective-permute-start | bytes 196616 | tf_op jit(solution)/shard_map/ppermute | solution.py:428
  29.7 2.6 %collective-permute-start.5 = (bf16[32,1024]{1,0:T(8,128)(2,1)S(1)}, bf16[32,1024]{1,0:T(8,128)(2,1)S(1)}, u32[]{:S(2)}, u32[]{:S(2)}) collective-permute-start(bf16[32,1024]{1,0:T(8,128)(2,1)S(1)} %get-tuple-element.32), channel_id=1, source_target_pairs={{0,2},{1,3},{2,0},{3,1},{4,6},{5,7},{6,4},{7,5},{8,10},{9,11},{10,... | collective-permute-start | bytes 196616 | tf_op jit(solution)/shard_map/ppermute | solution.py:428
  32.3 0.2 collective-permute-start.6
  32.5 0.5 %collective-permute-done.4.refs_1_ = bf16[32,1024]{1,0:T(8,128)(2,1)S(1)} collective-permute-done((bf16[32,1024]{1,0:T(8,128)(2,1)S(1)}, bf16[32,1024]{1,0:T(8,128)(2,1)S(1)}, u32[]{:S(2)}, u32[]{:S(2)}) %collective-permute-start.4) | collective-permute-done | bytes 65568 | tf_op jit(solution)/shard_map/ppermute | solution.py:428
  33.0 3.2 %collective-permute-done.5.refs_2_ = bf16[32,1024]{1,0:T(8,128)(2,1)S(1)} collective-permute-done((bf16[32,1024]{1,0:T(8,128)(2,1)S(1)}, bf16[32,1024]{1,0:T(8,128)(2,1)S(1)}, u32[]{:S(2)}, u32[]{:S(2)}) %collective-permute-start.5) | collective-permute-done | bytes 65568 | tf_op jit(solution)/shard_map/ppermute | solution.py:428
  36.3 2.1 %collective-permute-done.6.refs_3_ = bf16[32,1024]{1,0:T(8,128)(2,1)S(1)} collective-permute-done((bf16[32,1024]{1,0:T(8,128)(2,1)S(1)}, bf16[32,1024]{1,0:T(8,128)(2,1)S(1)}, u32[]{:S(2)}, u32[]{:S(2)}) %collective-permute-start.6) | collective-permute-done | bytes 65568 | tf_op jit(solution)/shard_map/ppermute | solution.py:428
  38.4 2.6 %rows.1 = (bf16[272,128]{1,0:T(8,128)(2,1)S(1)}, bf16[272,128]{1,0:T(8,128)(2,1)S(1)}, bf16[272,128]{1,0:T(8,128)(2,1)S(1)}, bf16[272,128]{1,0:T(8,128)(2,1)S(1)}) custom-call(bf16[2048,1024]{1,0:T(8,128)(2,1)S(1)} %get-tuple-element.24.refs_3_.wave, f32[8,8,1024]{2,1,0:T(8,128)S(1)} %get-tuple-element.25.turned, f32[3,8,1024]{2,1,0:T(8,128)S(1)} %get-tuple-element.26.later, ...), custom_call_target="tpu_custom_call" | custom-call | flops 2147483648 | bytes 4194304 | tf_op jit(solution)/shard_map/rows/pallas_call | solution.py:363
  40.9 0.1 collective-permute-start.7
  41.0 1.6 %collective-permute-start.8 = (bf16[272,128]{1,0:T(8,128)(2,1)S(1)}, bf16[272,128]{1,0:T(8,128)(2,1)S(1)}, u32[]{:S(2)}, u32[]{:S(2)}) collective-permute-start(bf16[272,128]{1,0:T(8,128)(2,1)S(1)} %get-tuple-element.36), channel_id=1, source_target_pairs={{0,2},{1,3},{2,0},{3,1},{4,6},{5,7},{6,4},{7,5},{8,10},{9,11},{10,... | collective-permute-start | bytes 208904 | tf_op jit(solution)/shard_map/ppermute | solution.py:428
  42.7 2.7 %collective-permute-start.9 = (bf16[272,128]{1,0:T(8,128)(2,1)S(1)}, bf16[272,128]{1,0:T(8,128)(2,1)S(1)}, u32[]{:S(2)}, u32[]{:S(2)}) collective-permute-start(bf16[272,128]{1,0:T(8,128)(2,1)S(1)} %get-tuple-element.37), channel_id=1, source_target_pairs={{0,3},{1,2},{2,1},{3,0},{4,7},{5,6},{6,5},{7,4},{8,11},{9,10},{10,... | collective-permute-start | bytes 208904 | tf_op jit(solution)/shard_map/ppermute | solution.py:428
  45.4 0.2 collective-permute-done.7.refs_1_
  45.6 0.7 %collective-permute-done.8.refs_2_ = bf16[272,128]{1,0:T(8,128)(2,1)S(1)} collective-permute-done((bf16[272,128]{1,0:T(8,128)(2,1)S(1)}, bf16[272,128]{1,0:T(8,128)(2,1)S(1)}, u32[]{:S(2)}, u32[]{:S(2)}) %collective-permute-start.8) | collective-permute-done | bytes 69664 | tf_op jit(solution)/shard_map/ppermute | solution.py:428
  46.4 2.4 %collective-permute-done.9.refs_3_ = bf16[272,128]{1,0:T(8,128)(2,1)S(1)} collective-permute-done((bf16[272,128]{1,0:T(8,128)(2,1)S(1)}, bf16[272,128]{1,0:T(8,128)(2,1)S(1)}, u32[]{:S(2)}, u32[]{:S(2)}) %collective-permute-start.9) | collective-permute-done | bytes 69664 | tf_op jit(solution)/shard_map/ppermute | solution.py:428
  48.8 0.8 %finish.1 = (f32[1,2,64,1024]{3,2,1,0:T(8,128)}, f32[1]{0:T(128)}) custom-call(bf16[272,128]{1,0:T(8,128)(2,1)S(1)} %get-tuple-element.34.refs_0_, bf16[272,128]{1,0:T(8,128)(2,1)S(1)} %collective-permute-done.7.refs_1_, bf16[272,128]{1,0:T(8,128)(2,1)S(1)} %collective-permute-done.8.refs_2_, bf16[272,128]{1,0:T(8,128)(2,1)S(1)} %collective-permute-done.9.refs_3_), custom_call_target="tpu_custom_call" | custom-call | tf_op jit(solution)/shard_map/finish/pallas_call | solution.py:405
Async XLA Ops:
  8.2 2.9 %collective-permute-start = (bf16[512,1024]{1,0:T(8,128)(2,1)S(1)}, bf16[512,1024]{1,0:T(8,128)(2,1)S(1)}, u32[]{:S(2)}, u32[]{:S(2)}) collective-permute-start(bf16[512,1024]{1,0:T(8,128)(2,1)S(1)} %get-tuple-element.22), channel_id=1, source_target_pairs={{0,4},{4,0},{8,12},{12,8},{16,20},{20,16},{24,28},{28,24},{1,5},{5... | collective-permute-start | bytes 3145736 | tf_op jit(solution)/shard_map/ppermute | solution.py:428
  11.3 10.0 %collective-permute-start.1 = (bf16[128,1024]{1,0:T(8,128)(2,1)S(1)}, bf16[128,1024]{1,0:T(8,128)(2,1)S(1)}, u32[]{:S(2)}, u32[]{:S(2)}) collective-permute-start(bf16[128,1024]{1,0:T(8,128)(2,1)S(1)} %get-tuple-element.27), channel_id=1, source_target_pairs={{0,8},{4,12},{8,0},{12,4},{16,24},{20,28},{24,16},{28,20},{1,9},{5... | collective-permute-start | bytes 786440 | tf_op jit(solution)/shard_map/ppermute | solution.py:428
  14.2 13.8 %collective-permute-start.2 = (bf16[128,1024]{1,0:T(8,128)(2,1)S(1)}, bf16[128,1024]{1,0:T(8,128)(2,1)S(1)}, u32[]{:S(2)}, u32[]{:S(2)}) collective-permute-start(bf16[128,1024]{1,0:T(8,128)(2,1)S(1)} %get-tuple-element.28), channel_id=1, source_target_pairs={{0,16},{4,20},{8,24},{12,28},{16,0},{20,4},{24,8},{28,12},{1,17},{... | collective-permute-start | bytes 786440 | tf_op jit(solution)/shard_map/ppermute | solution.py:428
  15.7 12.2 %collective-permute-start.3 = (bf16[128,1024]{1,0:T(8,128)(2,1)S(1)}, bf16[128,1024]{1,0:T(8,128)(2,1)S(1)}, u32[]{:S(2)}, u32[]{:S(2)}) collective-permute-start(bf16[128,1024]{1,0:T(8,128)(2,1)S(1)} %get-tuple-element.29), channel_id=1, source_target_pairs={{0,24},{4,28},{8,16},{12,20},{16,8},{20,12},{24,0},{28,4},{1,25},{... | collective-permute-start | bytes 786440 | tf_op jit(solution)/shard_map/ppermute | solution.py:428
  28.1 5.0 %collective-permute-start.4 = (bf16[32,1024]{1,0:T(8,128)(2,1)S(1)}, bf16[32,1024]{1,0:T(8,128)(2,1)S(1)}, u32[]{:S(2)}, u32[]{:S(2)}) collective-permute-start(bf16[32,1024]{1,0:T(8,128)(2,1)S(1)} %get-tuple-element.31), channel_id=1, source_target_pairs={{0,1},{1,0},{2,3},{3,2},{4,5},{5,4},{6,7},{7,6},{8,9},{9,8},{10,11... | collective-permute-start | bytes 196616 | tf_op jit(solution)/shard_map/ppermute | solution.py:428
  29.7 6.6 %collective-permute-start.5 = (bf16[32,1024]{1,0:T(8,128)(2,1)S(1)}, bf16[32,1024]{1,0:T(8,128)(2,1)S(1)}, u32[]{:S(2)}, u32[]{:S(2)}) collective-permute-start(bf16[32,1024]{1,0:T(8,128)(2,1)S(1)} %get-tuple-element.32), channel_id=1, source_target_pairs={{0,2},{1,3},{2,0},{3,1},{4,6},{5,7},{6,4},{7,5},{8,10},{9,11},{10,... | collective-permute-start | bytes 196616 | tf_op jit(solution)/shard_map/ppermute | solution.py:428
  32.3 6.1 %collective-permute-start.6 = (bf16[32,1024]{1,0:T(8,128)(2,1)S(1)}, bf16[32,1024]{1,0:T(8,128)(2,1)S(1)}, u32[]{:S(2)}, u32[]{:S(2)}) collective-permute-start(bf16[32,1024]{1,0:T(8,128)(2,1)S(1)} %get-tuple-element.33), channel_id=1, source_target_pairs={{0,3},{1,2},{2,1},{3,0},{4,7},{5,6},{6,5},{7,4},{8,11},{9,10},{10,... | collective-permute-start | bytes 196616 | tf_op jit(solution)/shard_map/ppermute | solution.py:428
  40.9 4.7 %collective-permute-start.7 = (bf16[272,128]{1,0:T(8,128)(2,1)S(1)}, bf16[272,128]{1,0:T(8,128)(2,1)S(1)}, u32[]{:S(2)}, u32[]{:S(2)}) collective-permute-start(bf16[272,128]{1,0:T(8,128)(2,1)S(1)} %get-tuple-element.35), channel_id=1, source_target_pairs={{0,1},{1,0},{2,3},{3,2},{4,5},{5,4},{6,7},{7,6},{8,9},{9,8},{10,11... | collective-permute-start | bytes 208904 | tf_op jit(solution)/shard_map/ppermute | solution.py:428
  41.0 5.4 %collective-permute-start.8 = (bf16[272,128]{1,0:T(8,128)(2,1)S(1)}, bf16[272,128]{1,0:T(8,128)(2,1)S(1)}, u32[]{:S(2)}, u32[]{:S(2)}) collective-permute-start(bf16[272,128]{1,0:T(8,128)(2,1)S(1)} %get-tuple-element.36), channel_id=1, source_target_pairs={{0,2},{1,3},{2,0},{3,1},{4,6},{5,7},{6,4},{7,5},{8,10},{9,11},{10,... | collective-permute-start | bytes 208904 | tf_op jit(solution)/shard_map/ppermute | solution.py:428
  42.7 6.1 %collective-permute-start.9 = (bf16[272,128]{1,0:T(8,128)(2,1)S(1)}, bf16[272,128]{1,0:T(8,128)(2,1)S(1)}, u32[]{:S(2)}, u32[]{:S(2)}) collective-permute-start(bf16[272,128]{1,0:T(8,128)(2,1)S(1)} %get-tuple-element.37), channel_id=1, source_target_pairs={{0,3},{1,2},{2,1},{3,0},{4,7},{5,6},{6,5},{7,4},{8,11},{9,10},{10,... | collective-permute-start | bytes 208904 | tf_op jit(solution)/shard_map/ppermute | solution.py:428

commit v3 on v2

v3 whole, which is shorter than its diff:
```python
import functools
import math

import jax
import jax.numpy as jnp
from jax import lax
from jax.experimental import pallas as pl
from jax.experimental.pallas import tpu as pltpu
from jax.sharding import PartitionSpec as P


FS = 4096
NG = 16384
FR = 64
BEAM_SLOPE = 0.66
LANES = 128
TILE = 8
MIB = 1 << 20
VMEM = pl.BlockSpec(memory_space=pltpu.VMEM)
SMEM = pl.BlockSpec(memory_space=pltpu.SMEM)
HBM = pl.BlockSpec(memory_space=pl.ANY)


def cis(phase):
    quarter = NG // 4
    turned = phase + quarter // 2
    quadrant = (turned & (NG - 1)) // quarter
    rest = (turned & (quarter - 1)) - quarter // 2
    t = rest.astype(jnp.float32) * (2.0 * math.pi / NG)
    t2 = t * t
    s = t * (1 + t2 * (-1 / 6 + t2 * (1 / 120 + t2 * (-1 / 5040 + t2 * (1 / 362880)))))
    c = 1 + t2 * (-1 / 2 + t2 * (1 / 24 + t2 * (-1 / 720 + t2 * (1 / 40320))))
    odd = (quadrant & 1) == 1
    real = jnp.where(odd, s, c)
    imag = jnp.where(odd, c, s)
    real = jnp.where((quadrant == 1) | (quadrant == 2), -real, real)
    imag = jnp.where(quadrant >= 2, -imag, imag)
    return real, imag


def times(a, b):
    return a[0] * b[0] - a[1] * b[1], a[0] * b[1] + a[1] * b[0]


def iota(shape, dim):
    return lax.broadcasted_iota(jnp.int32, shape, dim)


def stacked_rows(values, height):
    row = iota((height, 1), 0)
    result = jnp.zeros((height, 1), jnp.int32)
    for k, value in enumerate(values):
        result = jnp.where(row == k, value, result)
    return result


def store_stacked(ref, row, high, depth, real, imag):
    h = real.shape[0]
    real, imag, minus = (x.astype(jnp.bfloat16) for x in (real, imag, -imag))
    ref[row : row + h, :depth] = real
    ref[row : row + h, depth:] = minus
    ref[row + high : row + high + h, :depth] = imag
    ref[row + high : row + high + h, depth:] = real


def in_hbm(*arrays):
    return [pltpu.with_memory_space_constraint(x, pltpu.HBM) for x in arrays]


def small_copies(sources, targets, sems):
    return [pltpu.make_async_copy(s, t, sems.at[k]) for k, (s, t) in enumerate(zip(sources, targets))]


def build_table(table, small, first, slots, depth):
    few = (small[0], small[1])
    many = (small[2], small[3])
    for k in range(slots):
        k0, k1 = divmod(first + k, TILE)
        x = tuple(jnp.broadcast_to(small[4 + 2 * k0 + z, k1 : k1 + 1, :], (TILE, depth)) for z in range(2))
        xa = times(x, many)
        for a in range(0, FR // TILE, 2):
            parts = [
                times(tuple(jnp.broadcast_to(v[a + t : a + t + 1], (TILE, depth)) for v in xa), few)
                for t in range(2)
            ]
            real = jnp.concatenate([parts[0][0], parts[1][0]], axis=0)
            imag = jnp.concatenate([parts[0][1], parts[1][1]], axis=0)
            store_stacked(table, k * 2 * FR + a * TILE, FR, depth, real, imag)


def wave_rows(out, span, first, count, block):
    width = out.shape[1]
    lane = iota((TILE, width), 1)
    sub = iota((TILE, width), 0)
    few = cis(lane * sub)
    for k in range(count):
        base = (block * count + k) * (TILE * TILE)
        coarse = cis(lane * (first + base + sub * TILE))
        for a in range(0, TILE, 2):
            parts = [
                times(tuple(jnp.broadcast_to(v[a + t : a + t + 1], (TILE, width)) for v in coarse), few)
                for t in range(2)
            ]
            row = pl.multiple_of(base + a * TILE, 2 * TILE)
            for z in range(2):
                value = jnp.concatenate([parts[0][z], parts[1][z]], axis=0)
                out[pl.ds(row + z * span, 2 * TILE), :] = value.astype(out.dtype)


def multiply(table, right, first, out, beside=None):
    depth = right.shape[1]
    piece = 2 * LANES

    def step(n, carry):
        at = pl.ds(pl.multiple_of(n * piece, piece), piece)
        source = pl.ds(pl.multiple_of(first + n * piece, piece), piece)
        if beside is not None:
            beside(source, n)
        value = right[:, :, source].reshape(2 * depth, piece)
        out[:, at] = jnp.dot(table[...], value, preferred_element_type=jnp.float32).astype(out.dtype)
        return carry

    lax.fori_loop(0, out.shape[1] // piece, step, 0)


def first_kernel(slots, first_scale, second_scale, *refs):
    sources, (col, count, vis), outs = refs[:3], refs[3:6], refs[6:12]
    out, kept, other, own, turned, later = outs
    targets, (small, small_sems, vis_sems) = refs[12:15], refs[15:]
    _, depth, width = vis.shape
    piece = 2 * LANES
    loads = small_copies(sources, targets, small_sems)

    def block(at, n):
        return pltpu.make_async_copy(vis.at[:, :, at], kept.at[:, :, at], vis_sems.at[n])

    for copy in loads + [block(pl.ds(n * piece, piece), n) for n in range(width // piece)]:
        copy.start()
    for copy in loads:
        copy.wait()
    offs, order, roff = targets
    c = lax.axis_index("col")
    u = col[0] + iota((TILE, depth), 1)
    sub = iota((TILE, depth), 0)
    small[0], small[1] = cis(u * sub)
    small[2], small[3] = cis(u * (sub * TILE))
    live = jnp.where(iota((TILE, depth), 1) < count[0, 0], first_scale, 0.0)
    starts = []
    for flip in (1, 0):
        for k in range(slots):
            slot = (((c // 2) ^ k) * 2) + ((c % 2) ^ flip)
            starts.append((offs[0, order[slot]] + (FS // 2 - FR // 2)) % NG)
    for k in range(0, 2 * slots, TILE):
        xs = cis(u * stacked_rows(starts[k : k + TILE], TILE))
        at = 4 + 2 * (k // TILE)
        small[at], small[at + 1] = xs[0] * live, xs[1] * live
    build_table(other, small, 0, slots, depth)
    build_table(own, small, slots, slots, depth)
    rows = roff.shape[0]
    r = lax.axis_index("row")
    start = offs[1, order[c]]
    height, wide = later.shape[1:]
    blocks = stacked_rows([(start + (r ^ b) * wide) % NG for b in range(rows)], height)
    origins = [roff[r ^ p] for p in range(rows)]
    for p in range(rows):
        phase = cis((origins[p] + iota((height, width), 1)) * blocks)
        turned[2 * p], turned[2 * p + 1] = phase[0] * second_scale, phase[1] * second_scale
    later[0], later[1] = cis(iota((height, wide), 1) * stacked_rows(origins, height))
    for b in range(rows):
        j = ((r ^ b) * wide + iota((1, wide), 1)).astype(jnp.float32)
        later[2, b : b + 1, :] = 1.0 / (1.0 - BEAM_SLOPE * (j + 0.5) / FS)
    multiply(other, kept, 0, out, lambda at, n: block(at, n).wait())
    for n in range(out.shape[1] // piece, width // piece):
        block(pl.ds(n * piece, piece), n).wait()


def first_columns(slots, span, scales, wide, offs, order, roff, col, count, vis):
    _, depth, width = vis.shape
    tall = slots * 2 * FR
    rows = roff.shape[0]
    height = -(-rows // TILE) * TILE
    smalls = 4 + 2 * -(-2 * slots // TILE)
    return pl.pallas_call(
        functools.partial(first_kernel, slots, *scales),
        in_specs=[HBM] * 3 + [SMEM] * 2 + [HBM],
        out_specs=[VMEM] * 6,
        out_shape=[
            jax.ShapeDtypeStruct((tall, span), jnp.bfloat16),
            jax.ShapeDtypeStruct(vis.shape, vis.dtype),
            jax.ShapeDtypeStruct((tall, 2 * depth), jnp.bfloat16),
            jax.ShapeDtypeStruct((tall, 2 * depth), jnp.bfloat16),
            jax.ShapeDtypeStruct((2 * rows, height, width), jnp.float32),
            jax.ShapeDtypeStruct((3, height, wide), jnp.float32),
        ],
        scratch_shapes=[pltpu.SMEM(x.shape, x.dtype) for x in (offs, order, roff)]
        + [
            pltpu.VMEM((smalls, TILE, depth), jnp.float32),
            pltpu.SemaphoreType.DMA((3,)),
            pltpu.SemaphoreType.DMA((width // (2 * LANES),)),
        ],
        compiler_params=pltpu.CompilerParams(vmem_limit_bytes=20 * MIB),
        cost_estimate=pl.CostEstimate(flops=tall * 4 * depth * span, bytes_accessed=4 * depth * width, transcendentals=0),
        name="first",
    )(*in_hbm(offs, order, roff), col, count, *in_hbm(vis))


def more_kernel(first, waves, table, kept, after, out, *wave):
    del after
    span = out.shape[1]
    steps = span // (2 * LANES)

    def beside(source, n):
        if waves:
            wave_rows(wave[0], span, first, span // (steps * TILE * TILE), n)

    multiply(table, kept, first, out, beside)


def more_columns(first, span, dtype, wide, table, kept, after):
    _, depth, _ = kept.shape
    tall = table.shape[0]
    shape = [jax.ShapeDtypeStruct((tall, span), dtype)]
    if wide:
        shape.append(jax.ShapeDtypeStruct((2 * span, wide), jnp.bfloat16))
    return pl.pallas_call(
        functools.partial(more_kernel, first, bool(wide)),
        in_specs=[VMEM] * 2 + [HBM],
        out_specs=[VMEM] * len(shape),
        out_shape=shape,
        compiler_params=pltpu.CompilerParams(vmem_limit_bytes=16 * MIB),
        cost_estimate=pl.CostEstimate(flops=tall * 4 * depth * span, bytes_accessed=4 * depth * span, transcendentals=0),
        name="more",
    )(table, kept, after)


def pair_kernel(mine, taken, total, *sent):
    high = total.shape[0]
    total[...] = mine[:high] + taken[:high].astype(jnp.float32)
    for k, out in enumerate(sent):
        at = slice((k + 1) * high, (k + 2) * high)
        out[...] = (mine[at] + taken[at].astype(jnp.float32)).astype(out.dtype)


def pair_sum(slots, mine, taken):
    rows, width = mine.shape
    high = rows // slots
    return pl.pallas_call(
        pair_kernel,
        in_specs=[VMEM] * 2,
        out_specs=[VMEM] * slots,
        out_shape=[jax.ShapeDtypeStruct((high, width), jnp.float32)]
        + [jax.ShapeDtypeStruct((high, width), jnp.bfloat16)] * (slots - 1),
        compiler_params=pltpu.CompilerParams(vmem_limit_bytes=8 * MIB),
        name="pair",
    )(mine, taken)


def sum_kernel(arrived, total, *refs):
    taken, outs = refs[:arrived], refs[arrived:]
    double, _ = outs[0].shape
    high = double // 2
    rows = len(outs)
    span = high * rows
    r = lax.axis_index("row")

    def rows_at(at):
        value = total[at, :]
        for other in taken:
            value = value + other[at, :].astype(jnp.float32)
        return value

    for p in range(rows):
        for z in range(2):
            if high % TILE == 0:
                at = pl.ds(pl.multiple_of(z * span + (r ^ p) * high, high), high)
                outs[p][z * high : (z + 1) * high, :] = rows_at(at).astype(outs[p].dtype)
    if high % TILE != 0:
        value = rows_at(slice(0, 2 * span))
        for p in range(rows):
            parts = []
            for z in range(2):
                part = value[z * span : z * span + high]
                for q in range(1, rows):
                    at = z * span + q * high
                    part = jnp.where((r ^ p) == q, value[at : at + high], part)
                parts.append(part)
            outs[p][...] = jnp.concatenate(parts, axis=0).astype(outs[p].dtype)


def sum_of(rows, total, taken):
    depth = total.shape[1]
    return pl.pallas_call(
        functools.partial(sum_kernel, len(taken)),
        in_specs=[VMEM] * (len(taken) + 1),
        out_specs=[VMEM] * rows,
        out_shape=[jax.ShapeDtypeStruct((total.shape[0] // rows, depth), jnp.bfloat16)] * rows,
        compiler_params=pltpu.CompilerParams(vmem_limit_bytes=16 * MIB),
        name="sum",
    )(total, *taken)


def row_kernel(rows, first, earlier, last, wave, turned, later, *refs):
    pieces, refs = refs[:rows], refs[rows:]
    before, refs = refs[:earlier], refs[earlier:]
    outs, left = refs[:-1], refs[-1]
    double, span = pieces[0].shape
    high = double // 2
    width = wave.shape[1]
    for p in range(rows):
        value = pieces[p][...].astype(jnp.float32)
        value = (value[:high], value[high:])
        for b in range(rows):
            turn = tuple(
                jnp.broadcast_to(turned[2 * p + z, b : b + 1, first : first + span], (high, span)) for z in range(2)
            )
            real, imag = times(value, turn)
            store_stacked(left, (p * rows + b) * double, high, span, real, imag)
    piece = min(2 * LANES, width)
    largest = jnp.zeros((high, LANES), jnp.float32)
    for n in range(0, width, piece):
        product = jnp.dot(left[...], wave[:, n : n + piece], preferred_element_type=jnp.float32)
        if earlier:
            product = product + before[0][:, n : n + piece]
        if not last:
            outs[0][:, n : n + piece] = product
            continue
        for b in range(rows):
            real = imag = None
            for p in range(rows):
                at = (p * rows + b) * double
                value = (product[at : at + high], product[at + high : at + double])
                turn = tuple(later[z, p : p + 1, n : n + piece] for z in range(2))
                x, y = times(value, turn)
                real = x if real is None else real + x
                imag = y if imag is None else imag + y
            beam = later[2, b : b + 1, n : n + piece]
            real = real * beam
            imag = imag * beam
            power = real * real + imag * imag
            both = jnp.concatenate([real, imag], axis=0).astype(jnp.bfloat16)
            for m in range(0, piece, LANES):
                at = (n + m) // LANES * double
                outs[b][at : at + double] = both[:, m : m + LANES]
                largest = jnp.maximum(largest, power[:, m : m + LANES])
    if not last:
        return
    peak = jnp.broadcast_to(jnp.sqrt(jnp.max(largest, keepdims=True)), (2 * TILE, LANES))
    one = peak.astype(jnp.bfloat16).astype(jnp.float32)
    two = (peak - one).astype(jnp.bfloat16).astype(jnp.float32)
    three = peak - one - two
    sub = iota((2 * TILE, LANES), 0)
    peak = jnp.where(sub == 0, one, jnp.where(sub == 1, two, jnp.where(sub == 2, three, 0.0)))
    for b in range(rows):
        outs[b][width // LANES * double :] = peak.astype(jnp.bfloat16)


def rows_of(first, last, pieces, wave, turned, later, before):
    rows = len(pieces)
    double, span = pieces[0].shape
    width = wave.shape[1]
    if last:
        shape = [jax.ShapeDtypeStruct((width // LANES * double + 2 * TILE, LANES), jnp.bfloat16)] * rows
    else:
        shape = [jax.ShapeDtypeStruct((rows * rows * double, width), jnp.float32)]
    return pl.pallas_call(
        functools.partial(row_kernel, rows, first, len(before), last),
        in_specs=[VMEM] * (rows + 3 + len(before)),
        out_specs=[VMEM] * len(shape),
        out_shape=shape,
        scratch_shapes=[pltpu.VMEM((rows * rows * double, 2 * span), jnp.bfloat16)],
        compiler_params=pltpu.CompilerParams(vmem_limit_bytes=24 * MIB),
        cost_estimate=pl.CostEstimate(
            flops=rows * rows * double * 4 * span * width, bytes_accessed=4 * span * width, transcendentals=0
        ),
    )(wave, turned, later, *pieces, *before)


def finish_kernel(rows, chunks, *refs):
    pieces, (image, peak) = refs[:rows], refs[rows:]
    width = image.shape[3]
    high = image.shape[2] // (rows * chunks)
    tall = width // LANES * 2 * high
    r = lax.axis_index("row")
    largest = None
    for p in range(rows):
        for h in range(chunks):
            for n in range(0, width, LANES):
                row = h * tall + n // LANES * 2 * high
                if high % TILE == 0:
                    at = pl.ds(pl.multiple_of((h * rows + (r ^ p)) * high, high), high)
                    value = pieces[p][row : row + 2 * high, :].astype(jnp.float32)
                else:
                    at = pl.ds((h * rows + p) * high, high)
                    value = pieces[0][row : row + 2 * high, :].astype(jnp.float32)
                    for q in range(1, rows):
                        other = pieces[q][row : row + 2 * high, :].astype(jnp.float32)
                        value = jnp.where((r ^ p) == q, other, value)
                image[0, 0, at, n : n + LANES] = value[:high]
                image[0, 1, at, n : n + LANES] = value[high:]
        parts = pieces[p][chunks * tall :, :].astype(jnp.float32)
        value = (parts[0:1] + parts[1:2]) + parts[2:3]
        largest = value if largest is None else jnp.maximum(largest, value)
    peak[0] = jnp.max(largest)


def finish(pieces, chunks, width):
    rows = len(pieces)
    return pl.pallas_call(
        functools.partial(finish_kernel, rows, chunks),
        in_specs=[VMEM] * rows,
        out_specs=[VMEM, SMEM],
        out_shape=[
            jax.ShapeDtypeStruct((1, 2, FR, width), jnp.float32),
            jax.ShapeDtypeStruct((1,), jnp.float32),
        ],
        compiler_params=pltpu.CompilerParams(vmem_limit_bytes=16 * MIB),
        name="finish",
    )(*pieces)


def step(visibilities, col_offsets, row_offsets, facet_offsets, facet_order, vis_counts):
    cols = lax.axis_size("col")
    rows = lax.axis_size("row")
    _, depth, width = visibilities.shape
    slots = cols // 2
    wide = FS // rows
    chunks = 2
    span = width // chunks
    scales = (1.0 / math.sqrt(depth * cols), 0.5 / math.sqrt(width * rows))

    def swap(value, axis, count, bit):
        return lax.ppermute(value, axis, [(i, i ^ bit) for i in range(count)])

    given, kept, other, own, turned, later = first_columns(
        slots, span, scales, wide, facet_offsets.T, facet_order, row_offsets, col_offsets, vis_counts, visibilities
    )
    totals, sents, waves = [], [], []
    for h in range(chunks):
        if h > 0:
            (given,) = more_columns(h * span, span, jnp.bfloat16, 0, other, kept, totals[h - 1])
        taken = swap(given, "col", cols, 1)
        mine, wave = more_columns(h * span, span, jnp.float32, wide, own, kept, given)
        total, *sent = pair_sum(slots, mine, taken)
        waves.append(wave)
        totals.append(total)
        sents.append([swap(value, "col", cols, 2 * k + 2) for k, value in enumerate(sent)])
    pieces = []
    for h in range(chunks):
        mine, *others = sum_of(rows, totals[h], sents[h])
        far = [swap(value, "row", rows, p + 1) for p, value in reversed(list(enumerate(others)))]
        pieces.append([mine] + far[::-1])
    parts = []
    for h in range(chunks):
        parts = rows_of(h * span, h == chunks - 1, pieces[h], waves[h], turned, later, parts)
    far = [swap(part, "row", rows, p) for p, part in reversed(list(enumerate(parts))) if p > 0]
    parts = [parts[0]] + far[::-1]
    return tuple(finish(parts, 1, wide))


def solution(mesh):
    in_specs = (P(None, "col", "row"), P("col"), P(), P(), P(), P("col", "row"))
    out_specs = (P("col", None, None, "row"), P("col"))
    return jax.shard_map(step, mesh=mesh, in_specs=in_specs, out_specs=out_specs, check_vma=False)
```

time: 49.8 us -> 48.2 us (0.968)
  waiting for transfers between devices: 18.5 us -> 7.93 us
  starting transfers between devices: 13.8 us -> 23.6 us
  Pallas kernels: 15.3 us -> 14.6 us
    ppermute x10 -> x17, waiting for transfers between devices: 18.5 us -> 7.93 us  [swap(): return lax.ppermute(value, axis, [(i, i ^ bit) for i in range(count)])]
    ppermute x10 -> x17, starting transfers between devices: 13.8 us -> 23.6 us  [swap(): return lax.ppermute(value, axis, [(i, i ^ bit) for i in range(count)])]
    pallas_call x5 -> x7, Pallas kernels: 15 us -> 14.3 us  [the longest x3 6.76 us: more_columns(): pl.pallas_call(functools.partial(more_kernel, first, bool(wide)), in_spec...]
  transfers between devices with their start and end apart: 10 -> 17, of which waited for: 8 -> 5; matrix products, arithmetic and copies ran while one was open for 0% -> 0% of each run, Pallas kernels for 11% -> 14%
where the time goes in v3:
time: 48.2 us; the launch traced here: 48.1 us
  starting transfers between devices  23.6 us (49%)
  Pallas kernels  14.6 us (30%)
  waiting for transfers between devices  7.93 us (16%)
  between operations  2.03 us (4%)
    ppermute x17, starting transfers between devices, swap(): return lax.ppermute(value, axis, [(i, i ^ bit) for i in range(count)])  23.6 us
    ppermute x17, waiting for transfers between devices, swap(): return lax.ppermute(value, axis, [(i, i ^ bit) for i in range(count)])  7.93 us
    pallas_call x3, Pallas kernels, more_columns(): pl.pallas_call(functools.partial(more_kernel, first, bool(wide)), in_spec...  6.76 us
    pallas_call x1, Pallas kernels, first_columns(): pl.pallas_call(functools.partial(first_kernel, slots, *scales), in_specs=...  3.85 us
    pallas_call x2, Pallas kernels, rows_of(): pl.pallas_call(functools.partial(row_kernel, rows, first, len(before), la...  2.81 us
  transfers between devices with their start and end apart: 17, of which 5 were waited for; matrix products, arithmetic and copies ran while one was open for 0% of the time, Pallas kernels for 14%

profile of v3, /device:TPU:0, one launch (start us, length us, event | category | flops | bytes accessed | tf_op | source)
XLA Modules:
  0.0 48.1 jit_solution(465468531803217962)
XLA Ops:
  1.9 3.9 %first.1 = (bf16[512,512]{1,0:T(8,128)(2,1)S(1)}, bf16[2,1024,1024]{2,1,0:T(8,128)(2,1)S(1)}, bf16[512,2048]{1,0:T(8,128)(2,1)S(1)}, bf16[512,2048]{1,0:T(8,128)...) custom-call(s32[2,8]{1,0:T(2,128)} %bitcast.1, s32[8]{0:T(128)} %refs_1_.1, s32[4]{0:T(128)} %refs_2_.1, ...), custom_call_target="tpu_custom_call" | custom-call | flops 1073741824 | bytes 4194304 | tf_op jit(solution)/shard_map/first/pallas_call | solution.py:183
  5.8 0.6 %collective-permute-start = (bf16[512,512]{1,0:T(8,128)(2,1)S(1)}, bf16[512,512]{1,0:T(8,128)(2,1)S(1)}, u32[]{:S(2)}, u32[]{:S(2)}) collective-permute-start(bf16[512,512]{1,0:T(8,128)(2,1)S(1)} %get-tuple-element.35.after), channel_id=1, source_target_pairs={{0,4},{4,0},{8,12},{12,8},{16,20},{20,16},{24,28},{28,24},{1,5},{5... | collective-permute-start | bytes 1572872 | tf_op jit(solution)/shard_map/ppermute | solution.py:432
  6.3 2.6 %more.3 = (f32[512,512]{1,0:T(8,128)S(1)}, bf16[1024,1024]{1,0:T(8,128)(2,1)S(1)}) custom-call(bf16[512,2048]{1,0:T(8,128)(2,1)S(1)} %get-tuple-element.32.table, bf16[2,1024,1024]{2,1,0:T(8,128)(2,1)S(1)} %get-tuple-element.33.kept, bf16[512,512]{1,0:T(8,128)(2,1)S(1)} %get-tuple-element.35.after), custom_call_target="tpu_custom_call" | custom-call | flops 1073741824 | bytes 2097152 | tf_op jit(solution)/shard_map/more/pallas_call | solution.py:225
  9.0 0.1 pair.2
  9.1 1.5 %more.4.after = bf16[512,512]{1,0:T(8,128)(2,1)S(1)} custom-call(bf16[512,2048]{1,0:T(8,128)(2,1)S(1)} %get-tuple-element.34.table, bf16[2,1024,1024]{2,1,0:T(8,128)(2,1)S(1)} %get-tuple-element.33.kept, f32[128,512]{1,0:T(8,128)S(1)} %get-tuple-element.37.after.total), custom_call_target="tpu_custom_call" | custom-call | flops 1073741824 | bytes 2097152 | tf_op jit(solution)/shard_map/more/pallas_call | solution.py:225
  10.6 0.1 collective-permute-start.1
  10.7 3.0 %collective-permute-start.8 = (bf16[128,512]{1,0:T(8,128)(2,1)S(1)}, bf16[128,512]{1,0:T(8,128)(2,1)S(1)}, u32[]{:S(2)}, u32[]{:S(2)}) collective-permute-start(bf16[128,512]{1,0:T(8,128)(2,1)S(1)} %get-tuple-element.51), channel_id=1, source_target_pairs={{0,8},{4,12},{8,0},{12,4},{16,24},{20,28},{24,16},{28,20},{1,9},{5... | collective-permute-start | bytes 393224 | tf_op jit(solution)/shard_map/ppermute | solution.py:432
  13.6 1.5 %collective-permute-start.9 = (bf16[128,512]{1,0:T(8,128)(2,1)S(1)}, bf16[128,512]{1,0:T(8,128)(2,1)S(1)}, u32[]{:S(2)}, u32[]{:S(2)}) collective-permute-start(bf16[128,512]{1,0:T(8,128)(2,1)S(1)} %get-tuple-element.52), channel_id=1, source_target_pairs={{0,16},{4,20},{8,24},{12,28},{16,0},{20,4},{24,8},{28,12},{1,17},{... | collective-permute-start | bytes 393224 | tf_op jit(solution)/shard_map/ppermute | solution.py:432
  15.2 2.6 %more.5 = (f32[512,512]{1,0:T(8,128)S(1)}, bf16[1024,1024]{1,0:T(8,128)(2,1)S(1)}) custom-call(bf16[512,2048]{1,0:T(8,128)(2,1)S(1)} %get-tuple-element.32.table, bf16[2,1024,1024]{2,1,0:T(8,128)(2,1)S(1)} %get-tuple-element.33.kept, bf16[512,512]{1,0:T(8,128)(2,1)S(1)} %more.4.after), custom_call_target="tpu_custom_call" | custom-call | flops 1073741824 | bytes 2097152 | tf_op jit(solution)/shard_map/more/pallas_call | solution.py:225
  17.8 0.1 pair.3
  17.9 2.0 %collective-permute-start.2 = (bf16[128,512]{1,0:T(8,128)(2,1)S(1)}, bf16[128,512]{1,0:T(8,128)(2,1)S(1)}, u32[]{:S(2)}, u32[]{:S(2)}) collective-permute-start(bf16[128,512]{1,0:T(8,128)(2,1)S(1)} %get-tuple-element.43), channel_id=1, source_target_pairs={{0,8},{4,12},{8,0},{12,4},{16,24},{20,28},{24,16},{28,20},{1,9},{5... | collective-permute-start | bytes 393224 | tf_op jit(solution)/shard_map/ppermute | solution.py:432
  19.9 1.5 %collective-permute-start.3 = (bf16[128,512]{1,0:T(8,128)(2,1)S(1)}, bf16[128,512]{1,0:T(8,128)(2,1)S(1)}, u32[]{:S(2)}, u32[]{:S(2)}) collective-permute-start(bf16[128,512]{1,0:T(8,128)(2,1)S(1)} %get-tuple-element.44), channel_id=1, source_target_pairs={{0,16},{4,20},{8,24},{12,28},{16,0},{20,4},{24,8},{28,12},{1,17},{... | collective-permute-start | bytes 393224 | tf_op jit(solution)/shard_map/ppermute | solution.py:432
  21.5 0.0 collective-permute-start.4
  21.5 0.2 collective-permute-done.9.refs_1_
  21.7 0.1 sum.3
  21.8 1.9 %collective-permute-start.11 = (bf16[32,512]{1,0:T(8,128)(2,1)S(1)}, bf16[32,512]{1,0:T(8,128)(2,1)S(1)}, u32[]{:S(2)}, u32[]{:S(2)}) collective-permute-start(bf16[32,512]{1,0:T(8,128)(2,1)S(1)} %get-tuple-element.55), channel_id=1, source_target_pairs={{0,1},{1,0},{2,3},{3,2},{4,5},{5,4},{6,7},{7,6},{8,9},{9,8},{10,11... | collective-permute-start | bytes 98312 | tf_op jit(solution)/shard_map/ppermute | solution.py:432
  23.7 2.6 %collective-permute-start.12 = (bf16[32,512]{1,0:T(8,128)(2,1)S(1)}, bf16[32,512]{1,0:T(8,128)(2,1)S(1)}, u32[]{:S(2)}, u32[]{:S(2)}) collective-permute-start(bf16[32,512]{1,0:T(8,128)(2,1)S(1)} %get-tuple-element.56), channel_id=1, source_target_pairs={{0,2},{1,3},{2,0},{3,1},{4,6},{5,7},{6,4},{7,5},{8,10},{9,11},{10,... | collective-permute-start | bytes 98312 | tf_op jit(solution)/shard_map/ppermute | solution.py:432
  26.3 1.5 %collective-permute-start.13 = (bf16[32,512]{1,0:T(8,128)(2,1)S(1)}, bf16[32,512]{1,0:T(8,128)(2,1)S(1)}, u32[]{:S(2)}, u32[]{:S(2)}) collective-permute-start(bf16[32,512]{1,0:T(8,128)(2,1)S(1)} %get-tuple-element.57), channel_id=1, source_target_pairs={{0,3},{1,2},{2,1},{3,0},{4,7},{5,6},{6,5},{7,4},{8,11},{9,10},{10,... | collective-permute-start | bytes 98312 | tf_op jit(solution)/shard_map/ppermute | solution.py:432
  27.8 0.1 sum.2
  27.8 1.6 %collective-permute-start.5 = (bf16[32,512]{1,0:T(8,128)(2,1)S(1)}, bf16[32,512]{1,0:T(8,128)(2,1)S(1)}, u32[]{:S(2)}, u32[]{:S(2)}) collective-permute-start(bf16[32,512]{1,0:T(8,128)(2,1)S(1)} %get-tuple-element.47), channel_id=1, source_target_pairs={{0,1},{1,0},{2,3},{3,2},{4,5},{5,4},{6,7},{7,6},{8,9},{9,8},{10,11... | collective-permute-start | bytes 98312 | tf_op jit(solution)/shard_map/ppermute | solution.py:432
  29.4 2.6 %collective-permute-start.6 = (bf16[32,512]{1,0:T(8,128)(2,1)S(1)}, bf16[32,512]{1,0:T(8,128)(2,1)S(1)}, u32[]{:S(2)}, u32[]{:S(2)}) collective-permute-start(bf16[32,512]{1,0:T(8,128)(2,1)S(1)} %get-tuple-element.48), channel_id=1, source_target_pairs={{0,2},{1,3},{2,0},{3,1},{4,6},{5,7},{6,4},{7,5},{8,10},{9,11},{10,... | collective-permute-start | bytes 98312 | tf_op jit(solution)/shard_map/ppermute | solution.py:432
  32.0 0.2 collective-permute-start.7
  32.3 1.3 %shard_map.77.refs_4_ = f32[512,1024]{1,0:T(8,128)S(1)} custom-call(bf16[1024,1024]{1,0:T(8,128)(2,1)S(1)} %get-tuple-element.50.wave, f32[8,8,1024]{2,1,0:T(8,128)S(1)} %get-tuple-element.39.turned, f32[3,8,1024]{2,1,0:T(8,128)S(1)} %get-tuple-element.40.later, bf16[32,512]{1,0:T(8,128)(2,1)S(1)} %get-tuple-element.54.refs_0_, ...), custom_call_target="tpu_custom_call" | custom-call | flops 1073741824 | bytes 2097152 | tf_op jit(solution)/shard_map/pallas_call | solution.py:365
  33.5 1.3 %collective-permute-done.6.refs_2_ = bf16[32,512]{1,0:T(8,128)(2,1)S(1)} collective-permute-done((bf16[32,512]{1,0:T(8,128)(2,1)S(1)}, bf16[32,512]{1,0:T(8,128)(2,1)S(1)}, u32[]{:S(2)}, u32[]{:S(2)}) %collective-permute-start.6) | collective-permute-done | bytes 32800 | tf_op jit(solution)/shard_map/ppermute | solution.py:432
  34.9 3.2 %collective-permute-done.7.refs_3_ = bf16[32,512]{1,0:T(8,128)(2,1)S(1)} collective-permute-done((bf16[32,512]{1,0:T(8,128)(2,1)S(1)}, bf16[32,512]{1,0:T(8,128)(2,1)S(1)}, u32[]{:S(2)}, u32[]{:S(2)}) %collective-permute-start.7) | collective-permute-done | bytes 32800 | tf_op jit(solution)/shard_map/ppermute | solution.py:432
  38.1 1.6 %shard_map.78 = (bf16[272,128]{1,0:T(8,128)(2,1)S(1)}, bf16[272,128]{1,0:T(8,128)(2,1)S(1)}, bf16[272,128]{1,0:T(8,128)(2,1)S(1)}, bf16[272,128]{1,0:T(8,128)(2,1)S(1)}) custom-call(bf16[1024,1024]{1,0:T(8,128)(2,1)S(1)} %get-tuple-element.38.wave, f32[8,8,1024]{2,1,0:T(8,128)S(1)} %get-tuple-element.39.turned, f32[3,8,1024]{2,1,0:T(8,128)S(1)} %get-tuple-element.40.later, ...), custom_call_target="tpu_custom_call" | custom-call | flops 1073741824 | bytes 2097152 | tf_op jit(solution)/shard_map/pallas_call | solution.py:365
  39.7 0.1 collective-permute-start.14
  39.7 0.5 %collective-permute-start.15 = (bf16[272,128]{1,0:T(8,128)(2,1)S(1)}, bf16[272,128]{1,0:T(8,128)(2,1)S(1)}, u32[]{:S(2)}, u32[]{:S(2)}) collective-permute-start(bf16[272,128]{1,0:T(8,128)(2,1)S(1)} %get-tuple-element.60), channel_id=1, source_target_pairs={{0,2},{1,3},{2,0},{3,1},{4,6},{5,7},{6,4},{7,5},{8,10},{9,11},{10,... | collective-permute-start | bytes 208904 | tf_op jit(solution)/shard_map/ppermute | solution.py:432
  40.3 3.8 %collective-permute-start.16 = (bf16[272,128]{1,0:T(8,128)(2,1)S(1)}, bf16[272,128]{1,0:T(8,128)(2,1)S(1)}, u32[]{:S(2)}, u32[]{:S(2)}) collective-permute-start(bf16[272,128]{1,0:T(8,128)(2,1)S(1)} %get-tuple-element.61), channel_id=1, source_target_pairs={{0,3},{1,2},{2,1},{3,0},{4,7},{5,6},{6,5},{7,4},{8,11},{9,10},{10,... | collective-permute-start | bytes 208904 | tf_op jit(solution)/shard_map/ppermute | solution.py:432
  44.1 0.9 %collective-permute-done.15.refs_2_ = bf16[272,128]{1,0:T(8,128)(2,1)S(1)} collective-permute-done((bf16[272,128]{1,0:T(8,128)(2,1)S(1)}, bf16[272,128]{1,0:T(8,128)(2,1)S(1)}, u32[]{:S(2)}, u32[]{:S(2)}) %collective-permute-start.15) | collective-permute-done | bytes 69664 | tf_op jit(solution)/shard_map/ppermute | solution.py:432
  45.0 2.2 %collective-permute-done.16.refs_3_ = bf16[272,128]{1,0:T(8,128)(2,1)S(1)} collective-permute-done((bf16[272,128]{1,0:T(8,128)(2,1)S(1)}, bf16[272,128]{1,0:T(8,128)(2,1)S(1)}, u32[]{:S(2)}, u32[]{:S(2)}) %collective-permute-start.16) | collective-permute-done | bytes 69664 | tf_op jit(solution)/shard_map/ppermute | solution.py:432
  47.2 0.8 %finish.1 = (f32[1,2,64,1024]{3,2,1,0:T(8,128)}, f32[1]{0:T(128)}) custom-call(bf16[272,128]{1,0:T(8,128)(2,1)S(1)} %get-tuple-element.58.refs_0_, bf16[272,128]{1,0:T(8,128)(2,1)S(1)} %collective-permute-done.14.refs_1_, bf16[272,128]{1,0:T(8,128)(2,1)S(1)} %collective-permute-done.15.refs_2_, bf16[272,128]{1,0:T(8,128)(2,1)S(1)} %collective-permute-done.16.refs_3_), custom_call_target="tpu_custom_call" | custom-call | tf_op jit(solution)/shard_map/finish/pallas_call | solution.py:408
  (13 shorter events, 0.0 us)
Async XLA Ops:
  5.8 3.2 %collective-permute-start = (bf16[512,512]{1,0:T(8,128)(2,1)S(1)}, bf16[512,512]{1,0:T(8,128)(2,1)S(1)}, u32[]{:S(2)}, u32[]{:S(2)}) collective-permute-start(bf16[512,512]{1,0:T(8,128)(2,1)S(1)} %get-tuple-element.35.after), channel_id=1, source_target_pairs={{0,4},{4,0},{8,12},{12,8},{16,20},{20,16},{24,28},{28,24},{1,5},{5... | collective-permute-start | bytes 1572872 | tf_op jit(solution)/shard_map/ppermute | solution.py:432
  10.6 7.2 %collective-permute-start.1 = (bf16[512,512]{1,0:T(8,128)(2,1)S(1)}, bf16[512,512]{1,0:T(8,128)(2,1)S(1)}, u32[]{:S(2)}, u32[]{:S(2)}) collective-permute-start(bf16[512,512]{1,0:T(8,128)(2,1)S(1)} %more.4.after), channel_id=1, source_target_pairs={{0,4},{4,0},{8,12},{12,8},{16,20},{20,16},{24,28},{28,24},{1,5},{5... | collective-permute-start | bytes 1572872 | tf_op jit(solution)/shard_map/ppermute | solution.py:432
  10.7 10.8 %collective-permute-start.8 = (bf16[128,512]{1,0:T(8,128)(2,1)S(1)}, bf16[128,512]{1,0:T(8,128)(2,1)S(1)}, u32[]{:S(2)}, u32[]{:S(2)}) collective-permute-start(bf16[128,512]{1,0:T(8,128)(2,1)S(1)} %get-tuple-element.51), channel_id=1, source_target_pairs={{0,8},{4,12},{8,0},{12,4},{16,24},{20,28},{24,16},{28,20},{1,9},{5... | collective-permute-start | bytes 393224 | tf_op jit(solution)/shard_map/ppermute | solution.py:432
  13.6 8.1 %collective-permute-start.9 = (bf16[128,512]{1,0:T(8,128)(2,1)S(1)}, bf16[128,512]{1,0:T(8,128)(2,1)S(1)}, u32[]{:S(2)}, u32[]{:S(2)}) collective-permute-start(bf16[128,512]{1,0:T(8,128)(2,1)S(1)} %get-tuple-element.52), channel_id=1, source_target_pairs={{0,16},{4,20},{8,24},{12,28},{16,0},{20,4},{24,8},{28,12},{1,17},{... | collective-permute-start | bytes 393224 | tf_op jit(solution)/shard_map/ppermute | solution.py:432
  15.2 6.6 %collective-permute-start.10 = (bf16[128,512]{1,0:T(8,128)(2,1)S(1)}, bf16[128,512]{1,0:T(8,128)(2,1)S(1)}, u32[]{:S(2)}, u32[]{:S(2)}) collective-permute-start(bf16[128,512]{1,0:T(8,128)(2,1)S(1)} %get-tuple-element.53), channel_id=1, source_target_pairs={{0,24},{4,28},{8,16},{12,20},{16,8},{20,12},{24,0},{28,4},{1,25},{... | collective-permute-start | bytes 393224 | tf_op jit(solution)/shard_map/ppermute | solution.py:432
  17.9 8.3 %collective-permute-start.2 = (bf16[128,512]{1,0:T(8,128)(2,1)S(1)}, bf16[128,512]{1,0:T(8,128)(2,1)S(1)}, u32[]{:S(2)}, u32[]{:S(2)}) collective-permute-start(bf16[128,512]{1,0:T(8,128)(2,1)S(1)} %get-tuple-element.43), channel_id=1, source_target_pairs={{0,8},{4,12},{8,0},{12,4},{16,24},{20,28},{24,16},{28,20},{1,9},{5... | collective-permute-start | bytes 393224 | tf_op jit(solution)/shard_map/ppermute | solution.py:432
  19.9 7.8 %collective-permute-start.3 = (bf16[128,512]{1,0:T(8,128)(2,1)S(1)}, bf16[128,512]{1,0:T(8,128)(2,1)S(1)}, u32[]{:S(2)}, u32[]{:S(2)}) collective-permute-start(bf16[128,512]{1,0:T(8,128)(2,1)S(1)} %get-tuple-element.44), channel_id=1, source_target_pairs={{0,16},{4,20},{8,24},{12,28},{16,0},{20,4},{24,8},{28,12},{1,17},{... | collective-permute-start | bytes 393224 | tf_op jit(solution)/shard_map/ppermute | solution.py:432
  21.5 6.3 %collective-permute-start.4 = (bf16[128,512]{1,0:T(8,128)(2,1)S(1)}, bf16[128,512]{1,0:T(8,128)(2,1)S(1)}, u32[]{:S(2)}, u32[]{:S(2)}) collective-permute-start(bf16[128,512]{1,0:T(8,128)(2,1)S(1)} %get-tuple-element.45), channel_id=1, source_target_pairs={{0,24},{4,28},{8,16},{12,20},{16,8},{20,12},{24,0},{28,4},{1,25},{... | collective-permute-start | bytes 393224 | tf_op jit(solution)/shard_map/ppermute | solution.py:432
  21.8 10.2 %collective-permute-start.11 = (bf16[32,512]{1,0:T(8,128)(2,1)S(1)}, bf16[32,512]{1,0:T(8,128)(2,1)S(1)}, u32[]{:S(2)}, u32[]{:S(2)}) collective-permute-start(bf16[32,512]{1,0:T(8,128)(2,1)S(1)} %get-tuple-element.55), channel_id=1, source_target_pairs={{0,1},{1,0},{2,3},{3,2},{4,5},{5,4},{6,7},{7,6},{8,9},{9,8},{10,11... | collective-permute-start | bytes 98312 | tf_op jit(solution)/shard_map/ppermute | solution.py:432
  23.7 8.6 %collective-permute-start.12 = (bf16[32,512]{1,0:T(8,128)(2,1)S(1)}, bf16[32,512]{1,0:T(8,128)(2,1)S(1)}, u32[]{:S(2)}, u32[]{:S(2)}) collective-permute-start(bf16[32,512]{1,0:T(8,128)(2,1)S(1)} %get-tuple-element.56), channel_id=1, source_target_pairs={{0,2},{1,3},{2,0},{3,1},{4,6},{5,7},{6,4},{7,5},{8,10},{9,11},{10,... | collective-permute-start | bytes 98312 | tf_op jit(solution)/shard_map/ppermute | solution.py:432
  26.3 6.0 %collective-permute-start.13 = (bf16[32,512]{1,0:T(8,128)(2,1)S(1)}, bf16[32,512]{1,0:T(8,128)(2,1)S(1)}, u32[]{:S(2)}, u32[]{:S(2)}) collective-permute-start(bf16[32,512]{1,0:T(8,128)(2,1)S(1)} %get-tuple-element.57), channel_id=1, source_target_pairs={{0,3},{1,2},{2,1},{3,0},{4,7},{5,6},{6,5},{7,4},{8,11},{9,10},{10,... | collective-permute-start | bytes 98312 | tf_op jit(solution)/shard_map/ppermute | solution.py:432
  27.8 5.7 %collective-permute-start.5 = (bf16[32,512]{1,0:T(8,128)(2,1)S(1)}, bf16[32,512]{1,0:T(8,128)(2,1)S(1)}, u32[]{:S(2)}, u32[]{:S(2)}) collective-permute-start(bf16[32,512]{1,0:T(8,128)(2,1)S(1)} %get-tuple-element.47), channel_id=1, source_target_pairs={{0,1},{1,0},{2,3},{3,2},{4,5},{5,4},{6,7},{7,6},{8,9},{9,8},{10,11... | collective-permute-start | bytes 98312 | tf_op jit(solution)/shard_map/ppermute | solution.py:432
  29.4 5.4 %collective-permute-start.6 = (bf16[32,512]{1,0:T(8,128)(2,1)S(1)}, bf16[32,512]{1,0:T(8,128)(2,1)S(1)}, u32[]{:S(2)}, u32[]{:S(2)}) collective-permute-start(bf16[32,512]{1,0:T(8,128)(2,1)S(1)} %get-tuple-element.48), channel_id=1, source_target_pairs={{0,2},{1,3},{2,0},{3,1},{4,6},{5,7},{6,4},{7,5},{8,10},{9,11},{10,... | collective-permute-start | bytes 98312 | tf_op jit(solution)/shard_map/ppermute | solution.py:432
  32.0 6.1 %collective-permute-start.7 = (bf16[32,512]{1,0:T(8,128)(2,1)S(1)}, bf16[32,512]{1,0:T(8,128)(2,1)S(1)}, u32[]{:S(2)}, u32[]{:S(2)}) collective-permute-start(bf16[32,512]{1,0:T(8,128)(2,1)S(1)} %get-tuple-element.49), channel_id=1, source_target_pairs={{0,3},{1,2},{2,1},{3,0},{4,7},{5,6},{6,5},{7,4},{8,11},{9,10},{10,... | collective-permute-start | bytes 98312 | tf_op jit(solution)/shard_map/ppermute | solution.py:432
  39.7 4.5 %collective-permute-start.14 = (bf16[272,128]{1,0:T(8,128)(2,1)S(1)}, bf16[272,128]{1,0:T(8,128)(2,1)S(1)}, u32[]{:S(2)}, u32[]{:S(2)}) collective-permute-start(bf16[272,128]{1,0:T(8,128)(2,1)S(1)} %get-tuple-element.59), channel_id=1, source_target_pairs={{0,1},{1,0},{2,3},{3,2},{4,5},{5,4},{6,7},{7,6},{8,9},{9,8},{10,11... | collective-permute-start | bytes 208904 | tf_op jit(solution)/shard_map/ppermute | solution.py:432
  39.7 5.3 %collective-permute-start.15 = (bf16[272,128]{1,0:T(8,128)(2,1)S(1)}, bf16[272,128]{1,0:T(8,128)(2,1)S(1)}, u32[]{:S(2)}, u32[]{:S(2)}) collective-permute-start(bf16[272,128]{1,0:T(8,128)(2,1)S(1)} %get-tuple-element.60), channel_id=1, source_target_pairs={{0,2},{1,3},{2,0},{3,1},{4,6},{5,7},{6,4},{7,5},{8,10},{9,11},{10,... | collective-permute-start | bytes 208904 | tf_op jit(solution)/shard_map/ppermute | solution.py:432
  40.3 7.0 %collective-permute-start.16 = (bf16[272,128]{1,0:T(8,128)(2,1)S(1)}, bf16[272,128]{1,0:T(8,128)(2,1)S(1)}, u32[]{:S(2)}, u32[]{:S(2)}) collective-permute-start(bf16[272,128]{1,0:T(8,128)(2,1)S(1)} %get-tuple-element.61), channel_id=1, source_target_pairs={{0,3},{1,2},{2,1},{3,0},{4,7},{5,6},{6,5},{7,4},{8,11},{9,10},{10,... | collective-permute-start | bytes 208904 | tf_op jit(solution)/shard_map/ppermute | solution.py:432

commit v4 on v3

--- a/solution.py
+++ b/solution.py
@@ -21,12 +21,12 @@
 HBM = pl.BlockSpec(memory_space=pl.ANY)
 
 
-def cis(phase):
-    quarter = NG // 4
+def cis(phase, period=NG):
+    quarter = period // 4
     turned = phase + quarter // 2
-    quadrant = (turned & (NG - 1)) // quarter
+    quadrant = (turned & (period - 1)) // quarter
     rest = (turned & (quarter - 1)) - quarter // 2
-    t = rest.astype(jnp.float32) * (2.0 * math.pi / NG)
+    t = rest.astype(jnp.float32) * (2.0 * math.pi / period)
     t2 = t * t
     s = t * (1 + t2 * (-1 / 6 + t2 * (1 / 120 + t2 * (-1 / 5040 + t2 * (1 / 362880)))))
     c = 1 + t2 * (-1 / 2 + t2 * (1 / 24 + t2 * (-1 / 720 + t2 * (1 / 40320))))
@@ -88,39 +88,38 @@
             store_stacked(table, k * 2 * FR + a * TILE, FR, depth, real, imag)
 
 
-def wave_rows(out, span, first, count, block):
-    width = out.shape[1]
+def wave_rows(out, start):
+    half, width = out.shape[0] // 2, out.shape[1]
     lane = iota((TILE, width), 1)
     sub = iota((TILE, width), 0)
     few = cis(lane * sub)
-    for k in range(count):
-        base = (block * count + k) * (TILE * TILE)
-        coarse = cis(lane * (first + base + sub * TILE))
+    coarse = cis(lane * (start + sub * (2 * TILE)), 2 * NG)
+    stride = cis(lane * (TILE * TILE))
+    for base in range(0, half, TILE * TILE):
+        if base > 0:
+            coarse = times(coarse, stride)
         for a in range(0, TILE, 2):
             parts = [
                 times(tuple(jnp.broadcast_to(v[a + t : a + t + 1], (TILE, width)) for v in coarse), few)
                 for t in range(2)
             ]
-            row = pl.multiple_of(base + a * TILE, 2 * TILE)
+            row = base + a * TILE
             for z in range(2):
                 value = jnp.concatenate([parts[0][z], parts[1][z]], axis=0)
-                out[pl.ds(row + z * span, 2 * TILE), :] = value.astype(out.dtype)
-
-
-def multiply(table, right, first, out, beside=None):
-    depth = right.shape[1]
-    piece = 2 * LANES
-
-    def step(n, carry):
-        at = pl.ds(pl.multiple_of(n * piece, piece), piece)
-        source = pl.ds(pl.multiple_of(first + n * piece, piece), piece)
-        if beside is not None:
-            beside(source, n)
-        value = right[:, :, source].reshape(2 * depth, piece)
-        out[:, at] = jnp.dot(table[...], value, preferred_element_type=jnp.float32).astype(out.dtype)
-        return carry
-
-    lax.fori_loop(0, out.shape[1] // piece, step, 0)
+                out[row + z * half : row + z * half + 2 * TILE, :] = value.astype(out.dtype)
+
+
+def blocks_of(chunk, half, width):
+    return chunk * half, width - (chunk + 1) * half
+
+
+def multiply(table, right, chunk, out):
+    depth, width = right.shape[1:]
+    half = out.shape[1] // 2
+    for k, start in enumerate(blocks_of(chunk, half, width)):
+        value = right[:, :, start : start + half].reshape(2 * depth, half)
+        product = jnp.dot(table[...], value, preferred_element_type=jnp.float32)
+        out[:, k * half : (k + 1) * half] = product.astype(out.dtype)
 
 
 def first_kernel(slots, first_scale, second_scale, *refs):
@@ -128,13 +127,19 @@
     out, kept, other, own, turned, later = outs
     targets, (small, small_sems, vis_sems) = refs[12:15], refs[15:]
     _, depth, width = vis.shape
-    piece = 2 * LANES
+    half = out.shape[1] // 2
     loads = small_copies(sources, targets, small_sems)
 
-    def block(at, n):
+    def block(start, n):
+        at = pl.ds(start, half)
         return pltpu.make_async_copy(vis.at[:, :, at], kept.at[:, :, at], vis_sems.at[n])
 
-    for copy in loads + [block(pl.ds(n * piece, piece), n) for n in range(width // piece)]:
+    def wait(n, carry):
+        block(0, n).wait()
+        return carry
+
+    order_of_blocks = [start for h in range(width // (2 * half)) for start in blocks_of(h, half, width)]
+    for copy in loads + [block(start, n) for n, start in enumerate(order_of_blocks)]:
         copy.start()
     for copy in loads:
         copy.wait()
@@ -162,16 +167,21 @@
     height, wide = later.shape[1:]
     blocks = stacked_rows([(start + (r ^ b) * wide) % NG for b in range(rows)], height)
     origins = [roff[r ^ p] for p in range(rows)]
-    for p in range(rows):
-        phase = cis((origins[p] + iota((height, width), 1)) * blocks)
-        turned[2 * p], turned[2 * p + 1] = phase[0] * second_scale, phase[1] * second_scale
-    later[0], later[1] = cis(iota((height, wide), 1) * stacked_rows(origins, height))
+    lane = iota((height, half), 1)
+    for n, first in enumerate(order_of_blocks):
+        v = first + (half - 1 - lane if n % 2 == 0 else lane)
+        for p in range(rows):
+            phase = cis((origins[p] + v) * blocks)
+            for z in range(2):
+                turned[2 * p + z, :, n * half : (n + 1) * half] = phase[z] * second_scale
+    middle = [2 * origin + (width - 1) for origin in origins]
+    later[0], later[1] = cis(iota((height, wide), 1) * stacked_rows(middle, height), 2 * NG)
     for b in range(rows):
         j = ((r ^ b) * wide + iota((1, wide), 1)).astype(jnp.float32)
         later[2, b : b + 1, :] = 1.0 / (1.0 - BEAM_SLOPE * (j + 0.5) / FS)
-    multiply(other, kept, 0, out, lambda at, n: block(at, n).wait())
-    for n in range(out.shape[1] // piece, width // piece):
-        block(pl.ds(n * piece, piece), n).wait()
+    lax.fori_loop(0, 2, wait, 0)
+    multiply(other, kept, 0, out)
+    lax.fori_loop(2, len(order_of_blocks), wait, 0)
 
 
 def first_columns(slots, span, scales, wide, offs, order, roff, col, count, vis):
@@ -196,7 +206,7 @@
         + [
             pltpu.VMEM((smalls, TILE, depth), jnp.float32),
             pltpu.SemaphoreType.DMA((3,)),
-            pltpu.SemaphoreType.DMA((width // (2 * LANES),)),
+            pltpu.SemaphoreType.DMA((2 * width // span,)),
         ],
         compiler_params=pltpu.CompilerParams(vmem_limit_bytes=20 * MIB),
         cost_estimate=pl.CostEstimate(flops=tall * 4 * depth * span, bytes_accessed=4 * depth * width, transcendentals=0),
@@ -204,26 +214,22 @@
     )(*in_hbm(offs, order, roff), col, count, *in_hbm(vis))
 
 
-def more_kernel(first, waves, table, kept, after, out, *wave):
+def more_kernel(chunk, table, kept, after, out, *wave):
     del after
-    span = out.shape[1]
-    steps = span // (2 * LANES)
-
-    def beside(source, n):
-        if waves:
-            wave_rows(wave[0], span, first, span // (steps * TILE * TILE), n)
-
-    multiply(table, kept, first, out, beside)
-
-
-def more_columns(first, span, dtype, wide, table, kept, after):
+    if wave:
+        width = kept.shape[2]
+        wave_rows(wave[0], 2 * blocks_of(chunk, out.shape[1] // 2, width)[1] - (width - 1))
+    multiply(table, kept, chunk, out)
+
+
+def more_columns(chunk, span, dtype, wide, table, kept, after):
     _, depth, _ = kept.shape
     tall = table.shape[0]
     shape = [jax.ShapeDtypeStruct((tall, span), dtype)]
     if wide:
-        shape.append(jax.ShapeDtypeStruct((2 * span, wide), jnp.bfloat16))
-    return pl.pallas_call(
-        functools.partial(more_kernel, first, bool(wide)),
+        shape.append(jax.ShapeDtypeStruct((span, wide), jnp.bfloat16))
+    return pl.pallas_call(
+        functools.partial(more_kernel, chunk),
         in_specs=[VMEM] * 2 + [HBM],
         out_specs=[VMEM] * len(shape),
         out_shape=shape,
@@ -306,15 +312,28 @@
     double, span = pieces[0].shape
     high = double // 2
     width = wave.shape[1]
+    half = span // 2
+    mirror = jnp.where(iota((half, half), 0) + iota((half, half), 1) == half - 1, 1.0, 0.0).astype(jnp.bfloat16)
+    firsts = jnp.concatenate([pieces[p][:, :half] for p in range(rows)], axis=0)
+    firsts = jnp.dot(firsts, mirror, preferred_element_type=jnp.float32)
     for p in range(rows):
-        value = pieces[p][...].astype(jnp.float32)
-        value = (value[:high], value[high:])
+        near = firsts[p * double : (p + 1) * double]
+        far = pieces[p][:, half:].astype(jnp.float32)
         for b in range(rows):
-            turn = tuple(
-                jnp.broadcast_to(turned[2 * p + z, b : b + 1, first : first + span], (high, span)) for z in range(2)
-            )
-            real, imag = times(value, turn)
-            store_stacked(left, (p * rows + b) * double, high, span, real, imag)
+
+            def turn(value, at):
+                factor = (turned[2 * p + z, b : b + 1, first + at : first + at + half] for z in range(2))
+                factor = tuple(jnp.broadcast_to(v, (high, half)) for v in factor)
+                return times((value[:high], value[high:]), factor)
+
+            x, y = turn(near, 0), turn(far, half)
+            even = (y[0] + x[0], y[1] + x[1])
+            odd = (y[0] - x[0], y[1] - x[1])
+            at = (p * rows + b) * double
+            left[at : at + high, :half] = even[0].astype(left.dtype)
+            left[at : at + high, half:] = (-odd[1]).astype(left.dtype)
+            left[at + high : at + double, :half] = even[1].astype(left.dtype)
+            left[at + high : at + double, half:] = odd[0].astype(left.dtype)
     piece = min(2 * LANES, width)
     largest = jnp.zeros((high, LANES), jnp.float32)
     for n in range(0, width, piece):
@@ -367,10 +386,10 @@
         in_specs=[VMEM] * (rows + 3 + len(before)),
         out_specs=[VMEM] * len(shape),
         out_shape=shape,
-        scratch_shapes=[pltpu.VMEM((rows * rows * double, 2 * span), jnp.bfloat16)],
+        scratch_shapes=[pltpu.VMEM((rows * rows * double, span), jnp.bfloat16)],
         compiler_params=pltpu.CompilerParams(vmem_limit_bytes=24 * MIB),
         cost_estimate=pl.CostEstimate(
-            flops=rows * rows * double * 4 * span * width, bytes_accessed=4 * span * width, transcendentals=0
+            flops=rows * rows * double * 2 * span * width, bytes_accessed=2 * span * width, transcendentals=0
         ),
     )(wave, turned, later, *pieces, *before)
 
@@ -437,9 +456,9 @@
     totals, sents, waves = [], [], []
     for h in range(chunks):
         if h > 0:
-            (given,) = more_columns(h * span, span, jnp.bfloat16, 0, other, kept, totals[h - 1])
+            (given,) = more_columns(h, span, jnp.bfloat16, 0, other, kept, totals[h - 1])
         taken = swap(given, "col", cols, 1)
-        mine, wave = more_columns(h * span, span, jnp.float32, wide, own, kept, given)
+        mine, wave = more_columns(h, span, jnp.float32, wide, own, kept, given)
         total, *sent = pair_sum(slots, mine, taken)
         waves.append(wave)
         totals.append(total)

time: 48.2 us -> 45.7 us (0.948)
  Pallas kernels: 14.6 us -> 11.5 us
  waiting for transfers between devices: 7.93 us -> 8.66 us
    pallas_call x3, Pallas kernels: 6.76 us -> 4.76 us  [more_columns(): pl.pallas_call(functools.partial(more_kernel, chunk), in_specs=[VMEM] * 2...]
    pallas_call x2, Pallas kernels: 2.81 us -> 2.02 us  [rows_of(): pl.pallas_call(functools.partial(row_kernel, rows, first, len(before), la...]
    ppermute x17, waiting for transfers between devices: 7.93 us -> 8.66 us  [swap(): return lax.ppermute(value, axis, [(i, i ^ bit) for i in range(count)])]
  transfers between devices with their start and end apart: 17 -> 17, of which waited for: 5 -> 6; matrix products, arithmetic and copies ran while one was open for 0% -> 0% of each run, Pallas kernels for 14% -> 10%
where the time goes in v4:
time: 45.7 us; the launch traced here: 45.6 us
  starting transfers between devices  23.3 us (51%)
  Pallas kernels  11.5 us (25%)
  waiting for transfers between devices  8.66 us (19%)
  between operations  2.03 us (4%)
    ppermute x17, starting transfers between devices, swap(): return lax.ppermute(value, axis, [(i, i ^ bit) for i in range(count)])  23.3 us
    ppermute x17, waiting for transfers between devices, swap(): return lax.ppermute(value, axis, [(i, i ^ bit) for i in range(count)])  8.66 us
    pallas_call x3, Pallas kernels, more_columns(): pl.pallas_call(functools.partial(more_kernel, chunk), in_specs=[VMEM] * 2...  4.76 us
    pallas_call x1, Pallas kernels, first_columns(): pl.pallas_call(functools.partial(first_kernel, slots, *scales), in_specs=...  3.61 us
    pallas_call x2, Pallas kernels, rows_of(): pl.pallas_call(functools.partial(row_kernel, rows, first, len(before), la...  2.02 us
  transfers between devices with their start and end apart: 17, of which 6 were waited for; matrix products, arithmetic and copies ran while one was open for 0% of the time, Pallas kernels for 10%

profile of v4, /device:TPU:0, one launch (start us, length us, event | category | flops | bytes accessed | tf_op | source)
XLA Modules:
  0.0 45.6 jit_solution(1677612172725685389)
XLA Ops:
  1.9 3.6 %first.1 = (bf16[512,512]{1,0:T(8,128)(2,1)S(1)}, bf16[2,1024,1024]{2,1,0:T(8,128)(2,1)S(1)}, bf16[512,2048]{1,0:T(8,128)(2,1)S(1)}, bf16[512,2048]{1,0:T(8,128)...) custom-call(s32[2,8]{1,0:T(2,128)} %bitcast.1, s32[8]{0:T(128)} %refs_1_.1, s32[4]{0:T(128)} %refs_2_.1, ...), custom_call_target="tpu_custom_call" | custom-call | flops 1073741824 | bytes 4194304 | tf_op jit(solution)/shard_map/first/pallas_call | solution.py:193
  5.5 0.6 %collective-permute-start = (bf16[512,512]{1,0:T(8,128)(2,1)S(1)}, bf16[512,512]{1,0:T(8,128)(2,1)S(1)}, u32[]{:S(2)}, u32[]{:S(2)}) collective-permute-start(bf16[512,512]{1,0:T(8,128)(2,1)S(1)} %get-tuple-element.35.after), channel_id=1, source_target_pairs={{0,4},{4,0},{8,12},{12,8},{16,20},{20,16},{24,28},{28,24},{1,5},{5... | collective-permute-start | bytes 1572872 | tf_op jit(solution)/shard_map/ppermute | solution.py:451
  6.1 1.8 %more.3 = (f32[512,512]{1,0:T(8,128)S(1)}, bf16[512,1024]{1,0:T(8,128)(2,1)S(1)}) custom-call(bf16[512,2048]{1,0:T(8,128)(2,1)S(1)} %get-tuple-element.32.table, bf16[2,1024,1024]{2,1,0:T(8,128)(2,1)S(1)} %get-tuple-element.33.kept, bf16[512,512]{1,0:T(8,128)(2,1)S(1)} %get-tuple-element.35.after), custom_call_target="tpu_custom_call" | custom-call | flops 1073741824 | bytes 2097152 | tf_op jit(solution)/shard_map/more/pallas_call | solution.py:231
  7.9 0.1 pair.2
  8.0 1.2 %more.4.after = bf16[512,512]{1,0:T(8,128)(2,1)S(1)} custom-call(bf16[512,2048]{1,0:T(8,128)(2,1)S(1)} %get-tuple-element.34.table, bf16[2,1024,1024]{2,1,0:T(8,128)(2,1)S(1)} %get-tuple-element.33.kept, f32[128,512]{1,0:T(8,128)S(1)} %get-tuple-element.37.after.total), custom_call_target="tpu_custom_call" | custom-call | flops 1073741824 | bytes 2097152 | tf_op jit(solution)/shard_map/more/pallas_call | solution.py:231
  9.2 0.2 collective-permute-start.1
  9.4 2.9 %collective-permute-start.8 = (bf16[128,512]{1,0:T(8,128)(2,1)S(1)}, bf16[128,512]{1,0:T(8,128)(2,1)S(1)}, u32[]{:S(2)}, u32[]{:S(2)}) collective-permute-start(bf16[128,512]{1,0:T(8,128)(2,1)S(1)} %get-tuple-element.51), channel_id=1, source_target_pairs={{0,8},{4,12},{8,0},{12,4},{16,24},{20,28},{24,16},{28,20},{1,9},{5... | collective-permute-start | bytes 393224 | tf_op jit(solution)/shard_map/ppermute | solution.py:451
  12.3 1.5 %collective-permute-start.9 = (bf16[128,512]{1,0:T(8,128)(2,1)S(1)}, bf16[128,512]{1,0:T(8,128)(2,1)S(1)}, u32[]{:S(2)}, u32[]{:S(2)}) collective-permute-start(bf16[128,512]{1,0:T(8,128)(2,1)S(1)} %get-tuple-element.52), channel_id=1, source_target_pairs={{0,16},{4,20},{8,24},{12,28},{16,0},{20,4},{24,8},{28,12},{1,17},{... | collective-permute-start | bytes 393224 | tf_op jit(solution)/shard_map/ppermute | solution.py:451
  13.8 1.8 %more.5 = (f32[512,512]{1,0:T(8,128)S(1)}, bf16[512,1024]{1,0:T(8,128)(2,1)S(1)}) custom-call(bf16[512,2048]{1,0:T(8,128)(2,1)S(1)} %get-tuple-element.32.table, bf16[2,1024,1024]{2,1,0:T(8,128)(2,1)S(1)} %get-tuple-element.33.kept, bf16[512,512]{1,0:T(8,128)(2,1)S(1)} %more.4.after), custom_call_target="tpu_custom_call" | custom-call | flops 1073741824 | bytes 2097152 | tf_op jit(solution)/shard_map/more/pallas_call | solution.py:231
  15.6 0.1 pair.3
  15.7 2.0 %collective-permute-start.2 = (bf16[128,512]{1,0:T(8,128)(2,1)S(1)}, bf16[128,512]{1,0:T(8,128)(2,1)S(1)}, u32[]{:S(2)}, u32[]{:S(2)}) collective-permute-start(bf16[128,512]{1,0:T(8,128)(2,1)S(1)} %get-tuple-element.43), channel_id=1, source_target_pairs={{0,8},{4,12},{8,0},{12,4},{16,24},{20,28},{24,16},{28,20},{1,9},{5... | collective-permute-start | bytes 393224 | tf_op jit(solution)/shard_map/ppermute | solution.py:451
  17.7 1.5 %collective-permute-start.3 = (bf16[128,512]{1,0:T(8,128)(2,1)S(1)}, bf16[128,512]{1,0:T(8,128)(2,1)S(1)}, u32[]{:S(2)}, u32[]{:S(2)}) collective-permute-start(bf16[128,512]{1,0:T(8,128)(2,1)S(1)} %get-tuple-element.44), channel_id=1, source_target_pairs={{0,16},{4,20},{8,24},{12,28},{16,0},{20,4},{24,8},{28,12},{1,17},{... | collective-permute-start | bytes 393224 | tf_op jit(solution)/shard_map/ppermute | solution.py:451
  19.2 0.4 collective-permute-start.4
  19.6 0.5 %collective-permute-done.9.refs_1_ = bf16[128,512]{1,0:T(8,128)(2,1)S(1)} collective-permute-done((bf16[128,512]{1,0:T(8,128)(2,1)S(1)}, bf16[128,512]{1,0:T(8,128)(2,1)S(1)}, u32[]{:S(2)}, u32[]{:S(2)}) %collective-permute-start.9) | collective-permute-done | bytes 131104 | tf_op jit(solution)/shard_map/ppermute | solution.py:451
  20.1 1.1 %collective-permute-done.10.refs_2_ = bf16[128,512]{1,0:T(8,128)(2,1)S(1)} collective-permute-done((bf16[128,512]{1,0:T(8,128)(2,1)S(1)}, bf16[128,512]{1,0:T(8,128)(2,1)S(1)}, u32[]{:S(2)}, u32[]{:S(2)}) %collective-permute-start.10) | collective-permute-done | bytes 131104 | tf_op jit(solution)/shard_map/ppermute | solution.py:451
  21.1 0.1 sum.3
  21.2 1.6 %collective-permute-start.11 = (bf16[32,512]{1,0:T(8,128)(2,1)S(1)}, bf16[32,512]{1,0:T(8,128)(2,1)S(1)}, u32[]{:S(2)}, u32[]{:S(2)}) collective-permute-start(bf16[32,512]{1,0:T(8,128)(2,1)S(1)} %get-tuple-element.55), channel_id=1, source_target_pairs={{0,1},{1,0},{2,3},{3,2},{4,5},{5,4},{6,7},{7,6},{8,9},{9,8},{10,11... | collective-permute-start | bytes 98312 | tf_op jit(solution)/shard_map/ppermute | solution.py:451
  22.8 2.6 %collective-permute-start.12 = (bf16[32,512]{1,0:T(8,128)(2,1)S(1)}, bf16[32,512]{1,0:T(8,128)(2,1)S(1)}, u32[]{:S(2)}, u32[]{:S(2)}) collective-permute-start(bf16[32,512]{1,0:T(8,128)(2,1)S(1)} %get-tuple-element.56), channel_id=1, source_target_pairs={{0,2},{1,3},{2,0},{3,1},{4,6},{5,7},{6,4},{7,5},{8,10},{9,11},{10,... | collective-permute-start | bytes 98312 | tf_op jit(solution)/shard_map/ppermute | solution.py:451
  25.4 1.2 %collective-permute-start.13 = (bf16[32,512]{1,0:T(8,128)(2,1)S(1)}, bf16[32,512]{1,0:T(8,128)(2,1)S(1)}, u32[]{:S(2)}, u32[]{:S(2)}) collective-permute-start(bf16[32,512]{1,0:T(8,128)(2,1)S(1)} %get-tuple-element.57), channel_id=1, source_target_pairs={{0,3},{1,2},{2,1},{3,0},{4,7},{5,6},{6,5},{7,4},{8,11},{9,10},{10,... | collective-permute-start | bytes 98312 | tf_op jit(solution)/shard_map/ppermute | solution.py:451
  26.6 1.0 %collective-permute-start.5 = (bf16[32,512]{1,0:T(8,128)(2,1)S(1)}, bf16[32,512]{1,0:T(8,128)(2,1)S(1)}, u32[]{:S(2)}, u32[]{:S(2)}) collective-permute-start(bf16[32,512]{1,0:T(8,128)(2,1)S(1)} %get-tuple-element.47), channel_id=1, source_target_pairs={{0,1},{1,0},{2,3},{3,2},{4,5},{5,4},{6,7},{7,6},{8,9},{9,8},{10,11... | collective-permute-start | bytes 98312 | tf_op jit(solution)/shard_map/ppermute | solution.py:451
  27.7 2.6 %collective-permute-start.6 = (bf16[32,512]{1,0:T(8,128)(2,1)S(1)}, bf16[32,512]{1,0:T(8,128)(2,1)S(1)}, u32[]{:S(2)}, u32[]{:S(2)}) collective-permute-start(bf16[32,512]{1,0:T(8,128)(2,1)S(1)} %get-tuple-element.48), channel_id=1, source_target_pairs={{0,2},{1,3},{2,0},{3,1},{4,6},{5,7},{6,4},{7,5},{8,10},{9,11},{10,... | collective-permute-start | bytes 98312 | tf_op jit(solution)/shard_map/ppermute | solution.py:451
  30.3 0.8 %collective-permute-start.7 = (bf16[32,512]{1,0:T(8,128)(2,1)S(1)}, bf16[32,512]{1,0:T(8,128)(2,1)S(1)}, u32[]{:S(2)}, u32[]{:S(2)}) collective-permute-start(bf16[32,512]{1,0:T(8,128)(2,1)S(1)} %get-tuple-element.49), channel_id=1, source_target_pairs={{0,3},{1,2},{2,1},{3,0},{4,7},{5,6},{6,5},{7,4},{8,11},{9,10},{10,... | collective-permute-start | bytes 98312 | tf_op jit(solution)/shard_map/ppermute | solution.py:451
  31.1 0.9 %shard_map.77.refs_4_ = f32[512,1024]{1,0:T(8,128)S(1)} custom-call(bf16[512,1024]{1,0:T(8,128)(2,1)S(1)} %get-tuple-element.50.wave, f32[8,8,1024]{2,1,0:T(8,128)S(1)} %get-tuple-element.39.turned, f32[3,8,1024]{2,1,0:T(8,128)S(1)} %get-tuple-element.40.later, bf16[32,512]{1,0:T(8,128)(2,1)S(1)} %get-tuple-element.54.refs_0_, ...), custom_call_target="tpu_custom_call" | custom-call | flops 536870912 | bytes 1048576 | tf_op jit(solution)/shard_map/pallas_call | solution.py:384
  32.0 0.5 %collective-permute-done.6.refs_2_ = bf16[32,512]{1,0:T(8,128)(2,1)S(1)} collective-permute-done((bf16[32,512]{1,0:T(8,128)(2,1)S(1)}, bf16[32,512]{1,0:T(8,128)(2,1)S(1)}, u32[]{:S(2)}, u32[]{:S(2)}) %collective-permute-start.6) | collective-permute-done | bytes 32800 | tf_op jit(solution)/shard_map/ppermute | solution.py:451
  32.5 3.5 %collective-permute-done.7.refs_3_ = bf16[32,512]{1,0:T(8,128)(2,1)S(1)} collective-permute-done((bf16[32,512]{1,0:T(8,128)(2,1)S(1)}, bf16[32,512]{1,0:T(8,128)(2,1)S(1)}, u32[]{:S(2)}, u32[]{:S(2)}) %collective-permute-start.7) | collective-permute-done | bytes 32800 | tf_op jit(solution)/shard_map/ppermute | solution.py:451
  36.0 1.2 %shard_map.78 = (bf16[272,128]{1,0:T(8,128)(2,1)S(1)}, bf16[272,128]{1,0:T(8,128)(2,1)S(1)}, bf16[272,128]{1,0:T(8,128)(2,1)S(1)}, bf16[272,128]{1,0:T(8,128)(2,1)S(1)}) custom-call(bf16[512,1024]{1,0:T(8,128)(2,1)S(1)} %get-tuple-element.38.wave, f32[8,8,1024]{2,1,0:T(8,128)S(1)} %get-tuple-element.39.turned, f32[3,8,1024]{2,1,0:T(8,128)S(1)} %get-tuple-element.40.later, ...), custom_call_target="tpu_custom_call" | custom-call | flops 536870912 | bytes 1048576 | tf_op jit(solution)/shard_map/pallas_call | solution.py:384
  37.1 0.1 collective-permute-start.14
  37.2 1.4 %collective-permute-start.15 = (bf16[272,128]{1,0:T(8,128)(2,1)S(1)}, bf16[272,128]{1,0:T(8,128)(2,1)S(1)}, u32[]{:S(2)}, u32[]{:S(2)}) collective-permute-start(bf16[272,128]{1,0:T(8,128)(2,1)S(1)} %get-tuple-element.60), channel_id=1, source_target_pairs={{0,2},{1,3},{2,0},{3,1},{4,6},{5,7},{6,4},{7,5},{8,10},{9,11},{10,... | collective-permute-start | bytes 208904 | tf_op jit(solution)/shard_map/ppermute | solution.py:451
  38.6 3.0 %collective-permute-start.16 = (bf16[272,128]{1,0:T(8,128)(2,1)S(1)}, bf16[272,128]{1,0:T(8,128)(2,1)S(1)}, u32[]{:S(2)}, u32[]{:S(2)}) collective-permute-start(bf16[272,128]{1,0:T(8,128)(2,1)S(1)} %get-tuple-element.61), channel_id=1, source_target_pairs={{0,3},{1,2},{2,1},{3,0},{4,7},{5,6},{6,5},{7,4},{8,11},{9,10},{10,... | collective-permute-start | bytes 208904 | tf_op jit(solution)/shard_map/ppermute | solution.py:451
  41.6 1.1 %collective-permute-done.14.refs_1_ = bf16[272,128]{1,0:T(8,128)(2,1)S(1)} collective-permute-done((bf16[272,128]{1,0:T(8,128)(2,1)S(1)}, bf16[272,128]{1,0:T(8,128)(2,1)S(1)}, u32[]{:S(2)}, u32[]{:S(2)}) %collective-permute-start.14) | collective-permute-done | bytes 69664 | tf_op jit(solution)/shard_map/ppermute | solution.py:451
  42.7 2.1 %collective-permute-done.16.refs_3_ = bf16[272,128]{1,0:T(8,128)(2,1)S(1)} collective-permute-done((bf16[272,128]{1,0:T(8,128)(2,1)S(1)}, bf16[272,128]{1,0:T(8,128)(2,1)S(1)}, u32[]{:S(2)}, u32[]{:S(2)}) %collective-permute-start.16) | collective-permute-done | bytes 69664 | tf_op jit(solution)/shard_map/ppermute | solution.py:451
  44.7 0.8 %finish.1 = (f32[1,2,64,1024]{3,2,1,0:T(8,128)}, f32[1]{0:T(128)}) custom-call(bf16[272,128]{1,0:T(8,128)(2,1)S(1)} %get-tuple-element.58.refs_0_, bf16[272,128]{1,0:T(8,128)(2,1)S(1)} %collective-permute-done.14.refs_1_, bf16[272,128]{1,0:T(8,128)(2,1)S(1)} %collective-permute-done.15.refs_2_, bf16[272,128]{1,0:T(8,128)(2,1)S(1)} %collective-permute-done.16.refs_3_), custom_call_target="tpu_custom_call" | custom-call | tf_op jit(solution)/shard_map/finish/pallas_call | solution.py:427
  (13 shorter events, 0.1 us)
Async XLA Ops:
  5.5 2.3 %collective-permute-start = (bf16[512,512]{1,0:T(8,128)(2,1)S(1)}, bf16[512,512]{1,0:T(8,128)(2,1)S(1)}, u32[]{:S(2)}, u32[]{:S(2)}) collective-permute-start(bf16[512,512]{1,0:T(8,128)(2,1)S(1)} %get-tuple-element.35.after), channel_id=1, source_target_pairs={{0,4},{4,0},{8,12},{12,8},{16,20},{20,16},{24,28},{28,24},{1,5},{5... | collective-permute-start | bytes 1572872 | tf_op jit(solution)/shard_map/ppermute | solution.py:451
  9.2 6.3 %collective-permute-start.1 = (bf16[512,512]{1,0:T(8,128)(2,1)S(1)}, bf16[512,512]{1,0:T(8,128)(2,1)S(1)}, u32[]{:S(2)}, u32[]{:S(2)}) collective-permute-start(bf16[512,512]{1,0:T(8,128)(2,1)S(1)} %more.4.after), channel_id=1, source_target_pairs={{0,4},{4,0},{8,12},{12,8},{16,20},{20,16},{24,28},{28,24},{1,5},{5... | collective-permute-start | bytes 1572872 | tf_op jit(solution)/shard_map/ppermute | solution.py:451
  9.4 9.8 %collective-permute-start.8 = (bf16[128,512]{1,0:T(8,128)(2,1)S(1)}, bf16[128,512]{1,0:T(8,128)(2,1)S(1)}, u32[]{:S(2)}, u32[]{:S(2)}) collective-permute-start(bf16[128,512]{1,0:T(8,128)(2,1)S(1)} %get-tuple-element.51), channel_id=1, source_target_pairs={{0,8},{4,12},{8,0},{12,4},{16,24},{20,28},{24,16},{28,20},{1,9},{5... | collective-permute-start | bytes 393224 | tf_op jit(solution)/shard_map/ppermute | solution.py:451
  12.3 7.8 %collective-permute-start.9 = (bf16[128,512]{1,0:T(8,128)(2,1)S(1)}, bf16[128,512]{1,0:T(8,128)(2,1)S(1)}, u32[]{:S(2)}, u32[]{:S(2)}) collective-permute-start(bf16[128,512]{1,0:T(8,128)(2,1)S(1)} %get-tuple-element.52), channel_id=1, source_target_pairs={{0,16},{4,20},{8,24},{12,28},{16,0},{20,4},{24,8},{28,12},{1,17},{... | collective-permute-start | bytes 393224 | tf_op jit(solution)/shard_map/ppermute | solution.py:451
  13.8 7.3 %collective-permute-start.10 = (bf16[128,512]{1,0:T(8,128)(2,1)S(1)}, bf16[128,512]{1,0:T(8,128)(2,1)S(1)}, u32[]{:S(2)}, u32[]{:S(2)}) collective-permute-start(bf16[128,512]{1,0:T(8,128)(2,1)S(1)} %get-tuple-element.53), channel_id=1, source_target_pairs={{0,24},{4,28},{8,16},{12,20},{16,8},{20,12},{24,0},{28,4},{1,25},{... | collective-permute-start | bytes 393224 | tf_op jit(solution)/shard_map/ppermute | solution.py:451
  15.7 9.7 %collective-permute-start.2 = (bf16[128,512]{1,0:T(8,128)(2,1)S(1)}, bf16[128,512]{1,0:T(8,128)(2,1)S(1)}, u32[]{:S(2)}, u32[]{:S(2)}) collective-permute-start(bf16[128,512]{1,0:T(8,128)(2,1)S(1)} %get-tuple-element.43), channel_id=1, source_target_pairs={{0,8},{4,12},{8,0},{12,4},{16,24},{20,28},{24,16},{28,20},{1,9},{5... | collective-permute-start | bytes 393224 | tf_op jit(solution)/shard_map/ppermute | solution.py:451
  17.7 8.9 %collective-permute-start.3 = (bf16[128,512]{1,0:T(8,128)(2,1)S(1)}, bf16[128,512]{1,0:T(8,128)(2,1)S(1)}, u32[]{:S(2)}, u32[]{:S(2)}) collective-permute-start(bf16[128,512]{1,0:T(8,128)(2,1)S(1)} %get-tuple-element.44), channel_id=1, source_target_pairs={{0,16},{4,20},{8,24},{12,28},{16,0},{20,4},{24,8},{28,12},{1,17},{... | collective-permute-start | bytes 393224 | tf_op jit(solution)/shard_map/ppermute | solution.py:451
  19.2 7.3 %collective-permute-start.4 = (bf16[128,512]{1,0:T(8,128)(2,1)S(1)}, bf16[128,512]{1,0:T(8,128)(2,1)S(1)}, u32[]{:S(2)}, u32[]{:S(2)}) collective-permute-start(bf16[128,512]{1,0:T(8,128)(2,1)S(1)} %get-tuple-element.45), channel_id=1, source_target_pairs={{0,24},{4,28},{8,16},{12,20},{16,8},{20,12},{24,0},{28,4},{1,25},{... | collective-permute-start | bytes 393224 | tf_op jit(solution)/shard_map/ppermute | solution.py:451
  21.2 9.1 %collective-permute-start.11 = (bf16[32,512]{1,0:T(8,128)(2,1)S(1)}, bf16[32,512]{1,0:T(8,128)(2,1)S(1)}, u32[]{:S(2)}, u32[]{:S(2)}) collective-permute-start(bf16[32,512]{1,0:T(8,128)(2,1)S(1)} %get-tuple-element.55), channel_id=1, source_target_pairs={{0,1},{1,0},{2,3},{3,2},{4,5},{5,4},{6,7},{7,6},{8,9},{9,8},{10,11... | collective-permute-start | bytes 98312 | tf_op jit(solution)/shard_map/ppermute | solution.py:451
  22.8 8.3 %collective-permute-start.12 = (bf16[32,512]{1,0:T(8,128)(2,1)S(1)}, bf16[32,512]{1,0:T(8,128)(2,1)S(1)}, u32[]{:S(2)}, u32[]{:S(2)}) collective-permute-start(bf16[32,512]{1,0:T(8,128)(2,1)S(1)} %get-tuple-element.56), channel_id=1, source_target_pairs={{0,2},{1,3},{2,0},{3,1},{4,6},{5,7},{6,4},{7,5},{8,10},{9,11},{10,... | collective-permute-start | bytes 98312 | tf_op jit(solution)/shard_map/ppermute | solution.py:451
  25.4 5.7 %collective-permute-start.13 = (bf16[32,512]{1,0:T(8,128)(2,1)S(1)}, bf16[32,512]{1,0:T(8,128)(2,1)S(1)}, u32[]{:S(2)}, u32[]{:S(2)}) collective-permute-start(bf16[32,512]{1,0:T(8,128)(2,1)S(1)} %get-tuple-element.57), channel_id=1, source_target_pairs={{0,3},{1,2},{2,1},{3,0},{4,7},{5,6},{6,5},{7,4},{8,11},{9,10},{10,... | collective-permute-start | bytes 98312 | tf_op jit(solution)/shard_map/ppermute | solution.py:451
  26.6 5.4 %collective-permute-start.5 = (bf16[32,512]{1,0:T(8,128)(2,1)S(1)}, bf16[32,512]{1,0:T(8,128)(2,1)S(1)}, u32[]{:S(2)}, u32[]{:S(2)}) collective-permute-start(bf16[32,512]{1,0:T(8,128)(2,1)S(1)} %get-tuple-element.47), channel_id=1, source_target_pairs={{0,1},{1,0},{2,3},{3,2},{4,5},{5,4},{6,7},{7,6},{8,9},{9,8},{10,11... | collective-permute-start | bytes 98312 | tf_op jit(solution)/shard_map/ppermute | solution.py:451
  27.7 4.8 %collective-permute-start.6 = (bf16[32,512]{1,0:T(8,128)(2,1)S(1)}, bf16[32,512]{1,0:T(8,128)(2,1)S(1)}, u32[]{:S(2)}, u32[]{:S(2)}) collective-permute-start(bf16[32,512]{1,0:T(8,128)(2,1)S(1)} %get-tuple-element.48), channel_id=1, source_target_pairs={{0,2},{1,3},{2,0},{3,1},{4,6},{5,7},{6,4},{7,5},{8,10},{9,11},{10,... | collective-permute-start | bytes 98312 | tf_op jit(solution)/shard_map/ppermute | solution.py:451
  30.3 5.7 %collective-permute-start.7 = (bf16[32,512]{1,0:T(8,128)(2,1)S(1)}, bf16[32,512]{1,0:T(8,128)(2,1)S(1)}, u32[]{:S(2)}, u32[]{:S(2)}) collective-permute-start(bf16[32,512]{1,0:T(8,128)(2,1)S(1)} %get-tuple-element.49), channel_id=1, source_target_pairs={{0,3},{1,2},{2,1},{3,0},{4,7},{5,6},{6,5},{7,4},{8,11},{9,10},{10,... | collective-permute-start | bytes 98312 | tf_op jit(solution)/shard_map/ppermute | solution.py:451
  37.1 5.5 %collective-permute-start.14 = (bf16[272,128]{1,0:T(8,128)(2,1)S(1)}, bf16[272,128]{1,0:T(8,128)(2,1)S(1)}, u32[]{:S(2)}, u32[]{:S(2)}) collective-permute-start(bf16[272,128]{1,0:T(8,128)(2,1)S(1)} %get-tuple-element.59), channel_id=1, source_target_pairs={{0,1},{1,0},{2,3},{3,2},{4,5},{5,4},{6,7},{7,6},{8,9},{9,8},{10,11... | collective-permute-start | bytes 208904 | tf_op jit(solution)/shard_map/ppermute | solution.py:451
  37.2 5.4 %collective-permute-start.15 = (bf16[272,128]{1,0:T(8,128)(2,1)S(1)}, bf16[272,128]{1,0:T(8,128)(2,1)S(1)}, u32[]{:S(2)}, u32[]{:S(2)}) collective-permute-start(bf16[272,128]{1,0:T(8,128)(2,1)S(1)} %get-tuple-element.60), channel_id=1, source_target_pairs={{0,2},{1,3},{2,0},{3,1},{4,6},{5,7},{6,4},{7,5},{8,10},{9,11},{10,... | collective-permute-start | bytes 208904 | tf_op jit(solution)/shard_map/ppermute | solution.py:451
  38.6 6.1 %collective-permute-start.16 = (bf16[272,128]{1,0:T(8,128)(2,1)S(1)}, bf16[272,128]{1,0:T(8,128)(2,1)S(1)}, u32[]{:S(2)}, u32[]{:S(2)}) collective-permute-start(bf16[272,128]{1,0:T(8,128)(2,1)S(1)} %get-tuple-element.61), channel_id=1, source_target_pairs={{0,3},{1,2},{2,1},{3,0},{4,7},{5,6},{6,5},{7,4},{8,11},{9,10},{10,... | collective-permute-start | bytes 208904 | tf_op jit(solution)/shard_map/ppermute | solution.py:451

commit v5 on v4

--- a/solution.py
+++ b/solution.py
@@ -113,22 +113,26 @@
     return chunk * half, width - (chunk + 1) * half
 
 
-def multiply(table, right, chunk, out):
-    depth, width = right.shape[1:]
-    half = out.shape[1] // 2
-    for k, start in enumerate(blocks_of(chunk, half, width)):
+def multiply(table, right, blocks, out):
+    depth = right.shape[1]
+    half = out.shape[1] // len(blocks)
+    for k, start in enumerate(blocks):
         value = right[:, :, start : start + half].reshape(2 * depth, half)
         product = jnp.dot(table[...], value, preferred_element_type=jnp.float32)
         out[:, k * half : (k + 1) * half] = product.astype(out.dtype)
 
 
-def first_kernel(slots, first_scale, second_scale, *refs):
-    sources, (col, count, vis), outs = refs[:3], refs[3:6], refs[6:12]
-    out, kept, other, own, turned, later = outs
-    targets, (small, small_sems, vis_sems) = refs[12:15], refs[15:]
+def mirrored_blocks(half, width):
+    return [start for h in range(width // (2 * half)) for start in blocks_of(h, half, width)]
+
+
+def first_kernel(slots, scale, *refs):
+    sources, (col, count, vis), (out, kept, other, small) = refs[:2], refs[2:5], refs[5:9]
+    targets, (small_sems, vis_sems) = refs[9:11], refs[11:]
     _, depth, width = vis.shape
     half = out.shape[1] // 2
     loads = small_copies(sources, targets, small_sems)
+    starts = mirrored_blocks(half, width)
 
     def block(start, n):
         at = pl.ds(start, half)
@@ -138,127 +142,185 @@
         block(0, n).wait()
         return carry
 
-    order_of_blocks = [start for h in range(width // (2 * half)) for start in blocks_of(h, half, width)]
-    for copy in loads + [block(start, n) for n, start in enumerate(order_of_blocks)]:
+    for copy in loads + [block(start, n) for n, start in enumerate(starts)]:
         copy.start()
-    for copy in loads:
-        copy.wait()
-    offs, order, roff = targets
-    c = lax.axis_index("col")
     u = col[0] + iota((TILE, depth), 1)
     sub = iota((TILE, depth), 0)
     small[0], small[1] = cis(u * sub)
     small[2], small[3] = cis(u * (sub * TILE))
-    live = jnp.where(iota((TILE, depth), 1) < count[0, 0], first_scale, 0.0)
-    starts = []
+    c = lax.axis_index("col")
+
+    @pl.when(c >= 0)
+    def arrived():
+        for copy in loads:
+            copy.wait()
+
+    offs, order = targets
+    live = jnp.where(iota((TILE, depth), 1) < count[0, 0], scale, 0.0)
+    origins = []
     for flip in (1, 0):
         for k in range(slots):
             slot = (((c // 2) ^ k) * 2) + ((c % 2) ^ flip)
-            starts.append((offs[0, order[slot]] + (FS // 2 - FR // 2)) % NG)
+            origins.append((offs[0, order[slot]] + (FS // 2 - FR // 2)) % NG)
     for k in range(0, 2 * slots, TILE):
-        xs = cis(u * stacked_rows(starts[k : k + TILE], TILE))
+        xs = cis(u * stacked_rows(origins[k : k + TILE], TILE))
         at = 4 + 2 * (k // TILE)
         small[at], small[at + 1] = xs[0] * live, xs[1] * live
     build_table(other, small, 0, slots, depth)
-    build_table(own, small, slots, slots, depth)
+    lax.fori_loop(0, 2, wait, 0)
+    multiply(other, kept, blocks_of(0, half, width), out)
+    lax.fori_loop(2, len(starts), wait, 0)
+
+
+def first_columns(slots, span, scale, offs, order, col, count, vis):
+    _, depth, width = vis.shape
+    tall = slots * 2 * FR
+    smalls = 4 + 2 * -(-2 * slots // TILE)
+    return pl.pallas_call(
+        functools.partial(first_kernel, slots, scale),
+        in_specs=[HBM] * 2 + [SMEM] * 2 + [HBM],
+        out_specs=[VMEM] * 4,
+        out_shape=[
+            jax.ShapeDtypeStruct((tall, span), jnp.bfloat16),
+            jax.ShapeDtypeStruct(vis.shape, vis.dtype),
+            jax.ShapeDtypeStruct((tall, 2 * depth), jnp.bfloat16),
+            jax.ShapeDtypeStruct((smalls, TILE, depth), jnp.float32),
+        ],
+        scratch_shapes=[pltpu.SMEM(x.shape, x.dtype) for x in (offs, order)]
+        + [pltpu.SemaphoreType.DMA((2,)), pltpu.SemaphoreType.DMA((2 * width // span,))],
+        compiler_params=pltpu.CompilerParams(vmem_limit_bytes=20 * MIB),
+        cost_estimate=pl.CostEstimate(flops=tall * 4 * depth * span, bytes_accessed=4 * depth * width, transcendentals=0),
+        name="first",
+    )(*in_hbm(offs, order), col, count, *in_hbm(vis))
+
+
+def more_kernel(blocks, table, kept, after, out):
+    del after
+    multiply(table, kept, blocks, out)
+
+
+def more_columns(blocks, half, dtype, table, kept, after):
+    depth = kept.shape[1]
+    tall = table.shape[0]
+    span = half * len(blocks)
+    return pl.pallas_call(
+        functools.partial(more_kernel, blocks),
+        in_specs=[VMEM] * 2 + [HBM],
+        out_specs=VMEM,
+        out_shape=jax.ShapeDtypeStruct((tall, span), dtype),
+        compiler_params=pltpu.CompilerParams(vmem_limit_bytes=16 * MIB),
+        cost_estimate=pl.CostEstimate(flops=tall * 4 * depth * span, bytes_accessed=4 * depth * span, transcendentals=0),
+        name="more",
+    )(table, kept, after)
+
+
+def own_kernel(slots, blocks, small, kept, after, out, table):
+    del after
+    build_table(table, small, slots, slots, kept.shape[1])
+    multiply(table, kept, blocks, out)
+
+
+def own_columns(slots, blocks, half, small, kept, after):
+    depth = kept.shape[1]
+    tall = slots * 2 * FR
+    span = half * len(blocks)
+    return pl.pallas_call(
+        functools.partial(own_kernel, slots, blocks),
+        in_specs=[VMEM] * 2 + [HBM],
+        out_specs=[VMEM] * 2,
+        out_shape=[
+            jax.ShapeDtypeStruct((tall, span), jnp.float32),
+            jax.ShapeDtypeStruct((tall, 2 * depth), jnp.bfloat16),
+        ],
+        compiler_params=pltpu.CompilerParams(vmem_limit_bytes=16 * MIB),
+        cost_estimate=pl.CostEstimate(flops=tall * 4 * depth * span, bytes_accessed=4 * depth * span, transcendentals=0),
+        name="own",
+    )(small, kept, after)
+
+
+def turn_kernel(scale, chunks, after, *refs):
+    del after
+    sources, refs = refs[:3], refs[3:]
+    waves, (turned, later) = refs[:chunks], refs[chunks : chunks + 2]
+    targets, sems = refs[chunks + 2 : chunks + 5], refs[chunks + 5]
+    loads = small_copies(sources, targets, sems)
+    for copy in loads:
+        copy.start()
+    width = turned.shape[2]
+    half = width // (2 * chunks)
+    for h in range(chunks):
+        wave_rows(waves[h], 2 * blocks_of(h, half, width)[1] - (width - 1))
+
+    @pl.when(lax.axis_index("col") >= 0)
+    def arrived():
+        for copy in loads:
+            copy.wait()
+
+    offs, order, roff = targets
     rows = roff.shape[0]
     r = lax.axis_index("row")
-    start = offs[1, order[c]]
+    start = offs[1, order[lax.axis_index("col")]]
     height, wide = later.shape[1:]
     blocks = stacked_rows([(start + (r ^ b) * wide) % NG for b in range(rows)], height)
     origins = [roff[r ^ p] for p in range(rows)]
     lane = iota((height, half), 1)
-    for n, first in enumerate(order_of_blocks):
+    for n, first in enumerate(mirrored_blocks(half, width)):
         v = first + (half - 1 - lane if n % 2 == 0 else lane)
         for p in range(rows):
             phase = cis((origins[p] + v) * blocks)
             for z in range(2):
-                turned[2 * p + z, :, n * half : (n + 1) * half] = phase[z] * second_scale
+                turned[2 * p + z, :, n * half : (n + 1) * half] = phase[z] * scale
     middle = [2 * origin + (width - 1) for origin in origins]
     later[0], later[1] = cis(iota((height, wide), 1) * stacked_rows(middle, height), 2 * NG)
     for b in range(rows):
         j = ((r ^ b) * wide + iota((1, wide), 1)).astype(jnp.float32)
         later[2, b : b + 1, :] = 1.0 / (1.0 - BEAM_SLOPE * (j + 0.5) / FS)
-    lax.fori_loop(0, 2, wait, 0)
-    multiply(other, kept, 0, out)
-    lax.fori_loop(2, len(order_of_blocks), wait, 0)
-
-
-def first_columns(slots, span, scales, wide, offs, order, roff, col, count, vis):
-    _, depth, width = vis.shape
-    tall = slots * 2 * FR
+
+
+def turns(scale, chunks, width, wide, offs, order, roff, after):
     rows = roff.shape[0]
     height = -(-rows // TILE) * TILE
-    smalls = 4 + 2 * -(-2 * slots // TILE)
-    return pl.pallas_call(
-        functools.partial(first_kernel, slots, *scales),
-        in_specs=[HBM] * 3 + [SMEM] * 2 + [HBM],
-        out_specs=[VMEM] * 6,
-        out_shape=[
-            jax.ShapeDtypeStruct((tall, span), jnp.bfloat16),
-            jax.ShapeDtypeStruct(vis.shape, vis.dtype),
-            jax.ShapeDtypeStruct((tall, 2 * depth), jnp.bfloat16),
-            jax.ShapeDtypeStruct((tall, 2 * depth), jnp.bfloat16),
+    *waves, turned, later = pl.pallas_call(
+        functools.partial(turn_kernel, scale, chunks),
+        in_specs=[HBM] * 4,
+        out_specs=[VMEM] * (chunks + 2),
+        out_shape=[jax.ShapeDtypeStruct((width // chunks, wide), jnp.bfloat16)] * chunks
+        + [
             jax.ShapeDtypeStruct((2 * rows, height, width), jnp.float32),
             jax.ShapeDtypeStruct((3, height, wide), jnp.float32),
         ],
-        scratch_shapes=[pltpu.SMEM(x.shape, x.dtype) for x in (offs, order, roff)]
-        + [
-            pltpu.VMEM((smalls, TILE, depth), jnp.float32),
-            pltpu.SemaphoreType.DMA((3,)),
-            pltpu.SemaphoreType.DMA((2 * width // span,)),
-        ],
-        compiler_params=pltpu.CompilerParams(vmem_limit_bytes=20 * MIB),
-        cost_estimate=pl.CostEstimate(flops=tall * 4 * depth * span, bytes_accessed=4 * depth * width, transcendentals=0),
-        name="first",
-    )(*in_hbm(offs, order, roff), col, count, *in_hbm(vis))
-
-
-def more_kernel(chunk, table, kept, after, out, *wave):
-    del after
-    if wave:
-        width = kept.shape[2]
-        wave_rows(wave[0], 2 * blocks_of(chunk, out.shape[1] // 2, width)[1] - (width - 1))
-    multiply(table, kept, chunk, out)
-
-
-def more_columns(chunk, span, dtype, wide, table, kept, after):
-    _, depth, _ = kept.shape
-    tall = table.shape[0]
-    shape = [jax.ShapeDtypeStruct((tall, span), dtype)]
-    if wide:
-        shape.append(jax.ShapeDtypeStruct((span, wide), jnp.bfloat16))
-    return pl.pallas_call(
-        functools.partial(more_kernel, chunk),
-        in_specs=[VMEM] * 2 + [HBM],
-        out_specs=[VMEM] * len(shape),
-        out_shape=shape,
+        scratch_shapes=[pltpu.SMEM(x.shape, x.dtype) for x in (offs, order, roff)] + [pltpu.SemaphoreType.DMA((3,))],
         compiler_params=pltpu.CompilerParams(vmem_limit_bytes=16 * MIB),
-        cost_estimate=pl.CostEstimate(flops=tall * 4 * depth * span, bytes_accessed=4 * depth * span, transcendentals=0),
-        name="more",
-    )(table, kept, after)
-
-
-def pair_kernel(mine, taken, total, *sent):
-    high = total.shape[0]
-    total[...] = mine[:high] + taken[:high].astype(jnp.float32)
-    for k, out in enumerate(sent):
-        at = slice((k + 1) * high, (k + 2) * high)
-        out[...] = (mine[at] + taken[at].astype(jnp.float32)).astype(out.dtype)
+        cost_estimate=pl.CostEstimate(flops=10**9, bytes_accessed=4 * width * wide, transcendentals=0),
+        name="turns",
+    )(after, *in_hbm(offs, order, roff))
+    return waves, turned, later
+
+
+def pair_kernel(parts, mine, *refs):
+    taken, total, sent = refs[:parts], refs[parts], refs[parts + 1 :]
+    high, width = total.shape
+    piece = width // parts
+    for n in range(parts):
+        to = slice(n * piece, (n + 1) * piece)
+        total[:, to] = mine[:high, to] + taken[n][:high].astype(jnp.float32)
+        for k, out in enumerate(sent):
+            at = slice((k + 1) * high, (k + 2) * high)
+            out[:, to] = (mine[at, to] + taken[n][at].astype(jnp.float32)).astype(out.dtype)
 
 
 def pair_sum(slots, mine, taken):
     rows, width = mine.shape
     high = rows // slots
     return pl.pallas_call(
-        pair_kernel,
-        in_specs=[VMEM] * 2,
+        functools.partial(pair_kernel, len(taken)),
+        in_specs=[VMEM] * (1 + len(taken)),
         out_specs=[VMEM] * slots,
         out_shape=[jax.ShapeDtypeStruct((high, width), jnp.float32)]
         + [jax.ShapeDtypeStruct((high, width), jnp.bfloat16)] * (slots - 1),
         compiler_params=pltpu.CompilerParams(vmem_limit_bytes=8 * MIB),
         name="pair",
-    )(mine, taken)
+    )(mine, *taken)
 
 
 def sum_kernel(arrived, total, *refs):
@@ -445,29 +507,36 @@
     wide = FS // rows
     chunks = 2
     span = width // chunks
-    scales = (1.0 / math.sqrt(depth * cols), 0.5 / math.sqrt(width * rows))
+    half = span // 2
 
     def swap(value, axis, count, bit):
         return lax.ppermute(value, axis, [(i, i ^ bit) for i in range(count)])
 
-    given, kept, other, own, turned, later = first_columns(
-        slots, span, scales, wide, facet_offsets.T, facet_order, row_offsets, col_offsets, vis_counts, visibilities
+    given, kept, other, small = first_columns(
+        slots, span, 1.0 / math.sqrt(depth * cols), facet_offsets.T, facet_order, col_offsets, vis_counts, visibilities
     )
-    totals, sents, waves = [], [], []
+    totals, sents = [], []
     for h in range(chunks):
-        if h > 0:
-            (given,) = more_columns(h, span, jnp.bfloat16, 0, other, kept, totals[h - 1])
-        taken = swap(given, "col", cols, 1)
-        mine, wave = more_columns(h, span, jnp.float32, wide, own, kept, given)
+        blocks = blocks_of(h, half, width)
+        if h == 0:
+            taken = [swap(given, "col", cols, 1)]
+            mine, own = own_columns(slots, blocks, half, small, kept, given)
+        else:
+            taken = []
+            for n, block in enumerate(blocks):
+                given = more_columns((block,), half, jnp.bfloat16, other, kept, given if n else totals[h - 1])
+                taken.append(swap(given, "col", cols, 1))
+            mine = more_columns(blocks, half, jnp.float32, own, kept, given)
         total, *sent = pair_sum(slots, mine, taken)
-        waves.append(wave)
         totals.append(total)
         sents.append([swap(value, "col", cols, 2 * k + 2) for k, value in enumerate(sent)])
     pieces = []
     for h in range(chunks):
         mine, *others = sum_of(rows, totals[h], sents[h])
-        far = [swap(value, "row", rows, p + 1) for p, value in reversed(list(enumerate(others)))]
-        pieces.append([mine] + far[::-1])
+        pieces.append([mine] + [swap(value, "row", rows, p + 1) for p, value in enumerate(others)])
+    waves, turned, later = turns(
+        0.5 / math.sqrt(width * rows), chunks, width, wide, facet_offsets.T, facet_order, row_offsets, pieces[0][0]
+    )
     parts = []
     for h in range(chunks):
         parts = rows_of(h * span, h == chunks - 1, pieces[h], waves[h], turned, later, parts)

time: 45.7 us -> 46.8 us (1.024)
  starting transfers between devices: 23.3 us -> 24.2 us
    ppermute x17 -> x18, starting transfers between devices: 23.3 us -> 24.2 us  [swap(): return lax.ppermute(value, axis, [(i, i ^ bit) for i in range(count)])]
    ppermute x17 -> x18, waiting for transfers between devices: 8.66 us -> 8.91 us  [swap(): return lax.ppermute(value, axis, [(i, i ^ bit) for i in range(count)])]
    pallas_call x6 -> x8, Pallas kernels: 8.56 us -> 8.43 us  [the longest x1 2.87 us: first_columns(): pl.pallas_call(functools.partial(first_kernel, slots, scale), in_specs=[H...]
  transfers between devices with their start and end apart: 17 -> 18, of which waited for: 6 -> 7; matrix products, arithmetic and copies ran while one was open for 0% -> 0% of each run, Pallas kernels for 10% -> 11%
where the time goes in v5:
time: 46.8 us; the launch traced here: 46.6 us
  starting transfers between devices  24.2 us (52%)
  Pallas kernels  11.4 us (24%)
  waiting for transfers between devices  8.91 us (19%)
  between operations  2.06 us (4%)
    ppermute x18, starting transfers between devices, swap(): return lax.ppermute(value, axis, [(i, i ^ bit) for i in range(count)])  24.2 us
    ppermute x18, waiting for transfers between devices, swap(): return lax.ppermute(value, axis, [(i, i ^ bit) for i in range(count)])  8.91 us
    pallas_call x1, Pallas kernels, first_columns(): pl.pallas_call(functools.partial(first_kernel, slots, scale), in_specs=[H...  2.87 us
    pallas_call x3, Pallas kernels, more_columns(): pl.pallas_call(functools.partial(more_kernel, blocks), in_specs=[VMEM] *...  2.67 us
    pallas_call x2, Pallas kernels, rows_of(): pl.pallas_call(functools.partial(row_kernel, rows, first, len(before), la...  2.03 us
    pallas_call x1, Pallas kernels, turns(): pl.pallas_call(functools.partial(turn_kernel, scale, chunks), in_specs=[H...  1.42 us
    pallas_call x1, Pallas kernels, own_columns(): pl.pallas_call(functools.partial(own_kernel, slots, blocks), in_specs=[VM...  1.3 us
  transfers between devices with their start and end apart: 18, of which 7 were waited for; matrix products, arithmetic and copies ran while one was open for 0% of the time, Pallas kernels for 11%

profile of v5, /device:TPU:0, one launch (start us, length us, event | category | flops | bytes accessed | tf_op | source)
XLA Modules:
  0.0 46.6 jit_solution(13656474573771937022)
XLA Ops:
  1.9 2.9 %first.1 = (bf16[512,512]{1,0:T(8,128)(2,1)S(1)}, bf16[2,1024,1024]{2,1,0:T(8,128)(2,1)S(1)}, bf16[512,2048]{1,0:T(8,128)(2,1)S(1)}, f32[6,8,1024]{2,1,0:T(8,128)S(1)}) custom-call(s32[2,8]{1,0:T(2,128)} %bitcast.1, s32[8]{0:T(128)} %refs_1_.3, s32[1]{0:T(128)S(6)} %copy.8.refs_2_, s32[1,1]{1,0:T(1,128)S(6)} %copy.9.refs_3_, bf16[2,1024,1024]{2,1,0:T(8,128)(2,1)} %refs_4_.1), custom_call_target="tpu_custom_call" | custom-call | flops 1073741824 | bytes 4194304 | tf_op jit(solution)/shard_map/first/pallas_call | solution.py:179
  4.8 0.6 %collective-permute-start = (bf16[512,512]{1,0:T(8,128)(2,1)S(1)}, bf16[512,512]{1,0:T(8,128)(2,1)S(1)}, u32[]{:S(2)}, u32[]{:S(2)}) collective-permute-start(bf16[512,512]{1,0:T(8,128)(2,1)S(1)} %get-tuple-element.34.after), channel_id=1, source_target_pairs={{0,4},{4,0},{8,12},{12,8},{16,20},{20,16},{24,28},{28,24},{1,5},{5... | collective-permute-start | bytes 1572872 | tf_op jit(solution)/shard_map/ppermute | solution.py:513
  5.4 1.3 %own.1 = (f32[512,512]{1,0:T(8,128)S(1)}, bf16[512,2048]{1,0:T(8,128)(2,1)S(1)}) custom-call(f32[6,8,1024]{2,1,0:T(8,128)S(1)} %get-tuple-element.32.small, bf16[2,1024,1024]{2,1,0:T(8,128)(2,1)S(1)} %get-tuple-element.33.kept, bf16[512,512]{1,0:T(8,128)(2,1)S(1)} %get-tuple-element.34.after), custom_call_target="tpu_custom_call" | custom-call | flops 1073741824 | bytes 2097152 | tf_op jit(solution)/shard_map/own/pallas_call | solution.py:227
  6.7 0.2 collective-permute-done.refs_0_
  7.0 0.7 %more.3.after = bf16[512,256]{1,0:T(8,128)(2,1)S(1)} custom-call(bf16[512,2048]{1,0:T(8,128)(2,1)S(1)} %get-tuple-element.45.table, bf16[2,1024,1024]{2,1,0:T(8,128)(2,1)S(1)} %get-tuple-element.33.kept, f32[128,512]{1,0:T(8,128)S(1)} %get-tuple-element.36.total.after), custom_call_target="tpu_custom_call" | custom-call | flops 536870912 | bytes 1048576 | tf_op jit(solution)/shard_map/more/pallas_call | solution.py:206
  7.7 0.7 %more.4.after = bf16[512,256]{1,0:T(8,128)(2,1)S(1)} custom-call(bf16[512,2048]{1,0:T(8,128)(2,1)S(1)} %get-tuple-element.45.table, bf16[2,1024,1024]{2,1,0:T(8,128)(2,1)S(1)} %get-tuple-element.33.kept, bf16[512,256]{1,0:T(8,128)(2,1)S(1)} %more.3.after), custom_call_target="tpu_custom_call" | custom-call | flops 536870912 | bytes 1048576 | tf_op jit(solution)/shard_map/more/pallas_call | solution.py:206
  8.4 0.4 collective-permute-start.5
  8.9 0.1 collective-permute-start.4
  9.0 2.8 %collective-permute-start.1 = (bf16[128,512]{1,0:T(8,128)(2,1)S(1)}, bf16[128,512]{1,0:T(8,128)(2,1)S(1)}, u32[]{:S(2)}, u32[]{:S(2)}) collective-permute-start(bf16[128,512]{1,0:T(8,128)(2,1)S(1)} %get-tuple-element.37), channel_id=1, source_target_pairs={{0,8},{4,12},{8,0},{12,4},{16,24},{20,28},{24,16},{28,20},{1,9},{5... | collective-permute-start | bytes 393224 | tf_op jit(solution)/shard_map/ppermute | solution.py:513
  11.8 1.5 %collective-permute-start.2 = (bf16[128,512]{1,0:T(8,128)(2,1)S(1)}, bf16[128,512]{1,0:T(8,128)(2,1)S(1)}, u32[]{:S(2)}, u32[]{:S(2)}) collective-permute-start(bf16[128,512]{1,0:T(8,128)(2,1)S(1)} %get-tuple-element.38), channel_id=1, source_target_pairs={{0,16},{4,20},{8,24},{12,28},{16,0},{20,4},{24,8},{28,12},{1,17},{... | collective-permute-start | bytes 393224 | tf_op jit(solution)/shard_map/ppermute | solution.py:513
  13.4 1.2 %more.5.mine = f32[512,512]{1,0:T(8,128)S(1)} custom-call(bf16[512,2048]{1,0:T(8,128)(2,1)S(1)} %get-tuple-element.44.table, bf16[2,1024,1024]{2,1,0:T(8,128)(2,1)S(1)} %get-tuple-element.33.kept, bf16[512,256]{1,0:T(8,128)(2,1)S(1)} %more.4.after), custom_call_target="tpu_custom_call" | custom-call | flops 1073741824 | bytes 2097152 | tf_op jit(solution)/shard_map/more/pallas_call | solution.py:206
  14.6 0.1 pair.3
  14.7 2.0 %collective-permute-start.6 = (bf16[128,512]{1,0:T(8,128)(2,1)S(1)}, bf16[128,512]{1,0:T(8,128)(2,1)S(1)}, u32[]{:S(2)}, u32[]{:S(2)}) collective-permute-start(bf16[128,512]{1,0:T(8,128)(2,1)S(1)} %get-tuple-element.47), channel_id=1, source_target_pairs={{0,8},{4,12},{8,0},{12,4},{16,24},{20,28},{24,16},{28,20},{1,9},{5... | collective-permute-start | bytes 393224 | tf_op jit(solution)/shard_map/ppermute | solution.py:513
  16.8 1.5 %collective-permute-start.7 = (bf16[128,512]{1,0:T(8,128)(2,1)S(1)}, bf16[128,512]{1,0:T(8,128)(2,1)S(1)}, u32[]{:S(2)}, u32[]{:S(2)}) collective-permute-start(bf16[128,512]{1,0:T(8,128)(2,1)S(1)} %get-tuple-element.48), channel_id=1, source_target_pairs={{0,16},{4,20},{8,24},{12,28},{16,0},{20,4},{24,8},{28,12},{1,17},{... | collective-permute-start | bytes 393224 | tf_op jit(solution)/shard_map/ppermute | solution.py:513
  18.3 0.9 %collective-permute-start.8 = (bf16[128,512]{1,0:T(8,128)(2,1)S(1)}, bf16[128,512]{1,0:T(8,128)(2,1)S(1)}, u32[]{:S(2)}, u32[]{:S(2)}) collective-permute-start(bf16[128,512]{1,0:T(8,128)(2,1)S(1)} %get-tuple-element.49), channel_id=1, source_target_pairs={{0,24},{4,28},{8,16},{12,20},{16,8},{20,12},{24,0},{28,4},{1,25},{... | collective-permute-start | bytes 393224 | tf_op jit(solution)/shard_map/ppermute | solution.py:513
  19.2 1.0 %collective-permute-done.2.refs_1_ = bf16[128,512]{1,0:T(8,128)(2,1)S(1)} collective-permute-done((bf16[128,512]{1,0:T(8,128)(2,1)S(1)}, bf16[128,512]{1,0:T(8,128)(2,1)S(1)}, u32[]{:S(2)}, u32[]{:S(2)}) %collective-permute-start.2) | collective-permute-done | bytes 131104 | tf_op jit(solution)/shard_map/ppermute | solution.py:513
  20.1 0.6 %collective-permute-done.3.refs_2_ = bf16[128,512]{1,0:T(8,128)(2,1)S(1)} collective-permute-done((bf16[128,512]{1,0:T(8,128)(2,1)S(1)}, bf16[128,512]{1,0:T(8,128)(2,1)S(1)}, u32[]{:S(2)}, u32[]{:S(2)}) %collective-permute-start.3) | collective-permute-done | bytes 131104 | tf_op jit(solution)/shard_map/ppermute | solution.py:513
  20.7 1.6 %collective-permute-start.12 = (bf16[32,512]{1,0:T(8,128)(2,1)S(1)}, bf16[32,512]{1,0:T(8,128)(2,1)S(1)}, u32[]{:S(2)}, u32[]{:S(2)}) collective-permute-start(bf16[32,512]{1,0:T(8,128)(2,1)S(1)} %get-tuple-element.55), channel_id=1, source_target_pairs={{0,1},{1,0},{2,3},{3,2},{4,5},{5,4},{6,7},{7,6},{8,9},{9,8},{10,11... | collective-permute-start | bytes 98312 | tf_op jit(solution)/shard_map/ppermute | solution.py:513
  22.4 2.6 %collective-permute-start.13 = (bf16[32,512]{1,0:T(8,128)(2,1)S(1)}, bf16[32,512]{1,0:T(8,128)(2,1)S(1)}, u32[]{:S(2)}, u32[]{:S(2)}) collective-permute-start(bf16[32,512]{1,0:T(8,128)(2,1)S(1)} %get-tuple-element.56), channel_id=1, source_target_pairs={{0,2},{1,3},{2,0},{3,1},{4,6},{5,7},{6,4},{7,5},{8,10},{9,11},{10,... | collective-permute-start | bytes 98312 | tf_op jit(solution)/shard_map/ppermute | solution.py:513
  25.0 1.2 %collective-permute-start.14 = (bf16[32,512]{1,0:T(8,128)(2,1)S(1)}, bf16[32,512]{1,0:T(8,128)(2,1)S(1)}, u32[]{:S(2)}, u32[]{:S(2)}) collective-permute-start(bf16[32,512]{1,0:T(8,128)(2,1)S(1)} %get-tuple-element.57), channel_id=1, source_target_pairs={{0,3},{1,2},{2,1},{3,0},{4,7},{5,6},{6,5},{7,4},{8,11},{9,10},{10,... | collective-permute-start | bytes 98312 | tf_op jit(solution)/shard_map/ppermute | solution.py:513
  26.1 1.4 %turns.1 = (bf16[512,1024]{1,0:T(8,128)(2,1)S(1)}, bf16[512,1024]{1,0:T(8,128)(2,1)S(1)}, f32[8,8,1024]{2,1,0:T(8,128)S(1)}, f32[3,8,1024]{2,1,0:T(8,128)S(1)}) custom-call(bf16[32,512]{1,0:T(8,128)(2,1)S(1)} %get-tuple-element.40.after.refs_0_, s32[2,8]{1,0:T(2,128)} %bitcast.2, s32[8]{0:T(128)} %refs_1_.3, s32[4]{0:T(128)} %refs_2_.2), custom_call_target="tpu_custom_call" | custom-call | flops 1000000000 | bytes 4194304 | tf_op jit(solution)/shard_map/turns/pallas_call | solution.py:283
  27.7 3.2 %collective-permute-start.10 = (bf16[32,512]{1,0:T(8,128)(2,1)S(1)}, bf16[32,512]{1,0:T(8,128)(2,1)S(1)}, u32[]{:S(2)}, u32[]{:S(2)}) collective-permute-start(bf16[32,512]{1,0:T(8,128)(2,1)S(1)} %get-tuple-element.52), channel_id=1, source_target_pairs={{0,2},{1,3},{2,0},{3,1},{4,6},{5,7},{6,4},{7,5},{8,10},{9,11},{10,... | collective-permute-start | bytes 98312 | tf_op jit(solution)/shard_map/ppermute | solution.py:513
  31.0 1.2 %collective-permute-start.11 = (bf16[32,512]{1,0:T(8,128)(2,1)S(1)}, bf16[32,512]{1,0:T(8,128)(2,1)S(1)}, u32[]{:S(2)}, u32[]{:S(2)}) collective-permute-start(bf16[32,512]{1,0:T(8,128)(2,1)S(1)} %get-tuple-element.53), channel_id=1, source_target_pairs={{0,3},{1,2},{2,1},{3,0},{4,7},{5,6},{6,5},{7,4},{8,11},{9,10},{10,... | collective-permute-start | bytes 98312 | tf_op jit(solution)/shard_map/ppermute | solution.py:513
  32.1 0.9 %shard_map.77.refs_4_ = f32[512,1024]{1,0:T(8,128)S(1)} custom-call(bf16[512,1024]{1,0:T(8,128)(2,1)S(1)} %get-tuple-element.54.wave, f32[8,8,1024]{2,1,0:T(8,128)S(1)} %get-tuple-element.42.turned, f32[3,8,1024]{2,1,0:T(8,128)S(1)} %get-tuple-element.43.later, bf16[32,512]{1,0:T(8,128)(2,1)S(1)} %get-tuple-element.40.after.refs_0_, ...), custom_call_target="tpu_custom_call" | custom-call | flops 536870912 | bytes 1048576 | tf_op jit(solution)/shard_map/pallas_call | solution.py:446
  33.0 0.2 collective-permute-done.10.refs_2_
  33.2 3.8 %collective-permute-done.11.refs_3_ = bf16[32,512]{1,0:T(8,128)(2,1)S(1)} collective-permute-done((bf16[32,512]{1,0:T(8,128)(2,1)S(1)}, bf16[32,512]{1,0:T(8,128)(2,1)S(1)}, u32[]{:S(2)}, u32[]{:S(2)}) %collective-permute-start.11) | collective-permute-done | bytes 32800 | tf_op jit(solution)/shard_map/ppermute | solution.py:513
  37.0 1.2 %shard_map.78 = (bf16[272,128]{1,0:T(8,128)(2,1)S(1)}, bf16[272,128]{1,0:T(8,128)(2,1)S(1)}, bf16[272,128]{1,0:T(8,128)(2,1)S(1)}, bf16[272,128]{1,0:T(8,128)(2,1)S(1)}) custom-call(bf16[512,1024]{1,0:T(8,128)(2,1)S(1)} %get-tuple-element.41.wave, f32[8,8,1024]{2,1,0:T(8,128)S(1)} %get-tuple-element.42.turned, f32[3,8,1024]{2,1,0:T(8,128)S(1)} %get-tuple-element.43.later, ...), custom_call_target="tpu_custom_call" | custom-call | flops 536870912 | bytes 1048576 | tf_op jit(solution)/shard_map/pallas_call | solution.py:446
  38.3 1.4 %collective-permute-start.16 = (bf16[272,128]{1,0:T(8,128)(2,1)S(1)}, bf16[272,128]{1,0:T(8,128)(2,1)S(1)}, u32[]{:S(2)}, u32[]{:S(2)}) collective-permute-start(bf16[272,128]{1,0:T(8,128)(2,1)S(1)} %get-tuple-element.60), channel_id=1, source_target_pairs={{0,2},{1,3},{2,0},{3,1},{4,6},{5,7},{6,4},{7,5},{8,10},{9,11},{10,... | collective-permute-start | bytes 208904 | tf_op jit(solution)/shard_map/ppermute | solution.py:513
  39.6 3.0 %collective-permute-start.17 = (bf16[272,128]{1,0:T(8,128)(2,1)S(1)}, bf16[272,128]{1,0:T(8,128)(2,1)S(1)}, u32[]{:S(2)}, u32[]{:S(2)}) collective-permute-start(bf16[272,128]{1,0:T(8,128)(2,1)S(1)} %get-tuple-element.61), channel_id=1, source_target_pairs={{0,3},{1,2},{2,1},{3,0},{4,7},{5,6},{6,5},{7,4},{8,11},{9,10},{10,... | collective-permute-start | bytes 208904 | tf_op jit(solution)/shard_map/ppermute | solution.py:513
  42.6 0.9 %collective-permute-done.16.refs_2_ = bf16[272,128]{1,0:T(8,128)(2,1)S(1)} collective-permute-done((bf16[272,128]{1,0:T(8,128)(2,1)S(1)}, bf16[272,128]{1,0:T(8,128)(2,1)S(1)}, u32[]{:S(2)}, u32[]{:S(2)}) %collective-permute-start.16) | collective-permute-done | bytes 69664 | tf_op jit(solution)/shard_map/ppermute | solution.py:513
  43.5 2.2 %collective-permute-done.17.refs_3_ = bf16[272,128]{1,0:T(8,128)(2,1)S(1)} collective-permute-done((bf16[272,128]{1,0:T(8,128)(2,1)S(1)}, bf16[272,128]{1,0:T(8,128)(2,1)S(1)}, u32[]{:S(2)}, u32[]{:S(2)}) %collective-permute-start.17) | collective-permute-done | bytes 69664 | tf_op jit(solution)/shard_map/ppermute | solution.py:513
  45.8 0.8 %finish.1 = (f32[1,2,64,1024]{3,2,1,0:T(8,128)}, f32[1]{0:T(128)}) custom-call(bf16[272,128]{1,0:T(8,128)(2,1)S(1)} %get-tuple-element.58.refs_0_, bf16[272,128]{1,0:T(8,128)(2,1)S(1)} %collective-permute-done.15.refs_1_, bf16[272,128]{1,0:T(8,128)(2,1)S(1)} %collective-permute-done.16.refs_2_, bf16[272,128]{1,0:T(8,128)(2,1)S(1)} %collective-permute-done.17.refs_3_), custom_call_target="tpu_custom_call" | custom-call | tf_op jit(solution)/shard_map/finish/pallas_call | solution.py:489
  (17 shorter events, 0.4 us)
Async XLA Ops:
  4.8 2.1 %collective-permute-start = (bf16[512,512]{1,0:T(8,128)(2,1)S(1)}, bf16[512,512]{1,0:T(8,128)(2,1)S(1)}, u32[]{:S(2)}, u32[]{:S(2)}) collective-permute-start(bf16[512,512]{1,0:T(8,128)(2,1)S(1)} %get-tuple-element.34.after), channel_id=1, source_target_pairs={{0,4},{4,0},{8,12},{12,8},{16,20},{20,16},{24,28},{28,24},{1,5},{5... | collective-permute-start | bytes 1572872 | tf_op jit(solution)/shard_map/ppermute | solution.py:513
  8.4 6.2 %collective-permute-start.5 = (bf16[512,256]{1,0:T(8,128)(2,1)S(1)}, bf16[512,256]{1,0:T(8,128)(2,1)S(1)}, u32[]{:S(2)}, u32[]{:S(2)}) collective-permute-start(bf16[512,256]{1,0:T(8,128)(2,1)S(1)} %more.4.after), channel_id=1, source_target_pairs={{0,4},{4,0},{8,12},{12,8},{16,20},{20,16},{24,28},{28,24},{1,5},{5... | collective-permute-start | bytes 786440 | tf_op jit(solution)/shard_map/ppermute | solution.py:513
  8.9 5.8 %collective-permute-start.4 = (bf16[512,256]{1,0:T(8,128)(2,1)S(1)}, bf16[512,256]{1,0:T(8,128)(2,1)S(1)}, u32[]{:S(2)}, u32[]{:S(2)}) collective-permute-start(bf16[512,256]{1,0:T(8,128)(2,1)S(1)} %more.3.after), channel_id=1, source_target_pairs={{0,4},{4,0},{8,12},{12,8},{16,20},{20,16},{24,28},{28,24},{1,5},{5... | collective-permute-start | bytes 786440 | tf_op jit(solution)/shard_map/ppermute | solution.py:513
  9.0 9.3 %collective-permute-start.1 = (bf16[128,512]{1,0:T(8,128)(2,1)S(1)}, bf16[128,512]{1,0:T(8,128)(2,1)S(1)}, u32[]{:S(2)}, u32[]{:S(2)}) collective-permute-start(bf16[128,512]{1,0:T(8,128)(2,1)S(1)} %get-tuple-element.37), channel_id=1, source_target_pairs={{0,8},{4,12},{8,0},{12,4},{16,24},{20,28},{24,16},{28,20},{1,9},{5... | collective-permute-start | bytes 393224 | tf_op jit(solution)/shard_map/ppermute | solution.py:513
  11.8 8.3 %collective-permute-start.2 = (bf16[128,512]{1,0:T(8,128)(2,1)S(1)}, bf16[128,512]{1,0:T(8,128)(2,1)S(1)}, u32[]{:S(2)}, u32[]{:S(2)}) collective-permute-start(bf16[128,512]{1,0:T(8,128)(2,1)S(1)} %get-tuple-element.38), channel_id=1, source_target_pairs={{0,16},{4,20},{8,24},{12,28},{16,0},{20,4},{24,8},{28,12},{1,17},{... | collective-permute-start | bytes 393224 | tf_op jit(solution)/shard_map/ppermute | solution.py:513
  13.4 7.3 %collective-permute-start.3 = (bf16[128,512]{1,0:T(8,128)(2,1)S(1)}, bf16[128,512]{1,0:T(8,128)(2,1)S(1)}, u32[]{:S(2)}, u32[]{:S(2)}) collective-permute-start(bf16[128,512]{1,0:T(8,128)(2,1)S(1)} %get-tuple-element.39), channel_id=1, source_target_pairs={{0,24},{4,28},{8,16},{12,20},{16,8},{20,12},{24,0},{28,4},{1,25},{... | collective-permute-start | bytes 393224 | tf_op jit(solution)/shard_map/ppermute | solution.py:513
  14.7 10.2 %collective-permute-start.6 = (bf16[128,512]{1,0:T(8,128)(2,1)S(1)}, bf16[128,512]{1,0:T(8,128)(2,1)S(1)}, u32[]{:S(2)}, u32[]{:S(2)}) collective-permute-start(bf16[128,512]{1,0:T(8,128)(2,1)S(1)} %get-tuple-element.47), channel_id=1, source_target_pairs={{0,8},{4,12},{8,0},{12,4},{16,24},{20,28},{24,16},{28,20},{1,9},{5... | collective-permute-start | bytes 393224 | tf_op jit(solution)/shard_map/ppermute | solution.py:513
  16.8 10.8 %collective-permute-start.7 = (bf16[128,512]{1,0:T(8,128)(2,1)S(1)}, bf16[128,512]{1,0:T(8,128)(2,1)S(1)}, u32[]{:S(2)}, u32[]{:S(2)}) collective-permute-start(bf16[128,512]{1,0:T(8,128)(2,1)S(1)} %get-tuple-element.48), channel_id=1, source_target_pairs={{0,16},{4,20},{8,24},{12,28},{16,0},{20,4},{24,8},{28,12},{1,17},{... | collective-permute-start | bytes 393224 | tf_op jit(solution)/shard_map/ppermute | solution.py:513
  18.3 9.3 %collective-permute-start.8 = (bf16[128,512]{1,0:T(8,128)(2,1)S(1)}, bf16[128,512]{1,0:T(8,128)(2,1)S(1)}, u32[]{:S(2)}, u32[]{:S(2)}) collective-permute-start(bf16[128,512]{1,0:T(8,128)(2,1)S(1)} %get-tuple-element.49), channel_id=1, source_target_pairs={{0,24},{4,28},{8,16},{12,20},{16,8},{20,12},{24,0},{28,4},{1,25},{... | collective-permute-start | bytes 393224 | tf_op jit(solution)/shard_map/ppermute | solution.py:513
  20.7 10.2 %collective-permute-start.12 = (bf16[32,512]{1,0:T(8,128)(2,1)S(1)}, bf16[32,512]{1,0:T(8,128)(2,1)S(1)}, u32[]{:S(2)}, u32[]{:S(2)}) collective-permute-start(bf16[32,512]{1,0:T(8,128)(2,1)S(1)} %get-tuple-element.55), channel_id=1, source_target_pairs={{0,1},{1,0},{2,3},{3,2},{4,5},{5,4},{6,7},{7,6},{8,9},{9,8},{10,11... | collective-permute-start | bytes 98312 | tf_op jit(solution)/shard_map/ppermute | solution.py:513
  22.4 9.7 %collective-permute-start.13 = (bf16[32,512]{1,0:T(8,128)(2,1)S(1)}, bf16[32,512]{1,0:T(8,128)(2,1)S(1)}, u32[]{:S(2)}, u32[]{:S(2)}) collective-permute-start(bf16[32,512]{1,0:T(8,128)(2,1)S(1)} %get-tuple-element.56), channel_id=1, source_target_pairs={{0,2},{1,3},{2,0},{3,1},{4,6},{5,7},{6,4},{7,5},{8,10},{9,11},{10,... | collective-permute-start | bytes 98312 | tf_op jit(solution)/shard_map/ppermute | solution.py:513
  25.0 7.1 %collective-permute-start.14 = (bf16[32,512]{1,0:T(8,128)(2,1)S(1)}, bf16[32,512]{1,0:T(8,128)(2,1)S(1)}, u32[]{:S(2)}, u32[]{:S(2)}) collective-permute-start(bf16[32,512]{1,0:T(8,128)(2,1)S(1)} %get-tuple-element.57), channel_id=1, source_target_pairs={{0,3},{1,2},{2,1},{3,0},{4,7},{5,6},{6,5},{7,4},{8,11},{9,10},{10,... | collective-permute-start | bytes 98312 | tf_op jit(solution)/shard_map/ppermute | solution.py:513
  27.7 5.3 %collective-permute-start.9 = (bf16[32,512]{1,0:T(8,128)(2,1)S(1)}, bf16[32,512]{1,0:T(8,128)(2,1)S(1)}, u32[]{:S(2)}, u32[]{:S(2)}) collective-permute-start(bf16[32,512]{1,0:T(8,128)(2,1)S(1)} %get-tuple-element.51), channel_id=1, source_target_pairs={{0,1},{1,0},{2,3},{3,2},{4,5},{5,4},{6,7},{7,6},{8,9},{9,8},{10,11... | collective-permute-start | bytes 98312 | tf_op jit(solution)/shard_map/ppermute | solution.py:513
  27.7 5.5 %collective-permute-start.10 = (bf16[32,512]{1,0:T(8,128)(2,1)S(1)}, bf16[32,512]{1,0:T(8,128)(2,1)S(1)}, u32[]{:S(2)}, u32[]{:S(2)}) collective-permute-start(bf16[32,512]{1,0:T(8,128)(2,1)S(1)} %get-tuple-element.52), channel_id=1, source_target_pairs={{0,2},{1,3},{2,0},{3,1},{4,6},{5,7},{6,4},{7,5},{8,10},{9,11},{10,... | collective-permute-start | bytes 98312 | tf_op jit(solution)/shard_map/ppermute | solution.py:513
  31.0 6.1 %collective-permute-start.11 = (bf16[32,512]{1,0:T(8,128)(2,1)S(1)}, bf16[32,512]{1,0:T(8,128)(2,1)S(1)}, u32[]{:S(2)}, u32[]{:S(2)}) collective-permute-start(bf16[32,512]{1,0:T(8,128)(2,1)S(1)} %get-tuple-element.53), channel_id=1, source_target_pairs={{0,3},{1,2},{2,1},{3,0},{4,7},{5,6},{6,5},{7,4},{8,11},{9,10},{10,... | collective-permute-start | bytes 98312 | tf_op jit(solution)/shard_map/ppermute | solution.py:513
  38.2 4.5 %collective-permute-start.15 = (bf16[272,128]{1,0:T(8,128)(2,1)S(1)}, bf16[272,128]{1,0:T(8,128)(2,1)S(1)}, u32[]{:S(2)}, u32[]{:S(2)}) collective-permute-start(bf16[272,128]{1,0:T(8,128)(2,1)S(1)} %get-tuple-element.59), channel_id=1, source_target_pairs={{0,1},{1,0},{2,3},{3,2},{4,5},{5,4},{6,7},{7,6},{8,9},{9,8},{10,11... | collective-permute-start | bytes 208904 | tf_op jit(solution)/shard_map/ppermute | solution.py:513
  38.3 5.3 %collective-permute-start.16 = (bf16[272,128]{1,0:T(8,128)(2,1)S(1)}, bf16[272,128]{1,0:T(8,128)(2,1)S(1)}, u32[]{:S(2)}, u32[]{:S(2)}) collective-permute-start(bf16[272,128]{1,0:T(8,128)(2,1)S(1)} %get-tuple-element.60), channel_id=1, source_target_pairs={{0,2},{1,3},{2,0},{3,1},{4,6},{5,7},{6,4},{7,5},{8,10},{9,11},{10,... | collective-permute-start | bytes 208904 | tf_op jit(solution)/shard_map/ppermute | solution.py:513
  39.6 6.1 %collective-permute-start.17 = (bf16[272,128]{1,0:T(8,128)(2,1)S(1)}, bf16[272,128]{1,0:T(8,128)(2,1)S(1)}, u32[]{:S(2)}, u32[]{:S(2)}) collective-permute-start(bf16[272,128]{1,0:T(8,128)(2,1)S(1)} %get-tuple-element.61), channel_id=1, source_target_pairs={{0,3},{1,2},{2,1},{3,0},{4,7},{5,6},{6,5},{7,4},{8,11},{9,10},{10,... | collective-permute-start | bytes 208904 | tf_op jit(solution)/shard_map/ppermute | solution.py:513
